TPU v7x, 256 devices: a 4x2x16 block of a 4x16x16 slice. The times are simulated.
256 devices in a mesh: groups: 2 (over y), seq: 64 (over x, z), width: 2 (over core).
Axes of the slice: x: 4, y: 2, z: 16, core: 2. Of those that a mesh axis runs over, the one named last changes fastest.
The devices are a block of a 4x16x16 slice.
Arguments:
- span_tokens: bfloat16 [4096, 16384], P(('groups', 'seq'), 'width'), parts along dimension 0, may hold values from -6 to 6
- kv_weight: bfloat16 [16384, 1024], P('seq', 'width'), may hold values from -0.046875 to 0.046875
- query_weight: bfloat16 [16384, 8192], P('seq', 'width'), may hold values from -0.046875 to 0.046875
- out_weight: bfloat16 [8192, 16384], P('width', 'seq'), may hold values from -6 to 6
- cache_keys: bfloat16 [131072, 4, 128], P(('groups', 'seq'), 'width'), parts along dimension 0, may hold values from -1000 to 1000
- cache_values: bfloat16 [131072, 4, 128], P(('groups', 'seq'), 'width'), parts along dimension 0, may hold values from -6 to 6
- hidden: bfloat16 [2, 64, 16384], P(None, 'groups', 'seq'), parts along dimension 1, may hold values from -6 to 6
- lengths: int32 [64], P('groups'), parts along dimension 0, may hold values from 1 to 65536
- offset: int32 [2], P('groups'), parts along dimension 0, may hold values from 32768 to 65536
Outputs:
- span_kv: bfloat16 [4096, 1024], P(('groups', 'seq'), 'width'), parts along dimension 0
- attended: bfloat16 [2, 64, 16384], P(None, 'groups', ('seq', 'width')), parts along dimension 1
There are 2 independent parts, one for each index of `groups`. A program takes and returns all parts, laid end to end along the dimension named above; an argument that names none is the same for every part. Nothing has to cross between parts.
All inputs are finite; a program needn't handle non-finite values.
Results may differ from a plain program's by a relative error of at most 0.014.
The roundings to bfloat16 on the way count: a program that leaves them out, or rounds other values in their place, can miss the bound.
Values may be sent and summed in bfloat16 or wider, within the bound.
No kernel may reach another device: no remote copies, remote signals or barrier semaphores. Data moves between devices by JAX's collectives and lax.ppermute only.
A program may use at most 128 MiB of HBM per device.

v0:
```python
import math

import jax
import jax.numpy as jnp
from jax import lax
from jax.sharding import Mesh
from jax.sharding import PartitionSpec as P

HD = 128
QH = 64
KVH = 4
KEY_BLOCK = 256
SEQ = ("seq_0", "seq_1")
GROUPS_SEQ = ("groups", "seq_0", "seq_1")
SEQ_WIDTH = ("seq_0", "seq_1", "width")


MASKED_SCORE = -1e30


def joined_along(pieces, dim):
    dims = list(pieces.shape[1:])
    dims[dim] *= pieces.shape[0]
    return jnp.moveaxis(pieces, 0, dim).reshape(dims)


def copy_for_each(x, axis):
    copies = jnp.broadcast_to(x, (lax.axis_size(axis), *x.shape))
    return lax.all_to_all(copies, axis, split_axis=0, concat_axis=0, tiled=True)


def gathered_copies(x, axis, dim):
    return joined_along(copy_for_each(x, axis), dim)


def summed_rows(total, axes):
    for axis in axes:
        total = lax.psum_scatter(total, axis, scatter_dimension=0, tiled=True)
    return total


def stacked_from(x, axes, order):
    pieces = x
    for k in order:
        pieces = lax.all_gather(pieces, axes[k])
    done = order[::-1]
    back = [done.index(k) for k in range(len(axes))]
    pieces = pieces.transpose(*back, *range(len(axes), pieces.ndim))
    return pieces.reshape(-1, *x.shape)


def whole_of(x, axes, order, dim):
    return joined_along(stacked_from(x, axes, order), dim)


def side_by_side(arrays, axis, split_dim, concat_dim, along):
    columns = [a.reshape(*a.shape[:along], -1) for a in arrays]
    both = jnp.concatenate(columns, axis=along)
    out, at, gathered = (
        lax.all_to_all(both, axis, split_axis=split_dim, concat_axis=concat_dim, tiled=True),
        0,
        [],
    )
    for a, column in zip(arrays, columns):
        section = out[..., at : at + column.shape[along]]
        gathered.append(section.reshape(*section.shape[:along], *a.shape[along:]))
        at += column.shape[along]
    return tuple(gathered)


def split_up(x, dim, size):
    before, after = (x.shape[:dim], x.shape[dim + 1 :])
    return jnp.moveaxis(x.reshape(*before, size, -1, *after), dim, 0)


def summed_on_arrival(x, axis, dim):
    size = lax.axis_size(axis)
    pieces = lax.all_to_all(split_up(x, dim, size), axis, 0, 0, tiled=True)
    return jnp.sum(pieces.astype(jnp.float32), axis=0)


def combine(earlier, later):
    highest = jnp.maximum(earlier[0], later[0])
    keep_a = jnp.exp(earlier[0] - highest)
    keep_b = jnp.exp(later[0] - highest)
    return (
        highest,
        earlier[1] * keep_a + later[1] * keep_b,
        earlier[2] * keep_a[..., None] + later[2] * keep_b[..., None],
    )


def weigh_block(scores, allowed):
    masked = jnp.where(allowed, scores, MASKED_SCORE)
    highest = jnp.max(masked, axis=-1)
    weights = jnp.where(allowed, jnp.exp(masked - highest[..., None]), 0.0)
    return (highest, jnp.sum(weights, axis=-1), weights.astype(jnp.bfloat16))


def shared_block(queries, key_block, value_block, allowed, factor):
    scores = (
        jnp.einsum("hqd,khd->hqk", queries, key_block, preferred_element_type=jnp.float32) * factor
    )
    highest, weight_sum, weights = weigh_block(scores, allowed)
    summed = jnp.einsum("hqk,khd->hqd", weights, value_block, preferred_element_type=jnp.float32)
    return (highest, weight_sum, summed)


def local(
    span_tokens,
    kv_weight,
    query_weight,
    out_weight,
    cache_keys,
    cache_values,
    hidden,
    lengths,
    offset,
):
    factor = 1.0 / math.sqrt(HD)
    grouped = QH // KVH
    local_heads = kv_weight.shape[1] // (2 * HD)
    query_width = query_weight.shape[1]
    whole_tokens = gathered_copies(span_tokens, "width", 1)
    span_kv = jnp.dot(
        whole_tokens,
        lax.all_gather(kv_weight, SEQ, axis=0, tiled=True),
        preferred_element_type=jnp.float32,
    ).astype(jnp.bfloat16)
    step_count = hidden.shape[0]
    branch_count = hidden.shape[1]
    row_count = step_count * branch_count
    flat_rows = row_count * grouped
    states = hidden.reshape(row_count, hidden.shape[2])
    own_rows = summed_rows(
        jnp.concatenate(
            [
                jnp.dot(states, query_weight, preferred_element_type=jnp.float32),
                jnp.dot(states, kv_weight, preferred_element_type=jnp.float32),
            ],
            axis=1,
        ),
        SEQ,
    )
    projected = whole_of(own_rows.astype(jnp.bfloat16), SEQ, (0, 1), 0)
    query_part = projected[:, :query_width]
    queries = query_part.reshape(row_count, local_heads, grouped, HD).transpose(1, 0, 2, 3)
    queries = queries.reshape(local_heads, flat_rows, HD)
    fresh_pairs = projected[:, query_width:].reshape(step_count, branch_count, local_heads, 2, HD)
    visible = jnp.minimum(lengths, offset[0])
    visible_flat = jnp.repeat(jnp.tile(visible, step_count), grouped)
    cache_rows = cache_keys.shape[0]
    blocks = cache_rows // KEY_BLOCK
    anchor = lax.axis_index(SEQ) * cache_rows
    key_blocks = cache_keys.reshape(blocks, KEY_BLOCK, local_heads, HD)
    value_blocks = cache_values.reshape(blocks, KEY_BLOCK, local_heads, HD)
    leading = anchor + jnp.arange(blocks, dtype=jnp.int32) * KEY_BLOCK

    def cache_step(running, pieces):
        key_block, value_block, begin_at = pieces
        places = begin_at + jnp.arange(KEY_BLOCK, dtype=jnp.int32)
        allowed = (places[None, :] < visible_flat[:, None])[None]
        return (
            combine(running, shared_block(queries, key_block, value_block, allowed, factor)),
            None,
        )

    start_state = (
        jnp.full((local_heads, flat_rows), MASKED_SCORE, jnp.float32),
        jnp.zeros((local_heads, flat_rows), jnp.float32),
        jnp.zeros((local_heads, flat_rows, HD), jnp.float32),
    )
    cache_part, unused = lax.scan(cache_step, start_state, (key_blocks, value_blocks, leading))
    span_pairs = span_kv.reshape(span_kv.shape[0], local_heads, 2, HD)
    everywhere = jnp.ones((1, 1, 1), jnp.bool_)
    span_part = shared_block(queries, span_pairs[:, :, 0], span_pairs[:, :, 1], everywhere, factor)
    local_part = combine(cache_part, span_part)
    grid = query_part.reshape(step_count, branch_count, local_heads, grouped, HD)
    self_scores = (
        jnp.einsum(
            "tbhgd,ubhd->htbgu", grid, fresh_pairs[:, :, :, 0], preferred_element_type=jnp.float32
        )
        * factor
    )
    self_scores = self_scores.reshape(local_heads, flat_rows, step_count)
    causal = jnp.arange(step_count)[None, :] <= jnp.arange(step_count)[:, None]
    allowed = jnp.broadcast_to(
        causal[:, None, None, :], (step_count, branch_count, grouped, step_count)
    )
    allowed = allowed.reshape(flat_rows, step_count)[None]
    highest, weight_sum, weights = weigh_block(self_scores, allowed)
    weights = weights.reshape(local_heads, step_count, branch_count, grouped, step_count)
    summed = jnp.einsum(
        "htbgu,ubhd->htbgd", weights, fresh_pairs[:, :, :, 1], preferred_element_type=jnp.float32
    ).reshape(local_heads, flat_rows, HD)
    own_part = (highest, weight_sum, summed)
    received = side_by_side(
        (local_part[0][None], local_part[1][None], local_part[2][None]), SEQ, 2, 0, 3
    )
    highest = jnp.max(received[0], axis=0)
    keep = jnp.exp(received[0] - highest[None])
    folded = (
        highest,
        jnp.sum(received[1] * keep, axis=0),
        jnp.sum(received[2] * keep[..., None], axis=0),
    )
    share = flat_rows // lax.axis_size(SEQ)
    begin_at = lax.axis_index(SEQ) * share
    own_slice = tuple((lax.dynamic_slice_in_dim(member, begin_at, share, 1) for member in own_part))
    finished = combine(folded, own_slice)
    ready = (finished[2] / finished[1][..., None]).astype(jnp.bfloat16)
    attended = whole_of(ready, SEQ, (0, 1), 1)
    flat_out = attended.reshape(local_heads, row_count, grouped, HD).transpose(1, 0, 2, 3)
    flat_out = flat_out.reshape(row_count, query_width)
    partial_out = jnp.dot(flat_out, out_weight, preferred_element_type=jnp.float32)
    partial_out = partial_out.reshape(step_count, branch_count, out_weight.shape[1])
    summed_out = summed_on_arrival(partial_out.astype(jnp.bfloat16), "width", 2).astype(
        jnp.bfloat16
    )
    return (span_kv, summed_out)


def solution(mesh):
    finer = Mesh(
        mesh.devices.reshape(mesh.shape["groups"], 4, 16, mesh.shape["width"]),
        ("groups", "seq_0", "seq_1", "width"),
    )
    placed = (
        P(GROUPS_SEQ, "width"),
        P(SEQ, "width"),
        P(SEQ, "width"),
        P("width", SEQ),
        P(GROUPS_SEQ, "width", None),
        P(GROUPS_SEQ, "width", None),
        P(None, "groups", SEQ),
        P("groups"),
        P("groups"),
    )
    return jax.shard_map(
        local,
        mesh=finer,
        in_specs=placed,
        out_specs=(P(GROUPS_SEQ, "width"), P(None, "groups", SEQ_WIDTH)),
        check_vma=False,
    )
```

profile of v0, /device:TPU:33, one launch (start us, length us, event | category | flops | bytes accessed | tf_op | source)
XLA Modules:
  0.0 411.4 jit_solution(6676132296852941662)
XLA Ops:
  8.1 1.3 fusion.53
  9.7 1.2 fusion.52
  11.0 1.1 pad_maximum_fusion
  12.2 0.6 all-gather.8.cloned.1.call-update
  12.8 1.1 broadcast_in_dim.88
  13.9 24.1 %all-to-all-start = ((bf16[2,32,8192]{2,1,0:T(8,128)(2,1)}), bf16[2,32,8192]{2,1,0:T(8,128)(2,1)S(1)}, u32[]{:S(2)}, u32[]{:S(2)}) async-start(bf16[2,32,8192]{2,1,0:T(8,128)(2,1)} %broadcast_in_dim.88), calls=%async_computation | async-start | bytes 2097152 | tf_op jit(solution)/shard_map/all_to_all | solution.py:29
  38.0 1.7 all-to-all-done
  39.8 1.1 copy.172
  41.6 0.6 dynamic-slice
  42.2 14.9 %reduce-scatter.2.cloned.1.call-done = f32[16,4608]{1,0:T(8,128)} async-done(((f32[64,4608]{1,0:T(8,128)}), f32[16,4608]{1,0:T(8,128)}) %reduce-scatter.2.cloned.1.call-update) | async-done | bytes 294928 | tf_op jit(solution)/shard_map/reduce_scatter | solution.py:38
  57.1 52.6 %all-reduce.2 = bf16[16,4608]{1,0:T(8,128)(2,1)S(1)} all-reduce(f32[16,4608]{1,0:T(8,128)} %reduce-scatter.2.cloned.1.call-done), channel_id=7, replica_groups=mesh['groups'=2,'seq_0'=4,'seq_1'=16,'width'=2] {'seq_1'}, use_global_device_ids=true, to_apply=%region_1.0.clone | all-reduce | flops 73728 | bytes 442368
  109.7 0.7 fusion.37
  110.4 9.5 %all-gather.4 = bf16[4,1,4608]{2,1,0:T(2,128)(2,1)S(1)} all-gather(bf16[1,1,4608]{2,1,0:T(2,128)(2,1)S(1)} %fusion.37), channel_id=2, replica_groups=mesh['groups'=2,'seq_0'=4,'seq_1'=16,'width'=2] {'seq_0'}, dimensions={0}, use_global_device_ids=true | all-gather | bytes 46080 | tf_op jit(solution)/shard_map/all_gather | solution.py:45
  119.9 27.5 %all-gather.5 = bf16[16,4,4608]{2,1,0:T(4,128)(2,1)S(1)} all-gather(bf16[1,4,4608]{2,1,0:T(4,128)(2,1)S(1)} %bitcast.163), channel_id=3, replica_groups=mesh['groups'=2,'seq_0'=4,'seq_1'=16,'width'=2] {'seq_1'}, dimensions={0}, use_global_device_ids=true | all-gather | bytes 626688 | tf_op jit(solution)/shard_map/all_gather | solution.py:45
  147.6 0.7 copy-done.2
  148.3 0.8 copy-done.3
  149.2 38.0 %while.15 = (s32[]{:T(128)}, f32[2,1024]{1,0:T(2,128)S(1)}, f32[2,1024]{1,0:T(2,128)S(1)}, f32[2,1024,128]{2,1,0:T(8,128)}, s32[4]{0:T(128)S(1)}, /*index=5*/bf1...) while((s32[]{:T(128)}, f32[2,1024]{1,0:T(2,128)S(1)}, ...), condition=%wide.region_5.6_spmd.clone, body=%wide.region_2.5_spmd.clone.sunk | while | flops 276574464 | bytes 19270064 | solution.py:173
  149.3 0.6 dynamic_slice.40
  149.9 0.6 iota_add_fusion.2
  150.8 1.2 constant_dynamic-slice_fusion.5
  152.0 0.6 fusion.71
  152.6 1.3 copy-done.1
  153.9 0.6 fusion.72
  154.5 3.9 fusion.74
  158.6 0.6 dynamic_slice.40
  159.2 0.6 iota_add_fusion.2
  160.0 1.2 constant_dynamic-slice_fusion.5
  161.2 0.6 fusion.71
  161.8 1.3 copy-done.1
  163.1 0.6 fusion.72
  163.8 4.3 %fusion.74 = f32[2,1024,128]{2,1,0:T(8,128)} fusion(f32[2,256,1024]{2,1,0:T(8,128)} %copy-done.1, f32[2,1024,128]{2,1,0:T(8,128)} %get-tuple-element.267, f32[2,1024]{1,0:T(2,128)S(1)} %get-tuple-element.247, pred[1024,256]{0,1:T(8,128)(4,1)S(1)} %broadcast_compare_fusion.2, f32[2,1024]{1,0:T(2,128)S(1)} %get-tuple-element.250, ...), kind=kOutput, calls=%fused_computation.7.clone.1 | convolution fusion | flops 137887744 | bytes 4612097 | tf_op jit(solution)/shard_map/while/body/eval_jaxpr/hqk,khd->hqd/dot_general | solution.py:105
  168.2 0.6 dynamic_slice.40
  168.8 0.6 iota_add_fusion.2
  169.7 1.2 constant_dynamic-slice_fusion.5
  170.9 0.6 fusion.71
  171.5 1.3 copy-done.1
  172.8 0.6 fusion.72
  173.4 4.2 %fusion.74 = f32[2,1024,128]{2,1,0:T(8,128)} fusion(f32[2,256,1024]{2,1,0:T(8,128)} %copy-done.1, f32[2,1024,128]{2,1,0:T(8,128)} %get-tuple-element.267, f32[2,1024]{1,0:T(2,128)S(1)} %get-tuple-element.247, pred[1024,256]{0,1:T(8,128)(4,1)S(1)} %broadcast_compare_fusion.2, f32[2,1024]{1,0:T(2,128)S(1)} %get-tuple-element.250, ...), kind=kOutput, calls=%fused_computation.7.clone.1 | convolution fusion | flops 137887744 | bytes 4612097 | tf_op jit(solution)/shard_map/while/body/eval_jaxpr/hqk,khd->hqd/dot_general | solution.py:105
  177.8 0.6 dynamic_slice.40
  178.4 0.6 iota_add_fusion.2
  179.2 1.2 constant_dynamic-slice_fusion.5
  180.4 0.6 fusion.71
  181.0 1.3 copy-done.1
  182.3 0.6 fusion.72
  183.0 4.2 %fusion.74 = f32[2,1024,128]{2,1,0:T(8,128)} fusion(f32[2,256,1024]{2,1,0:T(8,128)} %copy-done.1, f32[2,1024,128]{2,1,0:T(8,128)} %get-tuple-element.267, f32[2,1024]{1,0:T(2,128)S(1)} %get-tuple-element.247, pred[1024,256]{0,1:T(8,128)(4,1)S(1)} %broadcast_compare_fusion.2, f32[2,1024]{1,0:T(2,128)S(1)} %get-tuple-element.250, ...), kind=kOutput, calls=%fused_computation.7.clone.1 | convolution fusion | flops 137887744 | bytes 4612097 | tf_op jit(solution)/shard_map/while/body/eval_jaxpr/hqk,khd->hqd/dot_general | solution.py:105
  187.1 2.6 copy.136
  189.7 32.7 %all-gather.8.cloned.1.call-done = bf16[16384,512]{1,0:T(8,128)(2,1)} async-done(((bf16[256,512]{1,0:T(8,128)(2,1)}), bf16[16384,512]{1,0:T(8,128)(2,1)}) %all-gather.8.cloned.1.call-update) | async-done | bytes 16777232 | tf_op jit(solution)/shard_map/all_gather | solution.py:127
  222.4 9.0 %convolution_convert_fusion = bf16[32,512]{1,0:T(8,128)(2,1)S(1)} fusion(bf16[32,16384]{1,0:T(8,128)(2,1)} %bitcast.153, bf16[16384,512]{1,0:T(8,128)(2,1)} %all-gather.8.cloned.1.call-done), kind=kOutput, calls=%fused_computation.43 | convolution fusion | flops 536887296 | bytes 17858560 | tf_op jit(solution)/shard_map/dot_general | solution.py:125
  232.0 1.6 fusion.22
  233.7 2.3 copy.139
  236.0 11.9 %all-to-all-start.1 = ((f32[1,2,1024,130]{3,1,0,2:T(2,128)}), f32[1,2,1024,130]{3,1,0,2:T(2,128)}, u32[]{:S(2)}, u32[]{:S(2)}) async-start(f32[1,2,1024,130]{3,1,0,2:T(2,128)} %copy.139), calls=%async_computation.2 | async-start | bytes 4194304 | tf_op jit(solution)/shard_map/all_to_all | solution.py:60
  248.0 0.8 slice.41
  248.9 1.4 fusion.50
  251.5 86.9 %all-to-all-done.1 = f32[1,2,1024,130]{3,1,0,2:T(2,128)} async-done(((f32[1,2,1024,130]{3,1,0,2:T(2,128)}), f32[1,2,1024,130]{3,1,0,2:T(2,128)}, u32[]{:S(2)}, u32[]{:S(2)}) %all-to-all-start.1) | async-done | bytes 1064992 | tf_op jit(solution)/shard_map/all_to_all | solution.py:60
  338.4 4.4 %copy.141 = f32[1,2,64,16,130]{2,3,4,1,0:T(8,128)} copy(f32[1,2,64,16,130]{4,1,3,2,0:T(2,128)} %bitcast.15) | data formatting | bytes 2129920 | tf_op jit(solution)/shard_map/all_to_all | solution.py:60
  342.8 0.8 slice_reduce_fusion
  343.6 0.8 exponential_bitcast_fusion
  344.4 0.9 fusion.39
  345.3 2.2 fusion.18
  347.8 9.1 %all-gather.2 = bf16[8,16,128]{2,1,0:T(8,128)(2,1)S(1)} all-gather(bf16[2,16,128]{2,1,0:T(8,128)(2,1)S(1)} %divide_convert_fusion), channel_id=4, replica_groups=mesh['groups'=2,'seq_0'=4,'seq_1'=16,'width'=2] {'seq_0'}, dimensions={0}, use_global_device_ids=true | all-gather | bytes 40960 | tf_op jit(solution)/shard_map/all_gather | solution.py:45
  356.9 28.0 %all-gather.3 = bf16[64,2,16,128]{3,2,1,0:T(8,128)(2,1)S(1)} all-gather(bf16[4,2,16,128]{3,2,1,0:T(8,128)(2,1)S(1)} %bitcast.166), channel_id=5, replica_groups=mesh['groups'=2,'seq_0'=4,'seq_1'=16,'width'=2] {'seq_1'}, dimensions={0}, use_global_device_ids=true | all-gather | bytes 557056 | tf_op jit(solution)/shard_map/all_gather | solution.py:45
  385.2 2.1 fusion.28
  387.2 16.1 %all_to_all.28 = bf16[2,2,32,128]{3,2,1,0:T(8,128)(2,1)S(1)} all-to-all(bf16[2,2,32,128]{3,2,1,0:T(8,128)(2,1)S(1)} %bitcast.167), channel_id=1, replica_groups=mesh['groups'=2,'seq_0'=4,'seq_1'=16,'width'=2] {'width'}, dimensions={0} | all-to-all | bytes 65536 | tf_op jit(solution)/shard_map/all_to_all | solution.py:78
  403.3 0.6 reduce_sum.64
  (76 shorter events, 4.9 us)
Async XLA Ops:
  8.0 1.7 copy-start
  8.0 49.1 %reduce-scatter.2.cloned.1.call-start = ((), (), s32[]{:S(2)}) async-start(), calls=%async_computation.5 | async-start | bytes 1474560 | tf_op jit(solution)/shard_map/reduce_scatter | solution.py:38
  11.0 1.8 copy-start.5
  12.1 210.3 %all-gather.8.cloned.1.call-start = ((), (), s32[]{:S(2)}) async-start(), calls=%async_computation.4 | async-start | bytes 17039360 | tf_op jit(solution)/shard_map/all_gather | solution.py:127
  13.9 27.6 %copy-start.7 = (s32[32]{0:T(128)S(1)}, s32[32]{0:T(128)}, u32[]{:S(2)}) copy-start(s32[32]{0:T(128)} %param.18) | copy-start | bytes 388
  13.9 27.7 %copy-start.8 = (u32[256]{0:T(256)S(1)}, u32[256]{0:T(256)}, u32[]{:S(2)}) copy-start(u32[256]{0:T(256)} %constant.56) | copy-start | bytes 3076
  13.9 25.9 %all-to-all-start = ((bf16[2,32,8192]{2,1,0:T(8,128)(2,1)}), bf16[2,32,8192]{2,1,0:T(8,128)(2,1)S(1)}, u32[]{:S(2)}, u32[]{:S(2)}) async-start(bf16[2,32,8192]{2,1,0:T(8,128)(2,1)} %broadcast_in_dim.88), calls=%async_computation | async-start | bytes 2097152 | tf_op jit(solution)/shard_map/all_to_all | solution.py:29
  147.5 0.8 copy-start.2
  148.3 0.8 copy-start.3
  152.6 1.4 copy-start.1
  161.8 1.4 copy-start.1
  171.5 1.4 copy-start.1
  181.0 1.4 copy-start.1
  231.5 2.2 copy-start.6
  236.0 12.9 %copy-start.4 = (bf16[8,8,32,128]{3,2,1,0:T(8,128)(2,1)S(1)}, bf16[8,8,32,128]{3,2,1,0:T(8,128)(2,1)}, u32[]{:S(2)}) copy-start(bf16[8,8,32,128]{3,2,1,0:T(8,128)(2,1)} %copy-done.3) | copy-start | bytes 1572868
  236.0 102.4 %all-to-all-start.1 = ((f32[1,2,1024,130]{3,1,0,2:T(2,128)}), f32[1,2,1024,130]{3,1,0,2:T(2,128)}, u32[]{:S(2)}, u32[]{:S(2)}) async-start(f32[1,2,1024,130]{3,1,0,2:T(2,128)} %copy.139), calls=%async_computation.2 | async-start | bytes 4194304 | tf_op jit(solution)/shard_map/all_to_all | solution.py:60
Sparse Core Ops, SparseCore 0:
  12.3 44.7 reduce-scatter.1
Sparse Core Ops, SparseCore 1:
  15.1 207.3 all-gather.7
where the time goes:
time: 413 us; the launch traced here: 411 us
  blocking collectives  143 us (35%)
  waiting for transfers between devices  137 us (33%)
  starting transfers between devices  36.2 us (9%)
  matrix products  36.2 us (9%)
  local copies, waits for them, and re-layouts  29.7 us (7%)
  between operations  16.5 us (4%)
  other arithmetic  13.1 us (3%)
    all_to_all x1, waiting for transfers between devices, side_by_side(): lax.all_to_all(both, axis, split_axis=split_dim, concat_axis=concat_dim,...  86.9 us
    all_gather x4, blocking collectives, stacked_from(): pieces = lax.all_gather(pieces, axes[k])  74 us
    unnamed x1, blocking collectives  52.6 us
    all_gather x1, waiting for transfers between devices, local(): lax.all_gather(kv_weight, SEQ, axis=0, tiled=True)  32.7 us
    all_to_all x1, starting transfers between devices, copy_for_each(): return lax.all_to_all(copies, axis, split_axis=0, concat_axis=0, tiled=True)  24.1 us
    dot_general x5, matrix products, shared_block(): jnp.einsum('hqk,khd->hqd', weights, value_block, preferred_element_type=j...  18.1 us
    all_to_all x1, blocking collectives, summed_on_arrival(): pieces = lax.all_to_all(split_up(x, dim, size), axis, 0, 0, tiled=True)  16.1 us
    reduce_scatter x1, waiting for transfers between devices, summed_rows(): total = lax.psum_scatter(total, axis, scatter_dimension=0, tiled=True)  14.9 us
  transfers between devices with their start and end apart: 4, of which 4 were waited for; matrix products, arithmetic and copies ran while one was open for 10% of the time, Pallas kernels for 0%

commit v1 on v0

v1 whole, which is shorter than its diff:
```python
import math

import jax
import jax.numpy as jnp
from jax import lax
from jax.experimental import pallas as pl
from jax.experimental.pallas import tpu as pltpu
from jax.sharding import Mesh
from jax.sharding import PartitionSpec as P

HD = 128
QH = 64
KVH = 4
SEQ = ("x", "z")
GROUPS_SEQ = ("groups", "x", "z")
SEQ_WIDTH = ("x", "z", "width")
MASKED_SCORE = -1e30
LOG2E = 1.4426950408889634
F32 = jnp.float32
BF16 = jnp.bfloat16


def exchanged(pieces, axis):
    return lax.all_to_all(pieces, axis, split_axis=0, concat_axis=0, tiled=True)


def copies_from(x, axis):
    return exchanged(jnp.broadcast_to(x, (lax.axis_size(axis), *x.shape)), axis)


def dot_f32(a, b):
    return jnp.dot(a, b, preferred_element_type=F32)


def project_body(states_ref, query_ref, fresh_ref, out_ref):
    states = states_ref[...]
    columns = query_ref.shape[1]
    out_ref[0, :, :columns] = dot_f32(states, query_ref[...])
    out_ref[0, :, columns:] = dot_f32(states, fresh_ref[...])


def project(states, query_weight, kv_weight, pieces):
    rows, depth = states.shape
    columns = query_weight.shape[1] // pieces
    extra = kv_weight.shape[1] // pieces
    return pl.pallas_call(
        project_body,
        grid=(pieces,),
        in_specs=[
            pl.BlockSpec((rows, depth), lambda c: (0, 0)),
            pl.BlockSpec((depth, columns), lambda c: (0, c)),
            pl.BlockSpec((depth, extra), lambda c: (0, c)),
        ],
        out_specs=pl.BlockSpec((1, rows, columns + extra), lambda c: (c, 0, 0)),
        out_shape=jax.ShapeDtypeStruct((pieces, rows, columns + extra), F32),
        name="project",
    )(states, query_weight, kv_weight)


def three_parts(x):
    high = x.astype(BF16).astype(F32)
    rest = x - high
    middle = rest.astype(BF16).astype(F32)
    return (high, middle, rest - middle)


def put_stats(lane, stats, head, heads, highest, total):
    for place, value in enumerate((*three_parts(highest), *three_parts(total))):
        stats = jnp.where(lane == place * heads + head, value, stats)
    return stats


def joined_stats(tail, heads):
    lanes = tail.shape[-1]
    whole = (
        tail + pltpu.roll(tail, lanes - heads, 1) + pltpu.roll(tail, lanes - 2 * heads, 1)
    )
    return whole, pltpu.roll(whole, lanes - 3 * heads, 1)


def split_stats(lane, highest, total, heads):
    parts = (*three_parts(highest), *three_parts(total))
    stats = jnp.where(lane < heads, parts[0], 0.0)
    for place in range(1, 6):
        here = (lane >= place * heads) & (lane < (place + 1) * heads)
        stats = jnp.where(here, pltpu.roll(parts[place], place * heads, 1), stats)
    return stats


def attend_body(q_ref, keys_ref, values_ref, span_ref, bias_ref, out_ref, k_ref, v_ref, *, scale):
    slots = keys_ref.shape[1]
    span = span_ref.shape[0]
    rows = q_ref.shape[1]
    heads = (q_ref.shape[2] - HD) // HD
    per_dot = 4
    total_keys = k_ref.shape[0]
    blank = jnp.zeros((total_keys - slots - span - rows, HD), BF16)
    k_ref[:slots, :] = keys_ref[0]
    v_ref[:slots, :] = values_ref[0]
    at = heads * HD
    k_ref[slots:, :] = jnp.concatenate([span_ref[:, :HD], q_ref[0, :, at:], blank], axis=0)
    v_ref[slots:, :] = jnp.concatenate([span_ref[:, HD:], q_ref[1, :, at:], blank], axis=0)
    bias = bias_ref[...]
    lane = lax.broadcasted_iota(jnp.int32, (rows, HD), 1)
    for piece in range(2):
        stats = jnp.zeros((rows, HD), F32)
        for first in range(0, heads, per_dot):
            q = jnp.concatenate(
                [
                    q_ref[piece, :, (first + i) * HD : (first + i + 1) * HD]
                    for i in range(per_dot)
                ],
                axis=0,
            )
            scores = lax.dot_general(
                q, k_ref[...], (((1,), (1,)), ((), ())), preferred_element_type=F32
            )
            scores = scores.reshape(per_dot, rows, total_keys) * scale + bias[None]
            highest = jnp.max(scores, axis=-1, keepdims=True)
            weights = jnp.exp2(scores - highest)
            total = jnp.sum(weights, axis=-1, keepdims=True)
            summed = dot_f32(
                weights.reshape(per_dot * rows, total_keys).astype(BF16), v_ref[...]
            )
            for i in range(per_dot):
                head = first + i
                out_ref[piece, :, head * HD : (head + 1) * HD] = summed[
                    i * rows : (i + 1) * rows
                ].astype(BF16)
                stats = put_stats(lane, stats, head, heads, highest[i], total[i])
        out_ref[piece, :, at:] = stats.astype(BF16)


def attend(projected, keys, values, span_kv, bias, scale):
    pieces, rows, width = projected.shape
    local_heads, slots, _ = keys.shape
    span = span_kv.shape[0]
    per_head = pieces // local_heads
    total_keys = bias.shape[1]
    body = lambda *refs: attend_body(*refs, scale=scale)
    return pl.pallas_call(
        body,
        grid=(local_heads,),
        in_specs=[
            pl.BlockSpec((per_head, rows, width), lambda h: (h, 0, 0)),
            pl.BlockSpec((1, slots, HD), lambda h: (h, 0, 0)),
            pl.BlockSpec((1, slots, HD), lambda h: (h, 0, 0)),
            pl.BlockSpec((span, 2 * HD), lambda h: (0, h)),
            pl.BlockSpec((rows, total_keys), lambda h: (0, 0)),
        ],
        out_specs=pl.BlockSpec((per_head, rows, width), lambda h: (h, 0, 0)),
        out_shape=jax.ShapeDtypeStruct((pieces, rows, width), BF16),
        scratch_shapes=[pltpu.VMEM((total_keys, HD), BF16), pltpu.VMEM((total_keys, HD), BF16)],
        name="attend",
    )(projected, keys, values, span_kv, bias)


def fold_body(in_ref, out_ref):
    sources, rows, width = in_ref.shape
    heads = (width - HD) // HD
    at = heads * HD
    lane = lax.broadcasted_iota(jnp.int32, (rows, HD), 1)
    stats = [joined_stats(in_ref[s, :, at:].astype(F32), heads) for s in range(sources)]
    highest = stats[0][0]
    for s in range(1, sources):
        highest = jnp.maximum(highest, stats[s][0])
    keeps = [jnp.exp2(jnp.where(lane < heads, m - highest, 0.0)) for m, _ in stats]
    total = keeps[0] * stats[0][1]
    for s in range(1, sources):
        total = total + keeps[s] * stats[s][1]
    for head in range(heads):
        cut = slice(head * HD, (head + 1) * HD)
        summed = in_ref[0, :, cut].astype(F32) * keeps[0][:, head : head + 1]
        for s in range(1, sources):
            summed = summed + in_ref[s, :, cut].astype(F32) * keeps[s][:, head : head + 1]
        out_ref[:, cut] = summed.astype(BF16)
    out_ref[:, at:] = split_stats(lane, highest, total, heads).astype(BF16)


def fold(received):
    sources, rows, width = received.shape
    return pl.pallas_call(
        fold_body,
        out_shape=jax.ShapeDtypeStruct((rows, width), BF16),
        name="fold",
    )(received)


def finish_body(in_ref, out_ref, *, group):
    rows, width = in_ref.shape
    heads = (width - HD) // HD
    at = heads * HD
    lane = lax.broadcasted_iota(jnp.int32, (rows, HD), 1)
    peak, total = joined_stats(in_ref[:, at:].astype(F32), heads)
    peak = jnp.where(lane < heads, peak, 0.0)
    highest = peak
    shift = group
    while shift < rows:
        highest = jnp.maximum(highest, pltpu.roll(highest, shift, 0))
        shift *= 2
    keep = jnp.exp2(peak - highest)
    total = keep * total

    def over_sources(x):
        size = 8
        y = x[:size]
        for first in range(size, rows, size):
            y = y + x[first : first + size]
        shift = group
        while shift < size:
            y = y + pltpu.roll(y, shift, 0)
            shift *= 2
        return y

    total = over_sources(total)
    for head in range(heads):
        cut = slice(head * HD, (head + 1) * HD)
        summed = over_sources(in_ref[:, cut].astype(F32) * keep[:, head : head + 1])
        out_ref[:, cut] = (summed / total[:, head : head + 1]).astype(BF16)


def finish(received):
    sources, group, width = received.shape
    flat = received.reshape(sources * group, width)
    out = pl.pallas_call(
        lambda *refs: finish_body(*refs, group=group),
        out_shape=jax.ShapeDtypeStruct((8, width - HD), BF16),
        name="finish",
    )(flat)
    return out[:group]


def close_body(att_ref, weight_ref, out_ref):
    pieces, rows, depth = att_ref.shape
    total = dot_f32(att_ref[0], weight_ref[:depth, :])
    for c in range(1, pieces):
        total = total + dot_f32(att_ref[c], weight_ref[c * depth : (c + 1) * depth, :])
    halves = out_ref.shape[0]
    columns = out_ref.shape[2]
    for w in range(halves):
        out_ref[w] = total[:, w * columns : (w + 1) * columns]


def close(attention, out_weight, halves):
    pieces, rows, depth = attention.shape
    return pl.pallas_call(
        close_body,
        out_shape=jax.ShapeDtypeStruct((halves, rows, out_weight.shape[1] // halves), F32),
        name="close",
    )(attention, out_weight)


def span_projection(span_tokens, kv_weight, after):
    xs = lax.axis_size("x")
    tokens, half = span_tokens.shape
    x = lax.axis_index("x")
    weights = lax.all_gather(kv_weight, "z", axis=0, tiled=True)
    depth = weights.shape[0]
    per_core = half // depth
    order = [(a, w) for a in range(xs) for w in range(2)]

    def flat(a, w):
        return a * 2 + w

    first = [(flat(a, w), flat(2 * w + (a & 1), a >> 1)) for a, w in order]
    second = [(flat(a, w), flat(2 * w + 1 - (a & 1), a >> 1)) for a, w in order]
    low = span_tokens[:, :depth]
    high = span_tokens[:, depth:]
    odd = (x & 1) == 1
    one = lax.ppermute(jnp.where(odd, high, low), ("x", "width"), first)
    two = lax.ppermute(jnp.where(odd, low, high), ("x", "width"), second)
    mine = jnp.stack([jnp.where(odd, two, one), jnp.where(odd, one, two)])
    theirs = lax.ppermute(mine, "width", [(0, 1), (1, 0)])
    upper = lax.axis_index("width") == 1
    ready = jnp.concatenate(
        [jnp.where(upper, theirs, mine), jnp.where(upper, mine, theirs)], axis=0
    )
    ready, after = lax.optimization_barrier((ready, after))
    partial = dot_f32(ready.reshape(xs * tokens, depth), weights)
    partial = partial.reshape(xs, tokens, kv_weight.shape[1])
    return jnp.sum(exchanged(partial, "x"), axis=0).astype(BF16), after


def local(
    span_tokens,
    kv_weight,
    query_weight,
    out_weight,
    cache_keys,
    cache_values,
    hidden,
    lengths,
    offset,
):
    xs = lax.axis_size("x")
    zs = lax.axis_size("z")
    step_count, branch_count, depth = hidden.shape
    rows = step_count * branch_count
    states = hidden.reshape(rows, depth)
    slots = cache_keys.shape[0]
    span = span_tokens.shape[0]
    scale = LOG2E / math.sqrt(HD)

    partial = project(states, query_weight, kv_weight, xs)
    own = jnp.sum(exchanged(partial, "x"), axis=0)
    own = own.reshape(zs, rows // zs, own.shape[1])
    own = jnp.sum(exchanged(own, "z"), axis=0).astype(BF16)
    columns = copies_from(own, "z").reshape(rows, own.shape[1])
    projected = copies_from(columns, "x")

    span_kv, projected = span_projection(span_tokens, kv_weight, projected)

    seat = lax.axis_index(SEQ)
    visible = jnp.tile(jnp.minimum(lengths, offset[0]), step_count)[:, None]
    places = seat * slots + jnp.arange(slots, dtype=jnp.int32)[None]
    row = jnp.arange(rows, dtype=jnp.int32)
    same = (row[:, None] % branch_count == row[None] % branch_count) & (row[None] <= row[:, None])
    filler = -(slots + span + rows) % HD
    allowed = jnp.concatenate(
        [
            places < visible,
            jnp.ones((rows, span), jnp.bool_),
            same & (seat == 0),
            jnp.zeros((rows, filler), jnp.bool_),
        ],
        axis=1,
    )
    bias = jnp.where(allowed, 0.0, MASKED_SCORE).astype(F32)
    keys = cache_keys.transpose(1, 0, 2)
    values = cache_values.transpose(1, 0, 2)

    partial = attend(projected, keys, values, span_kv, bias, scale)
    folded = fold(exchanged(partial, "x"))
    folded = folded.reshape(zs, rows // zs, folded.shape[1])
    attention = finish(exchanged(folded, "z"))
    columns = copies_from(attention, "z").reshape(rows, attention.shape[1])
    whole = copies_from(columns, "x")
    halves = exchanged(close(whole, out_weight, 2), "width")
    attended = (halves[0] + halves[1]).astype(BF16)
    return (span_kv, attended.reshape(step_count, branch_count, attended.shape[1]))


def solution(mesh):
    finer = Mesh(
        mesh.devices.reshape(mesh.shape["groups"], 4, 16, mesh.shape["width"]),
        ("groups", "x", "z", "width"),
    )
    placed = (
        P(GROUPS_SEQ, "width"),
        P(SEQ, "width"),
        P(SEQ, "width"),
        P("width", SEQ),
        P(GROUPS_SEQ, "width", None),
        P(GROUPS_SEQ, "width", None),
        P(None, "groups", SEQ),
        P("groups"),
        P("groups"),
    )
    return jax.shard_map(
        local,
        mesh=finer,
        in_specs=placed,
        out_specs=(P(GROUPS_SEQ, "width"), P(None, "groups", SEQ_WIDTH)),
        check_vma=False,
    )
```

time: 413 us -> 226 us (0.55)
  waiting for transfers between devices: 137 us -> 50.5 us
  blocking collectives: 143 us -> 70.3 us
  matrix products: 36.2 us -> 3.82 us
  local copies, waits for them, and re-layouts: 29.7 us -> 6.25 us
  starting transfers between devices: 36.2 us -> 56.9 us
  Pallas kernels: 0 us -> 18.2 us
  other arithmetic: 13.1 us -> 3.68 us
    all_gather x4 -> x0, blocking collectives: 74 us -> none  [stacked_from(): pieces = lax.all_gather(pieces, axes[k])]
    all_to_all x1 -> x5, blocking collectives: 16.1 us -> 70.3 us  [exchanged(): return lax.all_to_all(pieces, axis, split_axis=0, concat_axis=0, tiled=True)]
    unnamed x1 -> x0, blocking collectives: 52.6 us -> none
    all_to_all x2 -> x5, waiting for transfers between devices: 88.6 us -> 49.7 us  [exchanged(): return lax.all_to_all(pieces, axis, split_axis=0, concat_axis=0, tiled=True)]
    all_gather x1, waiting for transfers between devices: 32.7 us -> 0.01 us  [span_projection(): weights = lax.all_gather(kv_weight, 'z', axis=0, tiled=True)]
    dot_general x16 -> x1, matrix products: 36.2 us -> 3.82 us  [dot_f32(): return jnp.dot(a, b, preferred_element_type=F32)]
    pallas_call x0 -> x5, Pallas kernels: none -> 18.2 us  [the longest x1 7.32 us: attend(): pl.pallas_call(body, grid=(local_heads,), in_specs=[pl.BlockSpec((per_hea...]
    reduce_scatter x1 -> x0, waiting for transfers between devices: 14.9 us -> none  [summed_rows(): total = lax.psum_scatter(total, axis, scatter_dimension=0, tiled=True)]
  transfers between devices with their start and end apart: 4 -> 9, of which waited for: 4 -> 5; matrix products, arithmetic and copies ran while one was open for 10% -> 3% of each run, Pallas kernels for 0% -> 2%
where the time goes in v1:
time: 226 us; the launch traced here: 225 us
  blocking collectives  70.3 us (31%)
  starting transfers between devices  56.9 us (25%)
  waiting for transfers between devices  50.5 us (22%)
  Pallas kernels  18.2 us (8%)
  between operations  15 us (7%)
  local copies, waits for them, and re-layouts  6.25 us (3%)
  matrix products  3.82 us (2%)
  other arithmetic  3.68 us (2%)
    all_to_all x5, blocking collectives, exchanged(): return lax.all_to_all(pieces, axis, split_axis=0, concat_axis=0, tiled=True)  70.3 us
    all_to_all x5, waiting for transfers between devices, exchanged(): return lax.all_to_all(pieces, axis, split_axis=0, concat_axis=0, tiled=True)  49.7 us
    all_to_all x5, starting transfers between devices, exchanged(): return lax.all_to_all(pieces, axis, split_axis=0, concat_axis=0, tiled=True)  47.9 us
    pallas_call x1, Pallas kernels, attend(): pl.pallas_call(body, grid=(local_heads,), in_specs=[pl.BlockSpec((per_hea...  7.32 us
  transfers between devices with their start and end apart: 9, of which 5 were waited for; matrix products, arithmetic and copies ran while one was open for 3% of the time, Pallas kernels for 2%

profile of v1, /device:TPU:33, one launch (start us, length us, event | category | flops | bytes accessed | tf_op | source)
XLA Modules:
  0.0 224.5 jit_solution(8340236951440598876)
XLA Ops:
  7.2 0.0 copy-start.3
  7.2 0.1 all-gather.2.cloned.1.call-start
  7.3 0.7 all-gather.2.cloned.1.call-update
  8.0 1.1 broadcast_select_fusion.3
  9.1 4.3 %collective-permute-start = (bf16[32,4096]{1,0:T(8,128)(2,1)S(1)}, bf16[32,4096]{1,0:T(8,128)(2,1)S(1)}, u32[]{:S(2)}, u32[]{:S(2)}) collective-permute-start(bf16[32,4096]{1,0:T(8,128)(2,1)S(1)} %get-tuple-element.10), channel_id=1, source_target_pairs={{0,32},{1,96},{32,0},{33,64},{64,33},{65,97},{96,1},{97,65},{2,34}... | collective-permute-start | bytes 786440 | tf_op jit(solution)/shard_map/ppermute | solution.py:271
  13.4 2.1 collective-permute-start.1
  15.5 4.0 %project.1 = f32[4,64,1152]{2,1,0:T(8,128)} custom-call(bf16[64,256]{1,0:T(8,128)(2,1)} %bitcast.16, bf16[256,4096]{1,0:T(8,128)(2,1)} %query_ref.1, bf16[256,512]{1,0:T(8,128)(2,1)} %fresh_ref.1), custom_call_target="tpu_custom_call" | custom-call | tf_op jit(solution)/shard_map/project/pallas_call | solution.py:46
  19.5 3.6 %all-to-all-start = ((f32[4,64,1152]{2,1,0:T(8,128)}), f32[4,64,1152]{2,1,0:T(8,128)S(1)}, u32[]{:S(2)}, u32[]{:S(2)}) async-start(f32[4,64,1152]{2,1,0:T(8,128)} %project.1), calls=%async_computation | async-start | bytes 2359296 | tf_op jit(solution)/shard_map/all_to_all | solution.py:24
  23.8 0.0 copy-done.3
  23.9 0.1 lt.26
  23.9 0.1 broadcast_compare_fusion
  24.0 0.0 collective-permute-done
  24.1 0.0 collective-permute-done.1
  24.1 9.4 %all-to-all-done = f32[4,64,1152]{2,1,0:T(8,128)S(1)} async-done(((f32[4,64,1152]{2,1,0:T(8,128)}), f32[4,64,1152]{2,1,0:T(8,128)S(1)}, u32[]{:S(2)}, u32[]{:S(2)}) %all-to-all-start) | async-done | bytes 1179680 | tf_op jit(solution)/shard_map/all_to_all | solution.py:24
  33.5 0.1 reduce_sum.27
  33.6 0.8 reshape.69
  34.4 28.6 %all-to-all-start.1 = ((f32[16,4,1152]{2,1,0:T(4,128)}), f32[16,4,1152]{2,1,0:T(4,128)S(1)}, u32[]{:S(2)}, u32[]{:S(2)}) async-start(f32[16,4,1152]{2,1,0:T(4,128)} %reshape.69), calls=%async_computation.1 | async-start | bytes 589824 | tf_op jit(solution)/shard_map/all_to_all | solution.py:24
  63.0 0.1 pad_maximum_fusion.1
  63.1 2.5 %collective-permute-start.2 = (bf16[2,32,4096]{2,1,0:T(8,128)(2,1)S(1)}, bf16[2,32,4096]{2,1,0:T(8,128)(2,1)S(1)}, u32[]{:S(2)}, u32[]{:S(2)}) collective-permute-start(bf16[2,32,4096]{2,1,0:T(8,128)(2,1)S(1)} %pad_maximum_fusion.1), channel_id=1, source_target_pairs={{0,1},{1,0},{2,3},{3,2},{4,5},{5,4},{6,7},{7,6},{8,9},{9,8},{10,11... | collective-permute-start | bytes 1572872 | tf_op jit(solution)/shard_map/ppermute | solution.py:273
  65.5 0.1 fusion.4
  65.7 0.1 concatenate.7
  65.8 0.8 broadcast_select_fusion.4.refs_4_
  66.5 16.1 %all-to-all-done.1 = f32[16,4,1152]{2,1,0:T(4,128)S(1)} async-done(((f32[16,4,1152]{2,1,0:T(4,128)}), f32[16,4,1152]{2,1,0:T(4,128)S(1)}, u32[]{:S(2)}, u32[]{:S(2)}) %all-to-all-start.1) | async-done | bytes 294944 | tf_op jit(solution)/shard_map/all_to_all | solution.py:24
  82.7 0.1 reduce_sum.28
  82.7 0.7 broadcast_in_dim.31
  83.4 8.6 %all-to-all-start.2 = ((bf16[16,4,1152]{2,1,0:T(4,128)(2,1)}), bf16[16,4,1152]{2,1,0:T(4,128)(2,1)S(1)}, u32[]{:S(2)}, u32[]{:S(2)}) async-start(bf16[16,4,1152]{2,1,0:T(4,128)(2,1)} %broadcast_in_dim.31), calls=%async_computation.2 | async-start | bytes 294912 | tf_op jit(solution)/shard_map/all_to_all | solution.py:24
  92.0 0.0 collective-permute-done.2
  92.1 0.1 broadcast_select_fusion.1
  92.1 12.9 %all-to-all-done.2 = bf16[16,4,1152]{2,1,0:T(4,128)(2,1)S(1)} async-done(((bf16[16,4,1152]{2,1,0:T(4,128)(2,1)}), bf16[16,4,1152]{2,1,0:T(4,128)(2,1)S(1)}, u32[]{:S(2)}, u32[]{:S(2)}) %all-to-all-start.2) | async-done | bytes 147488 | tf_op jit(solution)/shard_map/all_to_all | solution.py:24
  105.1 0.9 broadcast_in_dim.32
  106.0 3.6 %all-to-all-start.3 = ((bf16[4,64,1152]{2,1,0:T(8,128)(2,1)}), bf16[4,64,1152]{2,1,0:T(8,128)(2,1)S(1)}, u32[]{:S(2)}, u32[]{:S(2)}) async-start(bf16[4,64,1152]{2,1,0:T(8,128)(2,1)} %broadcast_in_dim.32), calls=%async_computation.3 | async-start | bytes 1179648 | tf_op jit(solution)/shard_map/all_to_all | solution.py:24
  109.5 0.1 pad_maximum_fusion
  109.6 0.0 copy-start.1
  109.6 0.0 copy-start.2
  109.7 7.1 %all-to-all-done.3.refs_0_ = bf16[4,64,1152]{2,1,0:T(8,128)(2,1)S(1)} async-done(((bf16[4,64,1152]{2,1,0:T(8,128)(2,1)}), bf16[4,64,1152]{2,1,0:T(8,128)(2,1)S(1)}, u32[]{:S(2)}, u32[]{:S(2)}) %all-to-all-start.3) | async-done | bytes 589856 | tf_op jit(solution)/shard_map/all_to_all | solution.py:24
  116.7 0.0 copy-start
  116.7 0.0 all-gather.2.cloned.1.call-done
  116.7 3.8 %fusion = f32[4,32,512]{2,1,0:T(8,128)} fusion(bf16[4,32,4096]{2,1,0:T(8,128)(2,1)S(1)} %pad_maximum_fusion, bf16[4096,512]{1,0:T(8,128)(2,1)} %all-gather.2.cloned.1.call-done), kind=kOutput, calls=%fused_computation | convolution fusion | flops 536870912 | bytes 5505024 | tf_op jit(solution)/shard_map/dot_general | solution.py:32
  120.5 3.5 %all-to-all-start.4 = ((f32[4,32,512]{2,1,0:T(8,128)}), f32[4,32,512]{2,1,0:T(8,128)S(1)}, u32[]{:S(2)}, u32[]{:S(2)}) async-start(f32[4,32,512]{2,1,0:T(8,128)} %fusion), calls=%async_computation.4 | async-start | bytes 524288 | tf_op jit(solution)/shard_map/all_to_all | solution.py:24
  124.0 0.0 copy-done.1
  124.1 0.0 copy-done.2
  124.1 1.1 copy_bitcast_fusion
  125.2 0.0 copy-done
  125.2 4.3 %all-to-all-done.4 = f32[4,32,512]{2,1,0:T(8,128)S(1)} async-done(((f32[4,32,512]{2,1,0:T(8,128)}), f32[4,32,512]{2,1,0:T(8,128)S(1)}, u32[]{:S(2)}, u32[]{:S(2)}) %all-to-all-start.4) | async-done | bytes 262176 | tf_op jit(solution)/shard_map/all_to_all | solution.py:24
  129.5 0.6 reduce_sum.29.refs_3_
  130.1 7.3 %attend.1 = bf16[4,64,1152]{2,1,0:T(8,128)(2,1)} custom-call(bf16[4,64,1152]{2,1,0:T(8,128)(2,1)} %copy-done, bf16[2,1024,128]{2,1,0:T(8,128)(2,1)} %get-tuple-element.13.refs_1_, bf16[2,1024,128]{2,1,0:T(8,128)(2,1)} %get-tuple-element.12.refs_2_, bf16[32,512]{1,0:T(8,128)(2,1)} %reduce_sum.29.refs_3_, f32[64,1152]{1,0:T(8,128)} %broadcast_select_fusion.4.refs_4_), custom_call_target="tpu_custom_call" | custom-call | tf_op jit(solution)/shard_map/attend/pallas_call | solution.py:141
  137.4 11.5 %all_to_all.50.in_ref = bf16[4,64,1152]{2,1,0:T(8,128)(2,1)} all-to-all(bf16[4,64,1152]{2,1,0:T(8,128)(2,1)} %attend.1), channel_id=1, replica_groups=mesh['groups'=2,'x'=4,'z'=16,'width'=2] {'x'}, dimensions={0} | all-to-all | bytes 1179648 | tf_op jit(solution)/shard_map/all_to_all | solution.py:24
  149.0 2.2 fold.1
  151.2 0.9 reshape.71
  152.1 18.3 %all_to_all.51 = bf16[16,4,1152]{2,1,0:T(4,128)(2,1)S(1)} all-to-all(bf16[16,4,1152]{2,1,0:T(4,128)(2,1)S(1)} %reshape.71), channel_id=1, replica_groups=mesh['groups'=2,'x'=4,'z'=16,'width'=2] {'z'}, dimensions={0} | all-to-all | bytes 294912 | tf_op jit(solution)/shard_map/all_to_all | solution.py:24
  170.5 0.7 reshape.72.refs_0_
  171.2 1.8 finish.1
  172.9 0.7 slice.20
  173.7 16.1 %all_to_all.52 = bf16[16,4,1024]{2,1,0:T(4,128)(2,1)S(1)} all-to-all(bf16[16,4,1024]{2,1,0:T(4,128)(2,1)S(1)} %broadcast_in_dim.37), channel_id=1, replica_groups=mesh['groups'=2,'x'=4,'z'=16,'width'=2] {'z'}, dimensions={0} | all-to-all | bytes 262144 | tf_op jit(solution)/shard_map/all_to_all | solution.py:24
  189.8 0.1 broadcast_in_dim.38
  189.9 10.1 %all_to_all.53.att_ref = bf16[4,64,1024]{2,1,0:T(8,128)(2,1)} all-to-all(bf16[4,64,1024]{2,1,0:T(8,128)(2,1)S(1)} %broadcast_in_dim.38), channel_id=1, replica_groups=mesh['groups'=2,'x'=4,'z'=16,'width'=2] {'x'}, dimensions={0} | all-to-all | bytes 1048576 | tf_op jit(solution)/shard_map/all_to_all | solution.py:24
  199.9 2.9 %close.1 = f32[2,64,128]{2,1,0:T(8,128)} custom-call(bf16[4,64,1024]{2,1,0:T(8,128)(2,1)} %all_to_all.53.att_ref, bf16[4096,256]{1,0:T(8,128)(2,1)} %weight_ref.1), custom_call_target="tpu_custom_call" | custom-call | tf_op jit(solution)/shard_map/close/pallas_call | solution.py:246
  202.8 14.2 %all_to_all.54 = f32[2,64,128]{2,1,0:T(8,128)S(1)} all-to-all(f32[2,64,128]{2,1,0:T(8,128)} %close.1), channel_id=1, replica_groups=mesh['groups'=2,'x'=4,'z'=16,'width'=2] {'width'}, dimensions={0} | all-to-all | bytes 131072 | tf_op jit(solution)/shard_map/all_to_all | solution.py:24
  217.1 0.6 fusion.2
  (10 shorter events, 0.2 us)
Async XLA Ops:
  7.2 16.6 %copy-start.3 = (s32[32]{0:T(128)S(1)}, s32[32]{0:T(128)}, u32[]{:S(2)}) copy-start(s32[32]{0:T(128)} %param.16) | copy-start | bytes 388
  7.2 109.5 %all-gather.2.cloned.1.call-start = ((), (), s32[]{:S(2)}) async-start(), calls=%async_computation.10 | async-start | bytes 4456448 | tf_op jit(solution)/shard_map/all_gather | solution.py:257
  9.1 15.0 %collective-permute-start = (bf16[32,4096]{1,0:T(8,128)(2,1)S(1)}, bf16[32,4096]{1,0:T(8,128)(2,1)S(1)}, u32[]{:S(2)}, u32[]{:S(2)}) collective-permute-start(bf16[32,4096]{1,0:T(8,128)(2,1)S(1)} %get-tuple-element.10), channel_id=1, source_target_pairs={{0,32},{1,96},{32,0},{33,64},{64,33},{65,97},{96,1},{97,65},{2,34}... | collective-permute-start | bytes 786440 | tf_op jit(solution)/shard_map/ppermute | solution.py:271
  13.4 10.7 %collective-permute-start.1 = (bf16[32,4096]{1,0:T(8,128)(2,1)S(1)}, bf16[32,4096]{1,0:T(8,128)(2,1)S(1)}, u32[]{:S(2)}, u32[]{:S(2)}) collective-permute-start(bf16[32,4096]{1,0:T(8,128)(2,1)S(1)} %get-tuple-element.11), channel_id=1, source_target_pairs={{0,0},{1,64},{32,32},{33,96},{64,1},{65,65},{96,33},{97,97},{2,2},... | collective-permute-start | bytes 786440 | tf_op jit(solution)/shard_map/ppermute | solution.py:270
  19.5 14.0 %all-to-all-start = ((f32[4,64,1152]{2,1,0:T(8,128)}), f32[4,64,1152]{2,1,0:T(8,128)S(1)}, u32[]{:S(2)}, u32[]{:S(2)}) async-start(f32[4,64,1152]{2,1,0:T(8,128)} %project.1), calls=%async_computation | async-start | bytes 2359296 | tf_op jit(solution)/shard_map/all_to_all | solution.py:24
  34.4 48.3 %all-to-all-start.1 = ((f32[16,4,1152]{2,1,0:T(4,128)}), f32[16,4,1152]{2,1,0:T(4,128)S(1)}, u32[]{:S(2)}, u32[]{:S(2)}) async-start(f32[16,4,1152]{2,1,0:T(4,128)} %reshape.69), calls=%async_computation.1 | async-start | bytes 589824 | tf_op jit(solution)/shard_map/all_to_all | solution.py:24
  63.1 29.0 %collective-permute-start.2 = (bf16[2,32,4096]{2,1,0:T(8,128)(2,1)S(1)}, bf16[2,32,4096]{2,1,0:T(8,128)(2,1)S(1)}, u32[]{:S(2)}, u32[]{:S(2)}) collective-permute-start(bf16[2,32,4096]{2,1,0:T(8,128)(2,1)S(1)} %pad_maximum_fusion.1), channel_id=1, source_target_pairs={{0,1},{1,0},{2,3},{3,2},{4,5},{5,4},{6,7},{7,6},{8,9},{9,8},{10,11... | collective-permute-start | bytes 1572872 | tf_op jit(solution)/shard_map/ppermute | solution.py:273
  83.4 21.6 %all-to-all-start.2 = ((bf16[16,4,1152]{2,1,0:T(4,128)(2,1)}), bf16[16,4,1152]{2,1,0:T(4,128)(2,1)S(1)}, u32[]{:S(2)}, u32[]{:S(2)}) async-start(bf16[16,4,1152]{2,1,0:T(4,128)(2,1)} %broadcast_in_dim.31), calls=%async_computation.2 | async-start | bytes 294912 | tf_op jit(solution)/shard_map/all_to_all | solution.py:24
  106.0 10.8 %all-to-all-start.3 = ((bf16[4,64,1152]{2,1,0:T(8,128)(2,1)}), bf16[4,64,1152]{2,1,0:T(8,128)(2,1)S(1)}, u32[]{:S(2)}, u32[]{:S(2)}) async-start(bf16[4,64,1152]{2,1,0:T(8,128)(2,1)} %broadcast_in_dim.32), calls=%async_computation.3 | async-start | bytes 1179648 | tf_op jit(solution)/shard_map/all_to_all | solution.py:24
  109.6 14.4 %copy-start.1 = (bf16[1024,2,128]{2,1,0:T(2,128)(2,1)S(1)}, bf16[1024,2,128]{2,1,0:T(2,128)(2,1)}, u32[]{:S(2)}) copy-start(bf16[1024,2,128]{2,1,0:T(2,128)(2,1)} %param.14) | copy-start | bytes 1572868
  109.6 14.4 %copy-start.2 = (bf16[1024,2,128]{2,1,0:T(2,128)(2,1)S(1)}, bf16[1024,2,128]{2,1,0:T(2,128)(2,1)}, u32[]{:S(2)}) copy-start(bf16[1024,2,128]{2,1,0:T(2,128)(2,1)} %param.13) | copy-start | bytes 1572868
  116.7 8.5 %copy-start = (bf16[4,64,1152]{2,1,0:T(8,128)(2,1)}, bf16[4,64,1152]{2,1,0:T(8,128)(2,1)S(1)}, u32[]{:S(2)}) copy-start(bf16[4,64,1152]{2,1,0:T(8,128)(2,1)S(1)} %all-to-all-done.3.refs_0_) | copy-start | bytes 1769476
  120.5 8.9 %all-to-all-start.4 = ((f32[4,32,512]{2,1,0:T(8,128)}), f32[4,32,512]{2,1,0:T(8,128)S(1)}, u32[]{:S(2)}, u32[]{:S(2)}) async-start(f32[4,32,512]{2,1,0:T(8,128)} %fusion), calls=%async_computation.4 | async-start | bytes 524288 | tf_op jit(solution)/shard_map/all_to_all | solution.py:24
Sparse Core Ops, SparseCore 0:
  9.8 99.5 all-gather.1

commit v2 on v1

v2 whole, which is shorter than its diff:
```python
import math

import jax
import jax.numpy as jnp
from jax import lax
from jax.experimental import pallas as pl
from jax.experimental.pallas import tpu as pltpu
from jax.sharding import Mesh
from jax.sharding import PartitionSpec as P


HD = 128
SEQ = ("x", "z")
GROUPS_SEQ = ("groups", "x", "z")
SEQ_WIDTH = ("x", "z", "width")
MASKED_SCORE = -1e30
LOG2E = 1.4426950408889634
F32 = jnp.float32
BF16 = jnp.bfloat16
TILE = 8


def exchanged(pieces, axis):
    return lax.all_to_all(pieces, axis, split_axis=0, concat_axis=0, tiled=True)


def dot_f32(a, b):
    return jnp.dot(a, b, preferred_element_type=F32)


def on_chip(body, outs, *operands, scratch=(), free=()):
    shapes = jax.tree.map(lambda o: pltpu.VMEM(o.shape, o.dtype), outs)
    placed = [
        x if i in free else pltpu.with_memory_space_constraint(x, pltpu.VMEM)
        for i, x in enumerate(operands)
    ]
    params = pltpu.CompilerParams(vmem_limit_bytes=16 * 2**20)
    return pl.pallas_call(
        body, out_shape=shapes, scratch_shapes=scratch, compiler_params=params
    )(*placed)


def array(shape, dtype):
    return jax.ShapeDtypeStruct(shape, dtype)


def parts_of(rows, places):
    return places // (rows // TILE)


def project(states, query_weight, kv_weight, pieces):
    rows, _ = states.shape
    columns = query_weight.shape[1] // pieces
    extra = kv_weight.shape[1] // pieces

    def body(states_hbm, query_hbm, fresh_hbm, out_ref, states_ref, query_ref, fresh_ref, sems):
        copies = [
            pltpu.make_async_copy(states_hbm, states_ref, sems.at[0]),
            pltpu.make_async_copy(fresh_hbm, fresh_ref, sems.at[1]),
        ]
        for c in range(pieces):
            cut = slice(c * columns, (c + 1) * columns)
            copies.append(
                pltpu.make_async_copy(query_hbm.at[:, cut], query_ref.at[:, cut], sems.at[2 + c])
            )
        for copy in copies:
            copy.start()
        copies[0].wait()
        copies[1].wait()
        states = states_ref[...]
        for c in range(pieces):
            copies[2 + c].wait()
            out_ref[c, :, :columns] = dot_f32(states, query_ref[:, c * columns : (c + 1) * columns])
            out_ref[c, :, columns:] = dot_f32(states, fresh_ref[:, c * extra : (c + 1) * extra])

    anywhere = pl.BlockSpec(memory_space=pltpu.HBM)
    return pl.pallas_call(
        body,
        in_specs=[anywhere, anywhere, anywhere],
        out_shape=pltpu.VMEM((pieces, rows, columns + extra), F32),
        scratch_shapes=[
            pltpu.VMEM(states.shape, BF16),
            pltpu.VMEM(query_weight.shape, BF16),
            pltpu.VMEM(kv_weight.shape, BF16),
            pltpu.SemaphoreType.DMA((2 + pieces,)),
        ],
        compiler_params=pltpu.CompilerParams(vmem_limit_bytes=16 * 2**20),
        name="project",
    )(*[pltpu.with_memory_space_constraint(x, pltpu.HBM) for x in (states, query_weight, kv_weight)])


def add_over_x(received, places):
    sources, rows, width = received.shape
    parts = parts_of(rows, places)
    columns = (width - HD) // parts

    def body(in_ref, out_ref):
        total = in_ref[0]
        for s in range(1, sources):
            total = total + in_ref[s]
        for part in range(parts):
            for group in range(rows // TILE):
                place = part * (rows // TILE) + group
                some = total[group * TILE : (group + 1) * TILE]
                out_ref[place, :, :columns] = some[:, part * columns : (part + 1) * columns]
                out_ref[place, :, columns:] = some[:, width - HD :]

    return on_chip(body, array((places, TILE, columns + HD), F32), received)


def add_over_z(received):
    def body(in_ref, out_ref):
        total = in_ref[0]
        for s in range(1, in_ref.shape[0]):
            total = total + in_ref[s]
        total = total.astype(BF16)
        for s in range(in_ref.shape[0]):
            out_ref[s] = total

    return on_chip(body, array(received.shape, BF16), received)


def fan(received, rows, copies, tail):
    places, _, width = received.shape
    parts = parts_of(rows, places)
    columns = width - tail
    whole = parts * columns + tail

    def body(in_ref, out_ref):
        for part in range(parts):
            for pair in range(rows // TILE // 2):
                place = part * (rows // TILE) + 2 * pair
                some = jnp.concatenate(
                    [in_ref[place].astype(F32), in_ref[place + 1].astype(F32)], axis=0
                ).astype(BF16)
                at = slice(2 * pair * TILE, 2 * (pair + 1) * TILE)
                for c in range(copies):
                    out_ref[c, at, part * columns : (part + 1) * columns] = some[:, :columns]
                    if tail and part == 0:
                        out_ref[c, at, parts * columns :] = some[:, columns:]

    return on_chip(body, array((copies, rows, whole), BF16), received)


def three_parts(x):
    high = x.astype(BF16).astype(F32)
    rest = x - high
    middle = rest.astype(BF16).astype(F32)
    return (high, middle, rest - middle)


def joined_stats(tail, heads):
    lanes = tail.shape[-1]
    whole = tail + pltpu.roll(tail, lanes - heads, 1) + pltpu.roll(tail, lanes - 2 * heads, 1)
    return whole, pltpu.roll(whole, lanes - 3 * heads, 1)


def split_stats(highest, total, heads):
    lane = lax.broadcasted_iota(jnp.int32, highest.shape, 1)
    parts = (*three_parts(highest), *three_parts(total))
    stats = jnp.where(lane < heads, parts[0], 0.0)
    for place in range(1, 6):
        here = (lane >= place * heads) & (lane < (place + 1) * heads)
        stats = jnp.where(here, pltpu.roll(parts[place], place * heads, 1), stats)
    return stats


def heads_together(ref, piece, first, count):
    return jnp.concatenate(
        [ref[piece, :, (first + i) * HD : (first + i + 1) * HD] for i in range(count)], axis=0
    )


def score(q, keys):
    return lax.dot_general(q, keys, (((1,), (1,)), ((), ())), preferred_element_type=F32)


def attend(projected, keys, values, bias, scale):
    pieces, rows, width = projected.shape
    local_heads, slots, _ = keys.shape
    per_head = pieces // local_heads
    total_keys = bias.shape[1]
    heads = (width - HD) // HD
    per_dot = 256 // rows
    at = heads * HD
    blank_rows = total_keys - slots - rows

    def body(q_ref, keys_ref, values_ref, bias_ref, out_ref, stats_ref, k_ref, v_ref):
        bias = bias_ref[...]
        lane = lax.broadcasted_iota(jnp.int32, (rows, HD), 1)
        blank = [jnp.zeros((blank_rows, HD), BF16)] if blank_rows else []
        for h in range(local_heads):
            k_ref[h, :slots, :] = keys_ref[h]
            v_ref[h, :slots, :] = values_ref[h]
            for place, into in ((h * per_head, k_ref), (h * per_head + 1, v_ref)):
                into[h, slots:, :] = jnp.concatenate(
                    [q_ref[place, :, at:]] + blank, axis=0
                )
        for h in range(local_heads):
            for piece in range(h * per_head, (h + 1) * per_head):
                peaks = jnp.zeros((rows, HD), F32)
                totals = jnp.zeros((rows, HD), F32)
                for first in range(0, heads, per_dot):
                    q = heads_together(q_ref, piece, first, per_dot)
                    scores = score(q, k_ref[h])
                    scores = scores.reshape(per_dot, rows, total_keys) * scale + bias[None]
                    highest = jnp.max(scores, axis=-1, keepdims=True)
                    weights = jnp.exp2(scores - highest)
                    total = jnp.sum(weights, axis=-1, keepdims=True)
                    weights = weights.reshape(per_dot * rows, total_keys).astype(BF16)
                    summed = dot_f32(weights, v_ref[h])
                    for i in range(per_dot):
                        head = first + i
                        out_ref[piece, :, head * HD : (head + 1) * HD] = summed[
                            i * rows : (i + 1) * rows
                        ]
                        peaks = jnp.where(lane == head, highest[i], peaks)
                        totals = jnp.where(lane == head, total[i], totals)
                stats_ref[piece, 0] = peaks
                stats_ref[piece, 1] = totals

    outs = [array((pieces, rows, at), F32), array((pieces, 2, rows, HD), F32)]
    scratch = [pltpu.VMEM((local_heads, total_keys, HD), BF16)] * 2
    return on_chip(body, outs, projected, keys, values, bias, scratch=scratch)


def with_span(projected, summed, stats, span_kv, scale):
    pieces, rows, width = projected.shape
    heads = (width - HD) // HD
    per_dot = 256 // rows
    at = heads * HD
    local_heads = span_kv.shape[1] // (2 * HD)
    per_head = pieces // local_heads

    def body(q_ref, summed_ref, stats_ref, span_ref, out_ref):
        lane = lax.broadcasted_iota(jnp.int32, (rows, HD), 1)
        for piece in range(pieces):
            begin = (piece // per_head) * 2 * HD
            keys = span_ref[:, begin : begin + HD]
            values = span_ref[:, begin + HD : begin + 2 * HD]
            peaks = stats_ref[piece, 0]
            totals = stats_ref[piece, 1]
            new_peaks = jnp.zeros((rows, HD), F32)
            added = jnp.zeros((rows, HD), F32)
            for first in range(0, heads, per_dot):
                q = heads_together(q_ref, piece, first, per_dot)
                scores = score(q, keys).reshape(per_dot, rows, keys.shape[0]) * scale
                highest = jnp.max(scores, axis=-1, keepdims=True)
                old = [peaks[:, first + i : first + i + 1] for i in range(per_dot)]
                highest = jnp.maximum(highest, jnp.stack(old))
                weights = jnp.exp2(scores - highest)
                total = jnp.sum(weights, axis=-1, keepdims=True)
                weights = weights.reshape(per_dot * rows, keys.shape[0]).astype(BF16)
                extra = dot_f32(weights, values)
                for i in range(per_dot):
                    head = first + i
                    cut = slice(head * HD, (head + 1) * HD)
                    keep = jnp.exp2(old[i] - highest[i])
                    out_ref[piece, :, cut] = (
                        summed_ref[piece, :, cut] * keep + extra[i * rows : (i + 1) * rows]
                    ).astype(BF16)
                    new_peaks = jnp.where(lane == head, highest[i], new_peaks)
                    added = jnp.where(lane == head, total[i], added)
            kept = jnp.exp2(jnp.where(lane < heads, peaks - new_peaks, 0.0))
            stats = split_stats(new_peaks, totals * kept + added, heads)
            out_ref[piece, :, at:] = stats.astype(BF16)

    out = array((pieces, rows, width), BF16)
    return on_chip(body, out, projected, summed, stats, span_kv, free=(1,))


def fold(received, places):
    sources, rows, width = received.shape
    heads = (width - HD) // HD
    at = heads * HD
    parts = parts_of(rows, places)
    some_heads = heads // parts
    groups = rows // TILE
    columns = some_heads * HD

    def body(in_ref, out_ref):
        lane = lax.broadcasted_iota(jnp.int32, (rows, HD), 1)
        stats = [joined_stats(in_ref[s, :, at:].astype(F32), heads) for s in range(sources)]
        highest = stats[0][0]
        for s in range(1, sources):
            highest = jnp.maximum(highest, stats[s][0])
        keeps = [jnp.exp2(jnp.where(lane < heads, m - highest, 0.0)) for m, _ in stats]
        total = keeps[0] * stats[0][1]
        for s in range(1, sources):
            total = total + keeps[s] * stats[s][1]

        def put(part, cut, block):
            for group in range(groups):
                out_ref[part * groups + group, :, cut] = block[
                    group * TILE : (group + 1) * TILE
                ].astype(BF16)

        for part in range(parts):
            for i in range(some_heads):
                head = part * some_heads + i
                cut = slice(head * HD, (head + 1) * HD)
                summed = in_ref[0, :, cut].astype(F32) * keeps[0][:, head : head + 1]
                for s in range(1, sources):
                    keep = keeps[s][:, head : head + 1]
                    summed = summed + in_ref[s, :, cut].astype(F32) * keep
                put(part, slice(i * HD, (i + 1) * HD), summed)
            turn = (HD - part * some_heads) % HD
            peaks = pltpu.roll(highest, turn, 1) if turn else highest
            totals = pltpu.roll(total, turn, 1) if turn else total
            put(part, slice(columns, columns + HD), split_stats(peaks, totals, some_heads))

    return on_chip(body, array((places, TILE, columns + HD), BF16), received)


def finish(received):
    sources, group, width = received.shape
    heads = (width - HD) // HD
    at = heads * HD

    def body(in_ref, out_ref):
        lane = lax.broadcasted_iota(jnp.int32, (group, HD), 1)
        stats = [joined_stats(in_ref[s, :, at:].astype(F32), heads) for s in range(sources)]
        highest = stats[0][0]
        for s in range(1, sources):
            highest = jnp.maximum(highest, stats[s][0])
        keeps = [jnp.exp2(jnp.where(lane < heads, m - highest, 0.0)) for m, _ in stats]
        total = keeps[0] * stats[0][1]
        for s in range(1, sources):
            total = total + keeps[s] * stats[s][1]
        for head in range(heads):
            cut = slice(head * HD, (head + 1) * HD)
            summed = in_ref[0, :, cut].astype(F32) * keeps[0][:, head : head + 1]
            for s in range(1, sources):
                summed = summed + in_ref[s, :, cut].astype(F32) * keeps[s][:, head : head + 1]
            ready = (summed / total[:, head : head + 1]).astype(BF16)
            for s in range(sources):
                out_ref[s, :, cut] = ready

    return on_chip(body, array((sources, group, at), BF16), received)


def close(attention, out_weight, halves):
    pieces, rows, depth = attention.shape
    columns = out_weight.shape[1] // halves

    def body(in_ref, weight_ref, out_ref):
        total = dot_f32(in_ref[0], weight_ref[:depth, :])
        for c in range(1, pieces):
            total = total + dot_f32(in_ref[c], weight_ref[c * depth : (c + 1) * depth, :])
        for w in range(halves):
            out_ref[w] = total[:, w * columns : (w + 1) * columns]

    return on_chip(body, array((halves, rows, columns), F32), attention, out_weight)


def tokens_by_x(span_tokens, depth):
    xs = lax.axis_size("x")
    x = lax.axis_index("x")
    order = [(a, w) for a in range(xs) for w in range(2)]

    def flat(a, w):
        return a * 2 + w

    first = [(flat(a, w), flat(2 * w + (a & 1), a >> 1)) for a, w in order]
    second = [(flat(a, w), flat(2 * w + 1 - (a & 1), a >> 1)) for a, w in order]
    low = span_tokens[:, :depth]
    high = span_tokens[:, depth:]
    odd = (x & 1) == 1
    one = lax.ppermute(jnp.where(odd, high, low), ("x", "width"), first)
    two = lax.ppermute(jnp.where(odd, low, high), ("x", "width"), second)
    mine = jnp.stack([jnp.where(odd, two, one), jnp.where(odd, one, two)])
    theirs = lax.ppermute(mine, "width", [(0, 1), (1, 0)])
    upper = lax.axis_index("width") == 1
    return jnp.concatenate(
        [jnp.where(upper, theirs, mine), jnp.where(upper, mine, theirs)], axis=0
    )


def biases(lengths, offset, step_count, slots):
    branch_count = lengths.shape[0]
    rows = step_count * branch_count
    seat = lax.axis_index(SEQ)
    visible = jnp.tile(jnp.minimum(lengths, offset[0]), step_count)[:, None]
    places = seat * slots + jnp.arange(slots, dtype=jnp.int32)[None]
    row = jnp.arange(rows, dtype=jnp.int32)
    same = (row[:, None] % branch_count == row[None] % branch_count) & (row[None] <= row[:, None])
    filler = jnp.zeros((rows, -(slots + rows) % HD), jnp.bool_)
    allowed = jnp.concatenate([places < visible, same & (seat == 0), filler], axis=1)
    return jnp.where(allowed, 0.0, MASKED_SCORE).astype(F32)


def local(
    span_tokens,
    kv_weight,
    query_weight,
    out_weight,
    cache_keys,
    cache_values,
    hidden,
    lengths,
    offset,
):
    xs = lax.axis_size("x")
    zs = lax.axis_size("z")
    step_count, branch_count, depth = hidden.shape
    rows = step_count * branch_count
    scale = LOG2E / math.sqrt(HD)
    span_weight = lax.all_gather(kv_weight, "z", axis=0, tiled=True)
    tokens = span_tokens.shape[0]

    partial = project(hidden.reshape(rows, depth), query_weight, kv_weight, xs)
    partial = exchanged(partial, "x")
    partial, span_tokens = lax.optimization_barrier((partial, span_tokens))
    ready = tokens_by_x(span_tokens, span_weight.shape[0])
    partial = add_over_x(partial, zs)
    partial = exchanged(partial, "z")
    own = add_over_z(partial)
    own = exchanged(own, "z")
    columns = fan(own, rows, xs, HD)
    columns, ready = lax.optimization_barrier((columns, ready))
    projected = exchanged(columns, "x")

    span_partial = dot_f32(ready.reshape(xs * tokens, span_weight.shape[0]), span_weight)
    span_partial = span_partial.reshape(xs, tokens, kv_weight.shape[1])
    span_kv = jnp.sum(exchanged(span_partial, "x"), axis=0).astype(BF16)

    bias = biases(lengths, offset, step_count, cache_keys.shape[0])
    keys = cache_keys.transpose(1, 0, 2)
    values = cache_values.transpose(1, 0, 2)
    summed, stats = attend(projected, keys, values, bias, scale)
    partial = with_span(projected, summed, stats, span_kv, scale)
    folded = fold(exchanged(partial, "x"), zs)
    ours = finish(exchanged(folded, "z"))
    attention = exchanged(fan(exchanged(ours, "z"), rows, xs, 0), "x")
    halves = exchanged(close(attention, out_weight, 2), "width")
    attended = (halves[0] + halves[1]).astype(BF16)
    return (span_kv, attended.reshape(step_count, branch_count, attended.shape[1]))


def solution(mesh):
    finer = Mesh(
        mesh.devices.reshape(mesh.shape["groups"], 4, 16, mesh.shape["width"]),
        ("groups", "x", "z", "width"),
    )
    placed = (
        P(GROUPS_SEQ, "width"),
        P(SEQ, "width"),
        P(SEQ, "width"),
        P("width", SEQ),
        P(GROUPS_SEQ, "width", None),
        P(GROUPS_SEQ, "width", None),
        P(None, "groups", SEQ),
        P("groups"),
        P("groups"),
    )

    return jax.shard_map(
        local,
        mesh=finer,
        in_specs=placed,
        out_specs=(P(GROUPS_SEQ, "width"), P(None, "groups", SEQ_WIDTH)),
        check_vma=False,
    )
```

time: 226 us -> 213 us (0.942)
  starting transfers between devices: 56.9 us -> 52.6 us
  local copies, waits for them, and re-layouts: 6.25 us -> 2.6 us
  Pallas kernels: 18.2 us -> 15.4 us
  other arithmetic: 3.68 us -> 1.16 us
    all_to_all x5, starting transfers between devices: 47.9 us -> 29.6 us  [exchanged(): return lax.all_to_all(pieces, axis, split_axis=0, concat_axis=0, tiled=True)]
    ppermute x3, starting transfers between devices: 8.9 us -> 22.9 us  [the longest x1 20.9 us: tokens_by_x(): two = lax.ppermute(jnp.where(odd, low, high), ('x', 'width'), second)]
    pallas_call x5 -> x10, Pallas kernels: 18.2 us -> 15.4 us  [the longest x9 12.2 us: on_chip(): pl.pallas_call(body, out_shape=shapes, scratch_shapes=scratch, compiler_p...]
    reshape x5 -> x0, local copies, waits for them, and re-layouts: 2.52 us -> none  [the longest x1 0.95 us: local(): folded = folded.reshape(zs, rows // zs, folded.shape[1])]
  transfers between devices with their start and end apart: 9 -> 9, of which waited for: 5 -> 5; matrix products, arithmetic and copies ran while one was open for 3% -> 2% of each run, Pallas kernels for 2% -> 5%
where the time goes in v2:
time: 213 us; the launch traced here: 212 us
  blocking collectives  71.3 us (33%)
  starting transfers between devices  52.6 us (25%)
  waiting for transfers between devices  50.4 us (24%)
  Pallas kernels  15.4 us (7%)
  between operations  15 us (7%)
  matrix products  3.62 us (2%)
  local copies, waits for them, and re-layouts  2.6 us (1%)
    all_to_all x5, blocking collectives, exchanged(): return lax.all_to_all(pieces, axis, split_axis=0, concat_axis=0, tiled=True)  71.3 us
    all_to_all x5, waiting for transfers between devices, exchanged(): return lax.all_to_all(pieces, axis, split_axis=0, concat_axis=0, tiled=True)  48 us
    all_to_all x5, starting transfers between devices, exchanged(): return lax.all_to_all(pieces, axis, split_axis=0, concat_axis=0, tiled=True)  29.6 us
    ppermute x1, starting transfers between devices, tokens_by_x(): two = lax.ppermute(jnp.where(odd, low, high), ('x', 'width'), second)  20.9 us
    pallas_call x9, Pallas kernels, on_chip(): pl.pallas_call(body, out_shape=shapes, scratch_shapes=scratch, compiler_p...  12.2 us
  transfers between devices with their start and end apart: 9, of which 5 were waited for; matrix products, arithmetic and copies ran while one was open for 2% of the time, Pallas kernels for 5%

profile of v2, /device:TPU:33, one launch (start us, length us, event | category | flops | bytes accessed | tf_op | source)
XLA Modules:
  0.0 212.1 jit_solution(13513088863700765917)
XLA Ops:
  7.2 0.0 copy-start.4
  7.2 0.0 copy-start.7
  7.2 0.1 all-gather.2.cloned.1.call-start
  7.3 0.7 all-gather.2.cloned.1.call-update
  8.0 3.2 %project.1 = f32[4,64,1152]{2,1,0:T(8,128)} custom-call(bf16[64,256]{1,0:T(8,128)(2,1)} %bitcast.16, bf16[256,4096]{1,0:T(8,128)(2,1)} %query_hbm.1, bf16[256,512]{1,0:T(8,128)(2,1)} %fresh_hbm.1), custom_call_target="tpu_custom_call" | custom-call | tf_op jit(solution)/shard_map/project/pallas_call | solution.py:77
  11.2 5.1 %all-to-all-start = ((f32[4,64,1152]{2,1,0:T(8,128)}), f32[4,64,1152]{2,1,0:T(8,128)S(1)}, u32[]{:S(2)}, u32[]{:S(2)}) async-start(f32[4,64,1152]{2,1,0:T(8,128)} %project.1), calls=%async_computation | async-start | bytes 2359296 | tf_op jit(solution)/shard_map/all_to_all | solution.py:24
  17.0 9.8 %all-to-all-done.in_ref = f32[4,64,1152]{2,1,0:T(8,128)S(1)} async-done(((f32[4,64,1152]{2,1,0:T(8,128)}), f32[4,64,1152]{2,1,0:T(8,128)S(1)}, u32[]{:S(2)}, u32[]{:S(2)}) %all-to-all-start) | async-done | bytes 1179680 | tf_op jit(solution)/shard_map/all_to_all | solution.py:24
  26.8 0.0 copy-done.4
  26.8 20.9 %collective-permute-start = (bf16[32,4096]{1,0:T(8,128)(2,1)S(1)}, bf16[32,4096]{1,0:T(8,128)(2,1)S(1)}, u32[]{:S(2)}, u32[]{:S(2)}) collective-permute-start(bf16[32,4096]{1,0:T(8,128)(2,1)S(1)} %get-tuple-element.18), channel_id=1, source_target_pairs={{0,32},{1,96},{32,0},{33,64},{64,33},{65,97},{96,1},{97,65},{2,34}... | collective-permute-start | bytes 786440 | tf_op jit(solution)/shard_map/ppermute | solution.py:370
  47.7 1.9 collective-permute-start.1
  49.6 0.0 copy-done.7
  49.7 0.1 lt.26
  49.8 0.8 shard_map.104
  50.5 10.7 %all-to-all-start.1 = ((f32[16,8,640]{2,1,0:T(8,128)}), f32[16,8,640]{2,1,0:T(8,128)S(1)}, u32[]{:S(2)}, u32[]{:S(2)}) async-start(f32[16,8,640]{2,1,0:T(8,128)} %shard_map.104), calls=%async_computation.1 | async-start | bytes 655360 | tf_op jit(solution)/shard_map/all_to_all | solution.py:24
  61.3 0.0 collective-permute-done
  61.3 0.0 collective-permute-done.1
  61.4 0.1 pad_maximum_fusion.1
  61.4 0.1 collective-permute-start.2
  61.6 0.1 fusion.4
  61.7 0.1 broadcast_compare_fusion
  61.8 0.1 concatenate.7
  61.9 23.3 %all-to-all-done.1.in_ref = f32[16,8,640]{2,1,0:T(8,128)S(1)} async-done(((f32[16,8,640]{2,1,0:T(8,128)}), f32[16,8,640]{2,1,0:T(8,128)S(1)}, u32[]{:S(2)}, u32[]{:S(2)}) %all-to-all-start.1) | async-done | bytes 327712 | tf_op jit(solution)/shard_map/all_to_all | solution.py:24
  85.2 0.7 shard_map.105
  85.9 6.3 %all-to-all-start.2 = ((bf16[16,8,640]{2,1,0:T(8,128)(2,1)}), bf16[16,8,640]{2,1,0:T(8,128)(2,1)S(1)}, u32[]{:S(2)}, u32[]{:S(2)}) async-start(bf16[16,8,640]{2,1,0:T(8,128)(2,1)} %shard_map.105), calls=%async_computation.2 | async-start | bytes 327680 | tf_op jit(solution)/shard_map/all_to_all | solution.py:24
  92.2 0.0 collective-permute-done.2
  92.3 0.1 broadcast_select_fusion.1
  92.3 0.1 pad_maximum_fusion
  92.4 13.0 %all-to-all-done.2.in_ref = bf16[16,8,640]{2,1,0:T(8,128)(2,1)S(1)} async-done(((bf16[16,8,640]{2,1,0:T(8,128)(2,1)}), bf16[16,8,640]{2,1,0:T(8,128)(2,1)S(1)}, u32[]{:S(2)}, u32[]{:S(2)}) %all-to-all-start.2) | async-done | bytes 163872 | tf_op jit(solution)/shard_map/all_to_all | solution.py:24
  105.5 0.9 shard_map.106
  106.4 0.0 copy-start.5
  106.4 0.0 copy-start.6
  106.4 3.7 %all-to-all-start.4 = ((bf16[4,64,1152]{2,1,0:T(8,128)(2,1)}), bf16[4,64,1152]{2,1,0:T(8,128)(2,1)S(1)}, u32[]{:S(2)}, u32[]{:S(2)}) async-start(bf16[4,64,1152]{2,1,0:T(8,128)(2,1)} %shard_map.106), calls=%async_computation.4 | async-start | bytes 1179648 | tf_op jit(solution)/shard_map/all_to_all | solution.py:24
  110.1 1.7 all-gather.2.cloned.1.call-done
  111.8 3.6 %fusion = f32[4,32,512]{2,1,0:T(8,128)} fusion(bf16[4,32,4096]{2,1,0:T(8,128)(2,1)S(1)} %pad_maximum_fusion, bf16[4096,512]{1,0:T(8,128)(2,1)} %all-gather.2.cloned.1.call-done), kind=kOutput, calls=%fused_computation | convolution fusion | flops 536870912 | bytes 5505024 | tf_op jit(solution)/shard_map/dot_general | solution.py:28
  115.4 1.9 all-to-all-done.4.q_ref
  117.3 3.7 %all-to-all-start.3 = ((f32[4,32,512]{2,1,0:T(8,128)}), f32[4,32,512]{2,1,0:T(8,128)S(1)}, u32[]{:S(2)}, u32[]{:S(2)}) async-start(f32[4,32,512]{2,1,0:T(8,128)} %fusion), calls=%async_computation.3 | async-start | bytes 524288 | tf_op jit(solution)/shard_map/all_to_all | solution.py:24
  121.0 0.0 copy-done.5
  121.0 0.0 copy-done.6
  121.0 0.1 copy_bitcast_fusion
  121.2 0.0 copy-start
  121.2 4.6 %shard_map.107 = (f32[4,64,1024]{2,1,0:T(8,128)S(1)}, f32[4,2,64,128]{3,2,1,0:T(8,128)S(1)}) custom-call(bf16[4,64,1152]{2,1,0:T(8,128)(2,1)S(1)} %all-to-all-done.4.q_ref, bf16[2,1024,128]{2,1,0:T(8,128)(2,1)S(1)} %get-tuple-element.21.keys_ref, bf16[2,1024,128]{2,1,0:T(8,128)(2,1)S(1)} %get-tuple-element.20.values_ref, ...), custom_call_target="tpu_custom_call" | custom-call | tf_op jit(solution)/shard_map/pallas_call | solution.py:38
  125.8 0.0 copy-start.1
  125.8 1.0 copy-done.1
  126.8 0.0 all-to-all-done.3
  126.9 0.0 copy-start.3
  126.9 0.0 copy-start.2
  126.9 1.2 copy-done.2
  128.1 3.8 %shard_map.108 = bf16[4,64,1152]{2,1,0:T(8,128)(2,1)S(1)} custom-call(bf16[4,64,1152]{2,1,0:T(8,128)(2,1)S(1)} %all-to-all-done.4.q_ref, f32[4,64,1024]{2,1,0:T(8,128)S(1)} %copy-done.2, f32[4,2,64,128]{3,2,1,0:T(8,128)S(1)} %get-tuple-element.13.stats_ref, bf16[32,512]{1,0:T(8,128)(2,1)S(1)} %reduce_sum.9.span_ref), custom_call_target="tpu_custom_call" | custom-call | tf_op jit(solution)/shard_map/pallas_call | solution.py:38
  131.9 11.0 %all_to_all.50.in_ref = bf16[4,64,1152]{2,1,0:T(8,128)(2,1)S(1)} all-to-all(bf16[4,64,1152]{2,1,0:T(8,128)(2,1)S(1)} %shard_map.108), channel_id=1, replica_groups=mesh['groups'=2,'x'=4,'z'=16,'width'=2] {'x'}, dimensions={0} | all-to-all | bytes 1179648 | tf_op jit(solution)/shard_map/all_to_all | solution.py:24
  143.0 0.6 shard_map.109
  143.5 23.4 %all_to_all.51.in_ref = bf16[16,8,640]{2,1,0:T(8,128)(2,1)S(1)} all-to-all(bf16[16,8,640]{2,1,0:T(8,128)(2,1)S(1)} %shard_map.109), channel_id=1, replica_groups=mesh['groups'=2,'x'=4,'z'=16,'width'=2] {'z'}, dimensions={0} | all-to-all | bytes 327680 | tf_op jit(solution)/shard_map/all_to_all | solution.py:24
  166.9 0.3 shard_map.110
  167.2 16.4 %all_to_all.52.in_ref = bf16[16,8,512]{2,1,0:T(8,128)(2,1)S(1)} all-to-all(bf16[16,8,512]{2,1,0:T(8,128)(2,1)S(1)} %shard_map.110), channel_id=1, replica_groups=mesh['groups'=2,'x'=4,'z'=16,'width'=2] {'z'}, dimensions={0} | all-to-all | bytes 262144 | tf_op jit(solution)/shard_map/all_to_all | solution.py:24
  183.6 9.4 %all_to_all.53.in_ref = bf16[4,64,1024]{2,1,0:T(8,128)(2,1)S(1)} all-to-all(bf16[4,64,1024]{2,1,0:T(8,128)(2,1)S(1)} %shard_map.111), channel_id=1, replica_groups=mesh['groups'=2,'x'=4,'z'=16,'width'=2] {'x'}, dimensions={0} | all-to-all | bytes 1048576 | tf_op jit(solution)/shard_map/all_to_all | solution.py:24
  193.0 0.0 copy-done
  193.0 0.5 shard_map.112
  193.5 0.0 copy-done.3
  193.5 11.1 %all_to_all.54 = f32[2,64,128]{2,1,0:T(8,128)S(1)} all-to-all(f32[2,64,128]{2,1,0:T(8,128)S(1)} %shard_map.112), channel_id=1, replica_groups=mesh['groups'=2,'x'=4,'z'=16,'width'=2] {'width'}, dimensions={0} | all-to-all | bytes 131072 | tf_op jit(solution)/shard_map/all_to_all | solution.py:24
  204.6 0.6 fusion.2
  (10 shorter events, 0.2 us)
Async XLA Ops:
  7.2 19.6 %copy-start.4 = (bf16[32,8192]{1,0:T(8,128)(2,1)S(1)}, bf16[32,8192]{1,0:T(8,128)(2,1)}, u32[]{:S(2)}) copy-start(bf16[32,8192]{1,0:T(8,128)(2,1)} %param.9) | copy-start | bytes 1572868
  7.2 42.4 %copy-start.7 = (s32[32]{0:T(128)S(1)}, s32[32]{0:T(128)}, u32[]{:S(2)}) copy-start(s32[32]{0:T(128)} %param.16) | copy-start | bytes 388
  7.2 104.6 %all-gather.2.cloned.1.call-start = ((), (), s32[]{:S(2)}) async-start(), calls=%async_computation.10 | async-start | bytes 4456448 | tf_op jit(solution)/shard_map/all_gather | solution.py:408
  11.2 15.6 %all-to-all-start = ((f32[4,64,1152]{2,1,0:T(8,128)}), f32[4,64,1152]{2,1,0:T(8,128)S(1)}, u32[]{:S(2)}, u32[]{:S(2)}) async-start(f32[4,64,1152]{2,1,0:T(8,128)} %project.1), calls=%async_computation | async-start | bytes 2359296 | tf_op jit(solution)/shard_map/all_to_all | solution.py:24
  26.8 34.5 %collective-permute-start = (bf16[32,4096]{1,0:T(8,128)(2,1)S(1)}, bf16[32,4096]{1,0:T(8,128)(2,1)S(1)}, u32[]{:S(2)}, u32[]{:S(2)}) collective-permute-start(bf16[32,4096]{1,0:T(8,128)(2,1)S(1)} %get-tuple-element.18), channel_id=1, source_target_pairs={{0,32},{1,96},{32,0},{33,64},{64,33},{65,97},{96,1},{97,65},{2,34}... | collective-permute-start | bytes 786440 | tf_op jit(solution)/shard_map/ppermute | solution.py:370
  47.7 13.6 %collective-permute-start.1 = (bf16[32,4096]{1,0:T(8,128)(2,1)S(1)}, bf16[32,4096]{1,0:T(8,128)(2,1)S(1)}, u32[]{:S(2)}, u32[]{:S(2)}) collective-permute-start(bf16[32,4096]{1,0:T(8,128)(2,1)S(1)} %get-tuple-element.19), channel_id=1, source_target_pairs={{0,0},{1,64},{32,32},{33,96},{64,1},{65,65},{96,33},{97,97},{2,2},... | collective-permute-start | bytes 786440 | tf_op jit(solution)/shard_map/ppermute | solution.py:369
  50.5 34.6 %all-to-all-start.1 = ((f32[16,8,640]{2,1,0:T(8,128)}), f32[16,8,640]{2,1,0:T(8,128)S(1)}, u32[]{:S(2)}, u32[]{:S(2)}) async-start(f32[16,8,640]{2,1,0:T(8,128)} %shard_map.104), calls=%async_computation.1 | async-start | bytes 655360 | tf_op jit(solution)/shard_map/all_to_all | solution.py:24
  61.4 30.8 %collective-permute-start.2 = (bf16[2,32,4096]{2,1,0:T(8,128)(2,1)S(1)}, bf16[2,32,4096]{2,1,0:T(8,128)(2,1)S(1)}, u32[]{:S(2)}, u32[]{:S(2)}) collective-permute-start(bf16[2,32,4096]{2,1,0:T(8,128)(2,1)S(1)} %pad_maximum_fusion.1), channel_id=1, source_target_pairs={{0,1},{1,0},{2,3},{3,2},{4,5},{5,4},{6,7},{7,6},{8,9},{9,8},{10,11... | collective-permute-start | bytes 1572872 | tf_op jit(solution)/shard_map/ppermute | solution.py:372
  85.9 19.6 %all-to-all-start.2 = ((bf16[16,8,640]{2,1,0:T(8,128)(2,1)}), bf16[16,8,640]{2,1,0:T(8,128)(2,1)S(1)}, u32[]{:S(2)}, u32[]{:S(2)}) async-start(bf16[16,8,640]{2,1,0:T(8,128)(2,1)} %shard_map.105), calls=%async_computation.2 | async-start | bytes 327680 | tf_op jit(solution)/shard_map/all_to_all | solution.py:24
  106.4 14.6 %copy-start.5 = (bf16[1024,2,128]{2,1,0:T(2,128)(2,1)S(1)}, bf16[1024,2,128]{2,1,0:T(2,128)(2,1)}, u32[]{:S(2)}) copy-start(bf16[1024,2,128]{2,1,0:T(2,128)(2,1)} %param.14) | copy-start | bytes 1572868
  106.4 14.7 %copy-start.6 = (bf16[1024,2,128]{2,1,0:T(2,128)(2,1)S(1)}, bf16[1024,2,128]{2,1,0:T(2,128)(2,1)}, u32[]{:S(2)}) copy-start(bf16[1024,2,128]{2,1,0:T(2,128)(2,1)} %param.13) | copy-start | bytes 1572868
  106.4 11.0 %all-to-all-start.4 = ((bf16[4,64,1152]{2,1,0:T(8,128)(2,1)}), bf16[4,64,1152]{2,1,0:T(8,128)(2,1)S(1)}, u32[]{:S(2)}, u32[]{:S(2)}) async-start(bf16[4,64,1152]{2,1,0:T(8,128)(2,1)} %shard_map.106), calls=%async_computation.4 | async-start | bytes 1179648 | tf_op jit(solution)/shard_map/all_to_all | solution.py:24
  117.3 9.5 %all-to-all-start.3 = ((f32[4,32,512]{2,1,0:T(8,128)}), f32[4,32,512]{2,1,0:T(8,128)S(1)}, u32[]{:S(2)}, u32[]{:S(2)}) async-start(f32[4,32,512]{2,1,0:T(8,128)} %fusion), calls=%async_computation.3 | async-start | bytes 524288 | tf_op jit(solution)/shard_map/all_to_all | solution.py:24
  121.2 71.8 %copy-start = (bf16[4096,256]{1,0:T(8,128)(2,1)S(1)}, bf16[4096,256]{1,0:T(8,128)(2,1)}, u32[]{:S(2)}) copy-start(bf16[4096,256]{1,0:T(8,128)(2,1)} %weight_ref.1) | copy-start | bytes 6291460
  125.8 1.0 copy-start.1
  126.9 66.6 %copy-start.3 = (bf16[32,512]{1,0:T(8,128)(2,1)}, bf16[32,512]{1,0:T(8,128)(2,1)S(1)}, u32[]{:S(2)}) copy-start(bf16[32,512]{1,0:T(8,128)(2,1)S(1)} %reduce_sum.9.span_ref) | copy-start | bytes 98308
  126.9 1.2 copy-start.2
Sparse Core Ops, SparseCore 0:
  9.8 101.9 all-gather.1

commit v3 on v2

--- a/solution.py
+++ b/solution.py
@@ -10,9 +10,10 @@
 
 
 HD = 128
-SEQ = ("x", "z")
-GROUPS_SEQ = ("groups", "x", "z")
-SEQ_WIDTH = ("x", "z", "width")
+Z = ("zh", "zl")
+SEQ = ("x", *Z)
+GROUPS_SEQ = ("groups", *SEQ)
+SEQ_WIDTH = (*SEQ, "width")
 MASKED_SCORE = -1e30
 LOG2E = 1.4426950408889634
 F32 = jnp.float32
@@ -28,12 +29,9 @@
     return jnp.dot(a, b, preferred_element_type=F32)
 
 
-def on_chip(body, outs, *operands, scratch=(), free=()):
+def on_chip(body, outs, *operands, scratch=()):
     shapes = jax.tree.map(lambda o: pltpu.VMEM(o.shape, o.dtype), outs)
-    placed = [
-        x if i in free else pltpu.with_memory_space_constraint(x, pltpu.VMEM)
-        for i, x in enumerate(operands)
-    ]
+    placed = [pltpu.with_memory_space_constraint(x, pltpu.VMEM) for x in operands]
     params = pltpu.CompilerParams(vmem_limit_bytes=16 * 2**20)
     return pl.pallas_call(
         body, out_shape=shapes, scratch_shapes=scratch, compiler_params=params
@@ -175,27 +173,28 @@
     return lax.dot_general(q, keys, (((1,), (1,)), ((), ())), preferred_element_type=F32)
 
 
-def attend(projected, keys, values, bias, scale):
+def attend(projected, keys, values, span_kv, bias, scale):
     pieces, rows, width = projected.shape
     local_heads, slots, _ = keys.shape
+    span = span_kv.shape[0]
     per_head = pieces // local_heads
     total_keys = bias.shape[1]
     heads = (width - HD) // HD
     per_dot = 256 // rows
     at = heads * HD
-    blank_rows = total_keys - slots - rows
-
-    def body(q_ref, keys_ref, values_ref, bias_ref, out_ref, stats_ref, k_ref, v_ref):
+    blank_rows = total_keys - slots - rows - span
+
+    def body(q_ref, keys_ref, values_ref, span_ref, bias_ref, out_ref, k_ref, v_ref):
         bias = bias_ref[...]
         lane = lax.broadcasted_iota(jnp.int32, (rows, HD), 1)
         blank = [jnp.zeros((blank_rows, HD), BF16)] if blank_rows else []
         for h in range(local_heads):
             k_ref[h, :slots, :] = keys_ref[h]
             v_ref[h, :slots, :] = values_ref[h]
-            for place, into in ((h * per_head, k_ref), (h * per_head + 1, v_ref)):
-                into[h, slots:, :] = jnp.concatenate(
-                    [q_ref[place, :, at:]] + blank, axis=0
-                )
+            for side, into in enumerate((k_ref, v_ref)):
+                begin = (2 * h + side) * HD
+                more = [span_ref[:, begin : begin + HD], q_ref[h * per_head + side, :, at:]]
+                into[h, slots:, :] = jnp.concatenate(more + blank, axis=0)
         for h in range(local_heads):
             for piece in range(h * per_head, (h + 1) * per_head):
                 peaks = jnp.zeros((rows, HD), F32)
@@ -213,60 +212,14 @@
                         head = first + i
                         out_ref[piece, :, head * HD : (head + 1) * HD] = summed[
                             i * rows : (i + 1) * rows
-                        ]
+                        ].astype(BF16)
                         peaks = jnp.where(lane == head, highest[i], peaks)
                         totals = jnp.where(lane == head, total[i], totals)
-                stats_ref[piece, 0] = peaks
-                stats_ref[piece, 1] = totals
-
-    outs = [array((pieces, rows, at), F32), array((pieces, 2, rows, HD), F32)]
+                out_ref[piece, :, at:] = split_stats(peaks, totals, heads).astype(BF16)
+
+    out = array((pieces, rows, width), BF16)
     scratch = [pltpu.VMEM((local_heads, total_keys, HD), BF16)] * 2
-    return on_chip(body, outs, projected, keys, values, bias, scratch=scratch)
-
-
-def with_span(projected, summed, stats, span_kv, scale):
-    pieces, rows, width = projected.shape
-    heads = (width - HD) // HD
-    per_dot = 256 // rows
-    at = heads * HD
-    local_heads = span_kv.shape[1] // (2 * HD)
-    per_head = pieces // local_heads
-
-    def body(q_ref, summed_ref, stats_ref, span_ref, out_ref):
-        lane = lax.broadcasted_iota(jnp.int32, (rows, HD), 1)
-        for piece in range(pieces):
-            begin = (piece // per_head) * 2 * HD
-            keys = span_ref[:, begin : begin + HD]
-            values = span_ref[:, begin + HD : begin + 2 * HD]
-            peaks = stats_ref[piece, 0]
-            totals = stats_ref[piece, 1]
-            new_peaks = jnp.zeros((rows, HD), F32)
-            added = jnp.zeros((rows, HD), F32)
-            for first in range(0, heads, per_dot):
-                q = heads_together(q_ref, piece, first, per_dot)
-                scores = score(q, keys).reshape(per_dot, rows, keys.shape[0]) * scale
-                highest = jnp.max(scores, axis=-1, keepdims=True)
-                old = [peaks[:, first + i : first + i + 1] for i in range(per_dot)]
-                highest = jnp.maximum(highest, jnp.stack(old))
-                weights = jnp.exp2(scores - highest)
-                total = jnp.sum(weights, axis=-1, keepdims=True)
-                weights = weights.reshape(per_dot * rows, keys.shape[0]).astype(BF16)
-                extra = dot_f32(weights, values)
-                for i in range(per_dot):
-                    head = first + i
-                    cut = slice(head * HD, (head + 1) * HD)
-                    keep = jnp.exp2(old[i] - highest[i])
-                    out_ref[piece, :, cut] = (
-                        summed_ref[piece, :, cut] * keep + extra[i * rows : (i + 1) * rows]
-                    ).astype(BF16)
-                    new_peaks = jnp.where(lane == head, highest[i], new_peaks)
-                    added = jnp.where(lane == head, total[i], added)
-            kept = jnp.exp2(jnp.where(lane < heads, peaks - new_peaks, 0.0))
-            stats = split_stats(new_peaks, totals * kept + added, heads)
-            out_ref[piece, :, at:] = stats.astype(BF16)
-
-    out = array((pieces, rows, width), BF16)
-    return on_chip(body, out, projected, summed, stats, span_kv, free=(1,))
+    return on_chip(body, out, projected, keys, values, span_kv, bias, scratch=scratch)
 
 
 def fold(received, places):
@@ -353,30 +306,48 @@
     return on_chip(body, array((halves, rows, columns), F32), attention, out_weight)
 
 
-def tokens_by_x(span_tokens, depth):
-    xs = lax.axis_size("x")
-    x = lax.axis_index("x")
-    order = [(a, w) for a in range(xs) for w in range(2)]
-
-    def flat(a, w):
-        return a * 2 + w
-
-    first = [(flat(a, w), flat(2 * w + (a & 1), a >> 1)) for a, w in order]
-    second = [(flat(a, w), flat(2 * w + 1 - (a & 1), a >> 1)) for a, w in order]
-    low = span_tokens[:, :depth]
-    high = span_tokens[:, depth:]
-    odd = (x & 1) == 1
-    one = lax.ppermute(jnp.where(odd, high, low), ("x", "width"), first)
-    two = lax.ppermute(jnp.where(odd, low, high), ("x", "width"), second)
-    mine = jnp.stack([jnp.where(odd, two, one), jnp.where(odd, one, two)])
+def swapped_if(flag, x, axis):
+    return jnp.where(flag, jnp.flip(x, axis), x)
+
+
+def tokens_by_features(span_tokens, depth):
+    xs, zh, zl = (lax.axis_size(a) for a in ("x", "zh", "zl"))
+    tokens, _ = span_tokens.shape
+    block = depth // zh
+    x, side, core = (lax.axis_index(a) for a in ("x", "zl", "width"))
+    pieces = span_tokens.reshape(tokens, 2, zh, zl, block).transpose(1, 3, 0, 2, 4)
+    pieces = pieces.reshape(2, zl, tokens, depth)
+    pieces = swapped_if((x & 1) == 1, pieces, 0)
+    pieces = swapped_if(side == 1, pieces, 1)
+    mine = []
+    for i in range(2):
+        for j in range(zl):
+            pairs = []
+            for a in range(xs):
+                for b in range(zl):
+                    for w in range(2):
+                        to = ((2 * w + ((a & 1) ^ i)) * zl + (b ^ j)) * 2 + (a >> 1)
+                        pairs.append(((a * zl + b) * 2 + w, to))
+            mine.append(lax.ppermute(pieces[i, j], ("x", "zl", "width"), pairs))
+    mine = jnp.stack(mine)
     theirs = lax.ppermute(mine, "width", [(0, 1), (1, 0)])
-    upper = lax.axis_index("width") == 1
-    return jnp.concatenate(
-        [jnp.where(upper, theirs, mine), jnp.where(upper, mine, theirs)], axis=0
-    )
-
-
-def biases(lengths, offset, step_count, slots):
+    ready = jnp.stack([mine, theirs])
+    return swapped_if((core ^ (x >> 1)) == 1, ready, 0).reshape(-1, tokens, depth)
+
+
+def added_at_home(partial):
+    spots = lax.axis_size("x") * lax.axis_size("zl")
+    total = partial[0]
+    received = []
+    for mask in range(1, spots):
+        pairs = [(i, i ^ mask) for i in range(spots)]
+        received.append(lax.ppermute(partial[mask], ("x", "zl"), pairs))
+    for more in received:
+        total = total + more
+    return total.astype(BF16)
+
+
+def biases(lengths, offset, step_count, slots, span):
     branch_count = lengths.shape[0]
     rows = step_count * branch_count
     seat = lax.axis_index(SEQ)
@@ -384,8 +355,9 @@
     places = seat * slots + jnp.arange(slots, dtype=jnp.int32)[None]
     row = jnp.arange(rows, dtype=jnp.int32)
     same = (row[:, None] % branch_count == row[None] % branch_count) & (row[None] <= row[:, None])
-    filler = jnp.zeros((rows, -(slots + rows) % HD), jnp.bool_)
-    allowed = jnp.concatenate([places < visible, same & (seat == 0), filler], axis=1)
+    every = jnp.ones((rows, span), jnp.bool_)
+    filler = jnp.zeros((rows, -(slots + span + rows) % HD), jnp.bool_)
+    allowed = jnp.concatenate([places < visible, every, same & (seat == 0), filler], axis=1)
     return jnp.where(allowed, 0.0, MASKED_SCORE).astype(F32)
 
 
@@ -401,37 +373,32 @@
     offset,
 ):
     xs = lax.axis_size("x")
-    zs = lax.axis_size("z")
+    zs = lax.axis_size(Z)
     step_count, branch_count, depth = hidden.shape
     rows = step_count * branch_count
     scale = LOG2E / math.sqrt(HD)
-    span_weight = lax.all_gather(kv_weight, "z", axis=0, tiled=True)
     tokens = span_tokens.shape[0]
+    span_weight = lax.all_gather(kv_weight, "zh", axis=0, tiled=True)
 
     partial = project(hidden.reshape(rows, depth), query_weight, kv_weight, xs)
     partial = exchanged(partial, "x")
-    partial, span_tokens = lax.optimization_barrier((partial, span_tokens))
-    ready = tokens_by_x(span_tokens, span_weight.shape[0])
+    ready = tokens_by_features(span_tokens, span_weight.shape[0])
     partial = add_over_x(partial, zs)
-    partial = exchanged(partial, "z")
+    partial = exchanged(partial, Z)
     own = add_over_z(partial)
-    own = exchanged(own, "z")
+    own = exchanged(own, Z)
+    span_partial = dot_f32(ready.reshape(-1, span_weight.shape[0]), span_weight)
+    span_kv = added_at_home(span_partial.reshape(-1, tokens, kv_weight.shape[1]))
     columns = fan(own, rows, xs, HD)
-    columns, ready = lax.optimization_barrier((columns, ready))
     projected = exchanged(columns, "x")
 
-    span_partial = dot_f32(ready.reshape(xs * tokens, span_weight.shape[0]), span_weight)
-    span_partial = span_partial.reshape(xs, tokens, kv_weight.shape[1])
-    span_kv = jnp.sum(exchanged(span_partial, "x"), axis=0).astype(BF16)
-
-    bias = biases(lengths, offset, step_count, cache_keys.shape[0])
+    bias = biases(lengths, offset, step_count, cache_keys.shape[0], tokens)
     keys = cache_keys.transpose(1, 0, 2)
     values = cache_values.transpose(1, 0, 2)
-    summed, stats = attend(projected, keys, values, bias, scale)
-    partial = with_span(projected, summed, stats, span_kv, scale)
+    partial = attend(projected, keys, values, span_kv, bias, scale)
     folded = fold(exchanged(partial, "x"), zs)
-    ours = finish(exchanged(folded, "z"))
-    attention = exchanged(fan(exchanged(ours, "z"), rows, xs, 0), "x")
+    ours = finish(exchanged(folded, Z))
+    attention = exchanged(fan(exchanged(ours, Z), rows, xs, 0), "x")
     halves = exchanged(close(attention, out_weight, 2), "width")
     attended = (halves[0] + halves[1]).astype(BF16)
     return (span_kv, attended.reshape(step_count, branch_count, attended.shape[1]))
@@ -439,8 +406,8 @@
 
 def solution(mesh):
     finer = Mesh(
-        mesh.devices.reshape(mesh.shape["groups"], 4, 16, mesh.shape["width"]),
-        ("groups", "x", "z", "width"),
+        mesh.devices.reshape(mesh.shape["groups"], 4, 8, 2, mesh.shape["width"]),
+        ("groups", "x", "zh", "zl", "width"),
     )
     placed = (
         P(GROUPS_SEQ, "width"),

time: 213 us -> 214 us (level)
  starting transfers between devices: 52.6 us -> 71.6 us
  waiting for transfers between devices: 50.4 us -> 42.6 us
  blocking collectives: 71.3 us -> 65.9 us
  Pallas kernels: 15.4 us -> 11.7 us
    ppermute x3 -> x12, starting transfers between devices: 22.9 us -> 46.3 us  [the longest x4 27.9 us: tokens_by_features(): mine.append(lax.ppermute(pieces[i, j], ('x', 'zl', 'width'), pairs))]
    all_to_all x5 -> x4, waiting for transfers between devices: 48 us -> 30.6 us  [exchanged(): return lax.all_to_all(pieces, axis, split_axis=0, concat_axis=0, tiled=True)]
    ppermute x3 -> x12, waiting for transfers between devices: 0.01 us -> 11 us  [the longest x4 6.63 us: tokens_by_features(): mine.append(lax.ppermute(pieces[i, j], ('x', 'zl', 'width'), pairs))]
    all_to_all x5, blocking collectives: 71.3 us -> 65.9 us  [exchanged(): return lax.all_to_all(pieces, axis, split_axis=0, concat_axis=0, tiled=True)]
    all_to_all x5 -> x4, starting transfers between devices: 29.6 us -> 25.2 us  [exchanged(): return lax.all_to_all(pieces, axis, split_axis=0, concat_axis=0, tiled=True)]
    pallas_call x9 -> x8, Pallas kernels: 12.2 us -> 8.48 us  [on_chip(): pl.pallas_call(body, out_shape=shapes, scratch_shapes=scratch, compiler_p...]
  transfers between devices with their start and end apart: 9 -> 17, of which waited for: 5 -> 7; matrix products, arithmetic and copies ran while one was open for 2% -> 3% of each run, Pallas kernels for 5% -> 3%
where the time goes in v3:
time: 214 us
  starting transfers between devices  71.6 us (33%)
  blocking collectives  65.9 us (31%)
  waiting for transfers between devices  42.6 us (20%)
  between operations  15.1 us (7%)
  Pallas kernels  11.7 us (5%)
  local copies, waits for them, and re-layouts  3.09 us (1%)
  matrix products  2.32 us (1%)
    all_to_all x5, blocking collectives, exchanged(): return lax.all_to_all(pieces, axis, split_axis=0, concat_axis=0, tiled=True)  65.9 us
    all_to_all x4, waiting for transfers between devices, exchanged(): return lax.all_to_all(pieces, axis, split_axis=0, concat_axis=0, tiled=True)  30.6 us
    ppermute x4, starting transfers between devices, tokens_by_features(): mine.append(lax.ppermute(pieces[i, j], ('x', 'zl', 'width'), pairs))  27.9 us
    all_to_all x4, starting transfers between devices, exchanged(): return lax.all_to_all(pieces, axis, split_axis=0, concat_axis=0, tiled=True)  25.2 us
    ppermute x7, starting transfers between devices, added_at_home(): received.append(lax.ppermute(partial[mask], ('x', 'zl'), pairs))  12.9 us
    pallas_call x8, Pallas kernels, on_chip(): pl.pallas_call(body, out_shape=shapes, scratch_shapes=scratch, compiler_p...  8.48 us
    ppermute x4, waiting for transfers between devices, tokens_by_features(): mine.append(lax.ppermute(pieces[i, j], ('x', 'zl', 'width'), pairs))  6.63 us
    ppermute x1, starting transfers between devices, tokens_by_features(): theirs = lax.ppermute(mine, 'width', [(0, 1), (1, 0)])  5.52 us
  transfers between devices with their start and end apart: 17, of which 7 were waited for; matrix products, arithmetic and copies ran while one was open for 3% of the time, Pallas kernels for 3%

profile of v3, /device:TPU:33, one launch (start us, length us, event | category | flops | bytes accessed | tf_op | source)
XLA Modules:
  0.0 213.8 jit_solution(4809509248105288345)
XLA Ops:
  7.2 0.1 all-gather.2.cloned.1.call-start
  7.2 0.7 all-gather.2.cloned.1.call-update
  8.0 3.2 %project.1 = f32[4,64,1152]{2,1,0:T(8,128)} custom-call(bf16[64,256]{1,0:T(8,128)(2,1)} %bitcast.38, bf16[256,4096]{1,0:T(8,128)(2,1)} %query_hbm.1, bf16[256,512]{1,0:T(8,128)(2,1)} %fresh_hbm.1), custom_call_target="tpu_custom_call" | custom-call | tf_op jit(solution)/shard_map/project/pallas_call | solution.py:75
  11.2 5.1 %all-to-all-start = ((f32[4,64,1152]{2,1,0:T(8,128)}), f32[4,64,1152]{2,1,0:T(8,128)S(1)}, u32[]{:S(2)}, u32[]{:S(2)}) async-start(f32[4,64,1152]{2,1,0:T(8,128)} %project.1), calls=%async_computation | async-start | bytes 2359296 | tf_op jit(solution)/shard_map/all_to_all | solution.py:25
  16.4 0.4 reshape.72
  16.7 0.1 copy.19
  16.8 0.0 copy-start.10
  16.8 0.2 reshape.73
  17.1 0.1 reverse_select_fusion.2
  17.2 0.1 reverse_select_fusion.1
  17.4 6.1 %collective-permute-start.3 = (bf16[32,2048]{1,0:T(8,128)(2,1)S(1)}, bf16[32,2048]{1,0:T(8,128)(2,1)S(1)}, u32[]{:S(2)}, u32[]{:S(2)}) collective-permute-start(bf16[32,2048]{1,0:T(8,128)(2,1)S(1)} %get-tuple-element.12), channel_id=1, source_target_pairs={{0,34},{1,98},{2,32},{3,96},{32,2},{33,66},{34,0},{35,64},{64,35},... | collective-permute-start | bytes 393224 | tf_op jit(solution)/shard_map/ppermute | solution.py:331
  23.4 15.9 %collective-permute-start.2 = (bf16[32,2048]{1,0:T(8,128)(2,1)S(1)}, bf16[32,2048]{1,0:T(8,128)(2,1)S(1)}, u32[]{:S(2)}, u32[]{:S(2)}) collective-permute-start(bf16[32,2048]{1,0:T(8,128)(2,1)S(1)} %get-tuple-element.13), channel_id=1, source_target_pairs={{0,32},{1,96},{2,34},{3,98},{32,0},{33,64},{34,2},{35,66},{64,33},... | collective-permute-start | bytes 393224 | tf_op jit(solution)/shard_map/ppermute | solution.py:331
  39.3 2.8 %collective-permute-start.1 = (bf16[32,2048]{1,0:T(8,128)(2,1)S(1)}, bf16[32,2048]{1,0:T(8,128)(2,1)S(1)}, u32[]{:S(2)}, u32[]{:S(2)}) collective-permute-start(bf16[32,2048]{1,0:T(8,128)(2,1)S(1)} %get-tuple-element.14), channel_id=1, source_target_pairs={{0,2},{1,66},{2,0},{3,64},{32,34},{33,98},{34,32},{35,96},{64,3},{... | collective-permute-start | bytes 393224 | tf_op jit(solution)/shard_map/ppermute | solution.py:331
  42.1 3.2 %collective-permute-start = (bf16[32,2048]{1,0:T(8,128)(2,1)S(1)}, bf16[32,2048]{1,0:T(8,128)(2,1)S(1)}, u32[]{:S(2)}, u32[]{:S(2)}) collective-permute-start(bf16[32,2048]{1,0:T(8,128)(2,1)S(1)} %get-tuple-element.11), channel_id=1, source_target_pairs={{0,0},{1,64},{2,2},{3,66},{32,32},{33,96},{34,34},{35,98},{64,1},{... | collective-permute-start | bytes 393224 | tf_op jit(solution)/shard_map/ppermute | solution.py:331
  46.0 2.4 %collective-permute-done.2 = bf16[32,2048]{1,0:T(8,128)(2,1)S(1)} collective-permute-done((bf16[32,2048]{1,0:T(8,128)(2,1)S(1)}, bf16[32,2048]{1,0:T(8,128)(2,1)S(1)}, u32[]{:S(2)}, u32[]{:S(2)}) %collective-permute-start.2) | collective-permute-done | bytes 131104 | tf_op jit(solution)/shard_map/ppermute | solution.py:331
  48.4 4.2 %collective-permute-done.1 = bf16[32,2048]{1,0:T(8,128)(2,1)S(1)} collective-permute-done((bf16[32,2048]{1,0:T(8,128)(2,1)S(1)}, bf16[32,2048]{1,0:T(8,128)(2,1)S(1)}, u32[]{:S(2)}, u32[]{:S(2)}) %collective-permute-start.1) | collective-permute-done | bytes 131104 | tf_op jit(solution)/shard_map/ppermute | solution.py:331
  52.6 0.0 collective-permute-done
  52.6 0.1 fusion.10
  52.7 5.5 %collective-permute-start.4 = (bf16[4,32,2048]{2,1,0:T(8,128)(2,1)S(1)}, bf16[4,32,2048]{2,1,0:T(8,128)(2,1)S(1)}, u32[]{:S(2)}, u32[]{:S(2)}) collective-permute-start(bf16[4,32,2048]{2,1,0:T(8,128)(2,1)S(1)} %get-tuple-element.10), channel_id=1, source_target_pairs={{0,1},{1,0},{2,3},{3,2},{4,5},{5,4},{6,7},{7,6},{8,9},{9,8},{10,11... | collective-permute-start | bytes 1572872 | tf_op jit(solution)/shard_map/ppermute | solution.py:333
  58.2 0.0 all-to-all-done.in_ref
  58.2 0.8 shard_map.104
  59.0 7.7 %all-to-all-start.1 = ((f32[16,8,640]{2,1,0:T(8,128)}), f32[16,8,640]{2,1,0:T(8,128)S(1)}, u32[]{:S(2)}, u32[]{:S(2)}) async-start(f32[16,8,640]{2,1,0:T(8,128)} %shard_map.104), calls=%async_computation.1 | async-start | bytes 655360 | tf_op jit(solution)/shard_map/all_to_all | solution.py:25
  66.8 0.1 lt.26
  66.8 0.1 fusion.9
  66.9 0.1 broadcast_compare_fusion
  67.1 0.7 concatenate.3
  67.8 0.1 pad_maximum_fusion
  67.9 0.2 reverse_select_fusion
  68.1 25.3 %all-to-all-done.1.in_ref = f32[16,8,640]{2,1,0:T(8,128)S(1)} async-done(((f32[16,8,640]{2,1,0:T(8,128)}), f32[16,8,640]{2,1,0:T(8,128)S(1)}, u32[]{:S(2)}, u32[]{:S(2)}) %all-to-all-start.1) | async-done | bytes 327712 | tf_op jit(solution)/shard_map/all_to_all | solution.py:25
  93.5 0.7 shard_map.105
  94.2 8.7 %all-to-all-start.2 = ((bf16[16,8,640]{2,1,0:T(8,128)(2,1)}), bf16[16,8,640]{2,1,0:T(8,128)(2,1)S(1)}, u32[]{:S(2)}, u32[]{:S(2)}) async-start(bf16[16,8,640]{2,1,0:T(8,128)(2,1)} %shard_map.105), calls=%async_computation.2 | async-start | bytes 327680 | tf_op jit(solution)/shard_map/all_to_all | solution.py:25
  102.9 0.3 all-gather.2.cloned.1.call-done
  103.2 2.3 %fusion.12 = f32[256,512]{1,0:T(8,128)S(1)} fusion(bf16[256,2048]{1,0:T(8,128)(2,1)S(1)} %bitcast.32, bf16[2048,512]{1,0:T(8,128)(2,1)} %all-gather.2.cloned.1.call-done), kind=kOutput, calls=%fused_computation.32 | convolution fusion | flops 536870912 | bytes 3670016 | tf_op jit(solution)/shard_map/dot_general | solution.py:29
  105.5 0.0 copy-start.3
  105.5 0.0 copy-start.4
  105.5 0.7 fusion.11
  106.2 1.0 collective-permute-start.11
  107.3 2.2 %collective-permute-start.10 = (f32[32,512]{1,0:T(8,128)S(1)}, f32[32,512]{1,0:T(8,128)S(1)}, u32[]{:S(2)}, u32[]{:S(2)}) collective-permute-start(f32[32,512]{1,0:T(8,128)S(1)} %get-tuple-element.4), channel_id=1, source_target_pairs={{0,96},{2,98},{32,64},{34,66},{64,32},{66,34},{96,0},{98,2},{1,97}... | collective-permute-start | bytes 196616 | tf_op jit(solution)/shard_map/ppermute | solution.py:344
  109.6 5.2 %all-to-all-done.2.in_ref = bf16[16,8,640]{2,1,0:T(8,128)(2,1)S(1)} async-done(((bf16[16,8,640]{2,1,0:T(8,128)(2,1)}), bf16[16,8,640]{2,1,0:T(8,128)(2,1)S(1)}, u32[]{:S(2)}, u32[]{:S(2)}) %all-to-all-start.2) | async-done | bytes 163872 | tf_op jit(solution)/shard_map/all_to_all | solution.py:25
  114.8 0.9 shard_map.106
  115.6 3.7 %all-to-all-start.3 = ((bf16[4,64,1152]{2,1,0:T(8,128)(2,1)}), bf16[4,64,1152]{2,1,0:T(8,128)(2,1)S(1)}, u32[]{:S(2)}, u32[]{:S(2)}) async-start(bf16[4,64,1152]{2,1,0:T(8,128)(2,1)} %shard_map.106), calls=%async_computation.3 | async-start | bytes 1179648 | tf_op jit(solution)/shard_map/all_to_all | solution.py:25
  119.3 7.0 %collective-permute-start.9 = (f32[32,512]{1,0:T(8,128)}, f32[32,512]{1,0:T(8,128)S(1)}, u32[]{:S(2)}, u32[]{:S(2)}) collective-permute-start(f32[32,512]{1,0:T(8,128)} %get-tuple-element.5), channel_id=1, source_target_pairs={{0,66},{2,64},{32,98},{34,96},{64,2},{66,0},{96,34},{98,32},{1,67}... | collective-permute-start | bytes 196616 | tf_op jit(solution)/shard_map/ppermute | solution.py:344
  126.3 0.3 collective-permute-start.7
  126.6 0.0 collective-permute-done.11
  126.6 1.3 collective-permute-start.6
  127.9 0.0 collective-permute-done.10
  127.9 0.6 copy-done.8
  128.5 1.1 collective-permute-start.5
  129.6 0.1 copy_bitcast_fusion
  129.8 0.0 collective-permute-done.9
  129.8 2.3 %collective-permute-done.8 = f32[32,512]{1,0:T(8,128)S(1)} collective-permute-done((f32[32,512]{1,0:T(8,128)}, f32[32,512]{1,0:T(8,128)S(1)}, u32[]{:S(2)}, u32[]{:S(2)}) %collective-permute-start.8) | collective-permute-done | bytes 65568 | tf_op jit(solution)/shard_map/ppermute | solution.py:344
  132.1 2.0 collective-permute-done.6
  134.2 0.0 copy-start.1
  134.2 4.8 %shard_map.107 = bf16[4,64,1152]{2,1,0:T(8,128)(2,1)S(1)} custom-call(bf16[4,64,1152]{2,1,0:T(8,128)(2,1)S(1)} %all-to-all-done.3.q_ref, bf16[2,1024,128]{2,1,0:T(8,128)(2,1)S(1)} %get-tuple-element.16.keys_ref, bf16[2,1024,128]{2,1,0:T(8,128)(2,1)S(1)} %get-tuple-element.15.values_ref, bf16[32,512]{1,0:T(8,128)(2,1)S(1)} %fusion.6.span_ref, ...), custom_call_target="tpu_custom_call" | custom-call | tf_op jit(solution)/shard_map/pallas_call | solution.py:36
  139.0 0.0 copy-start
  139.0 11.4 %all_to_all.45.in_ref = bf16[4,64,1152]{2,1,0:T(8,128)(2,1)S(1)} all-to-all(bf16[4,64,1152]{2,1,0:T(8,128)(2,1)S(1)} %shard_map.107), channel_id=1, replica_groups=mesh['groups'=2,'x'=4,'zh'=8,'zl'=2,'width'=2] {'x'}, dimensions={0} | all-to-all | bytes 1179648 | tf_op jit(solution)/shard_map/all_to_all | solution.py:25
  150.5 0.6 shard_map.108
  151.1 18.3 %all_to_all.46.in_ref = bf16[16,8,640]{2,1,0:T(8,128)(2,1)S(1)} all-to-all(bf16[16,8,640]{2,1,0:T(8,128)(2,1)S(1)} %shard_map.108), channel_id=1, replica_groups=mesh['groups'=2,'x'=4,'zh'=8,'zl'=2,'width'=2] {'zh','zl'}, dimensions={0} | all-to-all | bytes 327680 | tf_op jit(solution)/shard_map/all_to_all | solution.py:25
  169.3 0.3 shard_map.109
  169.6 16.4 %all_to_all.47.in_ref = bf16[16,8,512]{2,1,0:T(8,128)(2,1)S(1)} all-to-all(bf16[16,8,512]{2,1,0:T(8,128)(2,1)S(1)} %shard_map.109), channel_id=1, replica_groups=mesh['groups'=2,'x'=4,'zh'=8,'zl'=2,'width'=2] {'zh','zl'}, dimensions={0} | all-to-all | bytes 262144 | tf_op jit(solution)/shard_map/all_to_all | solution.py:25
  186.0 9.4 %all_to_all.48.in_ref = bf16[4,64,1024]{2,1,0:T(8,128)(2,1)S(1)} all-to-all(bf16[4,64,1024]{2,1,0:T(8,128)(2,1)S(1)} %shard_map.110), channel_id=1, replica_groups=mesh['groups'=2,'x'=4,'zh'=8,'zl'=2,'width'=2] {'x'}, dimensions={0} | all-to-all | bytes 1048576 | tf_op jit(solution)/shard_map/all_to_all | solution.py:25
  195.4 0.5 shard_map.111
  195.8 10.5 %all_to_all.49 = f32[2,64,128]{2,1,0:T(8,128)S(1)} all-to-all(f32[2,64,128]{2,1,0:T(8,128)S(1)} %shard_map.111), channel_id=1, replica_groups=mesh['groups'=2,'x'=4,'zh'=8,'zl'=2,'width'=2] {'width'}, dimensions={0} | all-to-all | bytes 131072 | tf_op jit(solution)/shard_map/all_to_all | solution.py:25
  206.3 0.6 fusion.7
  (32 shorter events, 0.2 us)
Async XLA Ops:
  7.2 96.0 %all-gather.2.cloned.1.call-start = ((), (), s32[]{:S(2)}) async-start(), calls=%async_computation.9 | async-start | bytes 2359296 | tf_op jit(solution)/shard_map/all_gather | solution.py:381
  8.0 8.4 %copy-start.2 = (bf16[32,8192]{1,0:T(8,128)(2,1)S(1)}, bf16[32,8192]{1,0:T(8,128)(2,1)}, u32[]{:S(2)}) copy-start(bf16[32,8192]{1,0:T(8,128)(2,1)} %param.9) | copy-start | bytes 1572868
  11.2 47.0 %all-to-all-start = ((f32[4,64,1152]{2,1,0:T(8,128)}), f32[4,64,1152]{2,1,0:T(8,128)S(1)}, u32[]{:S(2)}, u32[]{:S(2)}) async-start(f32[4,64,1152]{2,1,0:T(8,128)} %project.1), calls=%async_computation | async-start | bytes 2359296 | tf_op jit(solution)/shard_map/all_to_all | solution.py:25
  16.8 29.1 %copy-start.10 = (s32[32]{0:T(128)S(1)}, s32[32]{0:T(128)}, u32[]{:S(2)}) copy-start(s32[32]{0:T(128)} %param.16) | copy-start | bytes 388
  17.4 28.6 %collective-permute-start.3 = (bf16[32,2048]{1,0:T(8,128)(2,1)S(1)}, bf16[32,2048]{1,0:T(8,128)(2,1)S(1)}, u32[]{:S(2)}, u32[]{:S(2)}) collective-permute-start(bf16[32,2048]{1,0:T(8,128)(2,1)S(1)} %get-tuple-element.12), channel_id=1, source_target_pairs={{0,34},{1,98},{2,32},{3,96},{32,2},{33,66},{34,0},{35,64},{64,35},... | collective-permute-start | bytes 393224 | tf_op jit(solution)/shard_map/ppermute | solution.py:331
  23.4 25.0 %collective-permute-start.2 = (bf16[32,2048]{1,0:T(8,128)(2,1)S(1)}, bf16[32,2048]{1,0:T(8,128)(2,1)S(1)}, u32[]{:S(2)}, u32[]{:S(2)}) collective-permute-start(bf16[32,2048]{1,0:T(8,128)(2,1)S(1)} %get-tuple-element.13), channel_id=1, source_target_pairs={{0,32},{1,96},{2,34},{3,98},{32,0},{33,64},{34,2},{35,66},{64,33},... | collective-permute-start | bytes 393224 | tf_op jit(solution)/shard_map/ppermute | solution.py:331
  39.3 13.3 %collective-permute-start.1 = (bf16[32,2048]{1,0:T(8,128)(2,1)S(1)}, bf16[32,2048]{1,0:T(8,128)(2,1)S(1)}, u32[]{:S(2)}, u32[]{:S(2)}) collective-permute-start(bf16[32,2048]{1,0:T(8,128)(2,1)S(1)} %get-tuple-element.14), channel_id=1, source_target_pairs={{0,2},{1,66},{2,0},{3,64},{32,34},{33,98},{34,32},{35,96},{64,3},{... | collective-permute-start | bytes 393224 | tf_op jit(solution)/shard_map/ppermute | solution.py:331
  42.1 10.5 %collective-permute-start = (bf16[32,2048]{1,0:T(8,128)(2,1)S(1)}, bf16[32,2048]{1,0:T(8,128)(2,1)S(1)}, u32[]{:S(2)}, u32[]{:S(2)}) collective-permute-start(bf16[32,2048]{1,0:T(8,128)(2,1)S(1)} %get-tuple-element.11), channel_id=1, source_target_pairs={{0,0},{1,64},{2,2},{3,66},{32,32},{33,96},{34,34},{35,98},{64,1},{... | collective-permute-start | bytes 393224 | tf_op jit(solution)/shard_map/ppermute | solution.py:331
  52.7 15.1 %collective-permute-start.4 = (bf16[4,32,2048]{2,1,0:T(8,128)(2,1)S(1)}, bf16[4,32,2048]{2,1,0:T(8,128)(2,1)S(1)}, u32[]{:S(2)}, u32[]{:S(2)}) collective-permute-start(bf16[4,32,2048]{2,1,0:T(8,128)(2,1)S(1)} %get-tuple-element.10), channel_id=1, source_target_pairs={{0,1},{1,0},{2,3},{3,2},{4,5},{5,4},{6,7},{7,6},{8,9},{9,8},{10,11... | collective-permute-start | bytes 1572872 | tf_op jit(solution)/shard_map/ppermute | solution.py:333
  59.0 34.5 %all-to-all-start.1 = ((f32[16,8,640]{2,1,0:T(8,128)}), f32[16,8,640]{2,1,0:T(8,128)S(1)}, u32[]{:S(2)}, u32[]{:S(2)}) async-start(f32[16,8,640]{2,1,0:T(8,128)} %shard_map.104), calls=%async_computation.1 | async-start | bytes 655360 | tf_op jit(solution)/shard_map/all_to_all | solution.py:25
  94.2 20.6 %all-to-all-start.2 = ((bf16[16,8,640]{2,1,0:T(8,128)(2,1)}), bf16[16,8,640]{2,1,0:T(8,128)(2,1)S(1)}, u32[]{:S(2)}, u32[]{:S(2)}) async-start(bf16[16,8,640]{2,1,0:T(8,128)(2,1)} %shard_map.105), calls=%async_computation.2 | async-start | bytes 327680 | tf_op jit(solution)/shard_map/all_to_all | solution.py:25
  103.2 6.3 %copy-start.5 = (pred[64,1152]{1,0:T(8,128)(4,1)S(1)}, pred[64,1152]{1,0:T(8,128)(4,1)}, u32[]{:S(2)}) copy-start(pred[64,1152]{1,0:T(8,128)(4,1)} %concatenate.3) | copy-start | bytes 221188
  105.5 24.1 %copy-start.3 = (bf16[1024,2,128]{2,1,0:T(2,128)(2,1)S(1)}, bf16[1024,2,128]{2,1,0:T(2,128)(2,1)}, u32[]{:S(2)}) copy-start(bf16[1024,2,128]{2,1,0:T(2,128)(2,1)} %param.14) | copy-start | bytes 1572868
  105.5 24.1 %copy-start.4 = (bf16[1024,2,128]{2,1,0:T(2,128)(2,1)S(1)}, bf16[1024,2,128]{2,1,0:T(2,128)(2,1)}, u32[]{:S(2)}) copy-start(bf16[1024,2,128]{2,1,0:T(2,128)(2,1)} %param.13) | copy-start | bytes 1572868
  106.2 20.3 %collective-permute-start.11 = (f32[32,512]{1,0:T(8,128)S(1)}, f32[32,512]{1,0:T(8,128)S(1)}, u32[]{:S(2)}, u32[]{:S(2)}) collective-permute-start(f32[32,512]{1,0:T(8,128)S(1)} %get-tuple-element.3), channel_id=1, source_target_pairs={{0,98},{2,96},{32,66},{34,64},{64,34},{66,32},{96,2},{98,0},{1,99}... | collective-permute-start | bytes 196616 | tf_op jit(solution)/shard_map/ppermute | solution.py:344
  107.3 20.6 %collective-permute-start.10 = (f32[32,512]{1,0:T(8,128)S(1)}, f32[32,512]{1,0:T(8,128)S(1)}, u32[]{:S(2)}, u32[]{:S(2)}) collective-permute-start(f32[32,512]{1,0:T(8,128)S(1)} %get-tuple-element.4), channel_id=1, source_target_pairs={{0,96},{2,98},{32,64},{34,66},{64,32},{66,34},{96,0},{98,2},{1,97}... | collective-permute-start | bytes 196616 | tf_op jit(solution)/shard_map/ppermute | solution.py:344
  115.6 18.6 %all-to-all-start.3 = ((bf16[4,64,1152]{2,1,0:T(8,128)(2,1)}), bf16[4,64,1152]{2,1,0:T(8,128)(2,1)S(1)}, u32[]{:S(2)}, u32[]{:S(2)}) async-start(bf16[4,64,1152]{2,1,0:T(8,128)(2,1)} %shard_map.106), calls=%async_computation.3 | async-start | bytes 1179648 | tf_op jit(solution)/shard_map/all_to_all | solution.py:25
  119.3 10.5 %collective-permute-start.9 = (f32[32,512]{1,0:T(8,128)}, f32[32,512]{1,0:T(8,128)S(1)}, u32[]{:S(2)}, u32[]{:S(2)}) collective-permute-start(f32[32,512]{1,0:T(8,128)} %get-tuple-element.5), channel_id=1, source_target_pairs={{0,66},{2,64},{32,98},{34,96},{64,2},{66,0},{96,34},{98,32},{1,67}... | collective-permute-start | bytes 196616 | tf_op jit(solution)/shard_map/ppermute | solution.py:344
  126.3 5.8 %collective-permute-start.8 = (f32[32,512]{1,0:T(8,128)}, f32[32,512]{1,0:T(8,128)S(1)}, u32[]{:S(2)}, u32[]{:S(2)}) collective-permute-start(f32[32,512]{1,0:T(8,128)} %get-tuple-element.6), channel_id=1, source_target_pairs={{0,64},{2,66},{32,96},{34,98},{64,0},{66,2},{96,32},{98,34},{1,65}... | collective-permute-start | bytes 196616 | tf_op jit(solution)/shard_map/ppermute | solution.py:344
  126.3 5.8 %collective-permute-start.7 = (f32[32,512]{1,0:T(8,128)}, f32[32,512]{1,0:T(8,128)S(1)}, u32[]{:S(2)}, u32[]{:S(2)}) collective-permute-start(f32[32,512]{1,0:T(8,128)} %get-tuple-element.7), channel_id=1, source_target_pairs={{0,34},{2,32},{32,2},{34,0},{64,98},{66,96},{96,66},{98,64},{1,35}... | collective-permute-start | bytes 196616 | tf_op jit(solution)/shard_map/ppermute | solution.py:344
  126.6 1.3 copy-start.6
  126.6 7.5 %collective-permute-start.6 = (f32[32,512]{1,0:T(8,128)}, f32[32,512]{1,0:T(8,128)S(1)}, u32[]{:S(2)}, u32[]{:S(2)}) collective-permute-start(f32[32,512]{1,0:T(8,128)} %get-tuple-element.8), channel_id=1, source_target_pairs={{0,32},{2,34},{32,0},{34,2},{64,96},{66,98},{96,64},{98,66},{1,33}... | collective-permute-start | bytes 196616 | tf_op jit(solution)/shard_map/ppermute | solution.py:344
  127.9 0.6 copy-start.8
  128.5 5.6 %collective-permute-start.5 = (f32[32,512]{1,0:T(8,128)}, f32[32,512]{1,0:T(8,128)S(1)}, u32[]{:S(2)}, u32[]{:S(2)}) collective-permute-start(f32[32,512]{1,0:T(8,128)} %get-tuple-element.2), channel_id=1, source_target_pairs={{0,2},{2,0},{32,34},{34,32},{64,66},{66,64},{96,98},{98,96},{1,3},... | collective-permute-start | bytes 196616 | tf_op jit(solution)/shard_map/ppermute | solution.py:344
  129.6 4.5 %copy-start.7 = (f32[32,512]{1,0:T(8,128)S(1)}, f32[32,512]{1,0:T(8,128)}, u32[]{:S(2)}) copy-start(f32[32,512]{1,0:T(8,128)} %copy-done.6) | copy-start | bytes 196612
  129.6 4.5 %copy-start.9 = (f32[32,512]{1,0:T(8,128)S(1)}, f32[32,512]{1,0:T(8,128)}, u32[]{:S(2)}) copy-start(f32[32,512]{1,0:T(8,128)} %copy-done.8) | copy-start | bytes 196612
  134.2 16.9 %copy-start.1 = (bf16[32,512]{1,0:T(8,128)(2,1)}, bf16[32,512]{1,0:T(8,128)(2,1)S(1)}, u32[]{:S(2)}) copy-start(bf16[32,512]{1,0:T(8,128)(2,1)S(1)} %fusion.6.span_ref) | copy-start | bytes 98308
  139.0 56.3 %copy-start = (bf16[4096,256]{1,0:T(8,128)(2,1)S(1)}, bf16[4096,256]{1,0:T(8,128)(2,1)}, u32[]{:S(2)}) copy-start(bf16[4096,256]{1,0:T(8,128)(2,1)} %weight_ref.1) | copy-start | bytes 6291460
Sparse Core Ops, SparseCore 0:
  9.8 93.3 all-gather.1

commit v4 on v3

--- a/solution.py
+++ b/solution.py
@@ -10,8 +10,7 @@
 
 
 HD = 128
-Z = ("zh", "zl")
-SEQ = ("x", *Z)
+SEQ = ("x", "z")
 GROUPS_SEQ = ("groups", *SEQ)
 SEQ_WIDTH = (*SEQ, "width")
 MASKED_SCORE = -1e30
@@ -310,38 +309,58 @@
     return jnp.where(flag, jnp.flip(x, axis), x)
 
 
+def halves_of_blocks(span_tokens, places):
+    tokens, width = span_tokens.shape
+    block = width // (4 * places)
+
+    def body(in_ref, out_ref):
+        for k in range(2):
+            for place in range(places):
+                for half in range(2):
+                    begin = ((k * places + place) * 2 + half) * block
+                    cut = slice(place * block, (place + 1) * block)
+                    out_ref[half, k, :, cut] = in_ref[:, begin : begin + block]
+
+    out = array((2, 2, tokens, places * block), BF16)
+    return on_chip(body, out, span_tokens)
+
+
+def with_neighbour(x):
+    count = lax.axis_size("groups")
+    return lax.ppermute(x, "groups", [(g, g ^ 1) for g in range(count)])
+
+
 def tokens_by_features(span_tokens, depth):
-    xs, zh, zl = (lax.axis_size(a) for a in ("x", "zh", "zl"))
-    tokens, _ = span_tokens.shape
-    block = depth // zh
-    x, side, core = (lax.axis_index(a) for a in ("x", "zl", "width"))
-    pieces = span_tokens.reshape(tokens, 2, zh, zl, block).transpose(1, 3, 0, 2, 4)
-    pieces = pieces.reshape(2, zl, tokens, depth)
-    pieces = swapped_if((x & 1) == 1, pieces, 0)
-    pieces = swapped_if(side == 1, pieces, 1)
+    xs, zs = (lax.axis_size(a) for a in ("x", "z"))
+    tokens = span_tokens.shape[0]
+    group, x, core = (lax.axis_index(a) for a in ("groups", "x", "width"))
+    odd = (group & 1) == 1
+    pieces = halves_of_blocks(span_tokens, zs)
+    received = with_neighbour(jnp.where(odd, pieces[0], pieces[1]))
+    both = jnp.stack([jnp.where(odd, pieces[1], pieces[0]), received], axis=1)
+    both = swapped_if((x & 1) == 1, both, 0)
     mine = []
     for i in range(2):
-        for j in range(zl):
-            pairs = []
-            for a in range(xs):
-                for b in range(zl):
-                    for w in range(2):
-                        to = ((2 * w + ((a & 1) ^ i)) * zl + (b ^ j)) * 2 + (a >> 1)
-                        pairs.append(((a * zl + b) * 2 + w, to))
-            mine.append(lax.ppermute(pieces[i, j], ("x", "zl", "width"), pairs))
+        pairs = []
+        for a in range(xs):
+            for w in range(2):
+                pairs.append((a * 2 + w, (2 * w + ((a & 1) ^ i)) * 2 + (a >> 1)))
+        mine.append(lax.ppermute(both[i], ("x", "width"), pairs))
     mine = jnp.stack(mine)
     theirs = lax.ppermute(mine, "width", [(0, 1), (1, 0)])
     ready = jnp.stack([mine, theirs])
-    return swapped_if((core ^ (x >> 1)) == 1, ready, 0).reshape(-1, tokens, depth)
+    return swapped_if((core ^ (x >> 1)) == 1, ready, 0).reshape(xs, 2, tokens, depth)
 
 
 def added_at_home(partial):
-    spots = lax.axis_size("x") * lax.axis_size("zl")
+    xs = lax.axis_size("x")
+    received = with_neighbour(partial[:, 1])
+    partial = partial[:, 0] + received
     total = partial[0]
     received = []
-    for mask in range(1, spots):
-        pairs = [(i, i ^ mask) for i in range(spots)]
-        received.append(lax.ppermute(partial[mask], ("x", "zl"), pairs))
+    for mask in range(1, xs):
+        pairs = [(i, i ^ mask) for i in range(xs)]
+        received.append(lax.ppermute(partial[mask], "x", pairs))
     for more in received:
         total = total + more
     return total.astype(BF16)
@@ -373,22 +392,25 @@
     offset,
 ):
     xs = lax.axis_size("x")
-    zs = lax.axis_size(Z)
+    zs = lax.axis_size("z")
     step_count, branch_count, depth = hidden.shape
     rows = step_count * branch_count
     scale = LOG2E / math.sqrt(HD)
     tokens = span_tokens.shape[0]
-    span_weight = lax.all_gather(kv_weight, "zh", axis=0, tiled=True)
+    half = kv_weight.shape[0] // 2
+    begin = (lax.axis_index("groups") & 1) * half
+    span_weight = lax.dynamic_slice_in_dim(kv_weight, begin, half, 0)
+    span_weight = lax.all_gather(span_weight, "z", axis=0, tiled=True)
 
     partial = project(hidden.reshape(rows, depth), query_weight, kv_weight, xs)
     partial = exchanged(partial, "x")
     ready = tokens_by_features(span_tokens, span_weight.shape[0])
     partial = add_over_x(partial, zs)
-    partial = exchanged(partial, Z)
+    partial = exchanged(partial, "z")
     own = add_over_z(partial)
-    own = exchanged(own, Z)
+    own = exchanged(own, "z")
     span_partial = dot_f32(ready.reshape(-1, span_weight.shape[0]), span_weight)
-    span_kv = added_at_home(span_partial.reshape(-1, tokens, kv_weight.shape[1]))
+    span_kv = added_at_home(span_partial.reshape(xs, 2, tokens, kv_weight.shape[1]))
     columns = fan(own, rows, xs, HD)
     projected = exchanged(columns, "x")
 
@@ -397,8 +419,8 @@
     values = cache_values.transpose(1, 0, 2)
     partial = attend(projected, keys, values, span_kv, bias, scale)
     folded = fold(exchanged(partial, "x"), zs)
-    ours = finish(exchanged(folded, Z))
-    attention = exchanged(fan(exchanged(ours, Z), rows, xs, 0), "x")
+    ours = finish(exchanged(folded, "z"))
+    attention = exchanged(fan(exchanged(ours, "z"), rows, xs, 0), "x")
     halves = exchanged(close(attention, out_weight, 2), "width")
     attended = (halves[0] + halves[1]).astype(BF16)
     return (span_kv, attended.reshape(step_count, branch_count, attended.shape[1]))
@@ -406,8 +428,8 @@
 
 def solution(mesh):
     finer = Mesh(
-        mesh.devices.reshape(mesh.shape["groups"], 4, 8, 2, mesh.shape["width"]),
-        ("groups", "x", "zh", "zl", "width"),
+        mesh.devices.reshape(mesh.shape["groups"], 4, 16, mesh.shape["width"]),
+        ("groups", "x", "z", "width"),
     )
     placed = (
         P(GROUPS_SEQ, "width"),

time: 214 us -> 208 us (0.972)
  starting transfers between devices: 71.6 us -> 60.4 us
  blocking collectives: 65.9 us -> 68.8 us
    ppermute x11 -> x7, starting transfers between devices: 40.8 us -> 29.3 us  [the longest x2 22.2 us: tokens_by_features(): mine.append(lax.ppermute(both[i], ('x', 'width'), pairs))]
    all_to_all x4, starting transfers between devices: 25.2 us -> 31 us  [exchanged(): return lax.all_to_all(pieces, axis, split_axis=0, concat_axis=0, tiled=True)]
    ppermute x1, starting transfers between devices: 5.52 us -> 0.14 us  [tokens_by_features(): theirs = lax.ppermute(mine, 'width', [(0, 1), (1, 0)])]
    ppermute x11 -> x7, waiting for transfers between devices: 11 us -> 15.8 us  [the longest x2 10.4 us: tokens_by_features(): mine.append(lax.ppermute(both[i], ('x', 'width'), pairs))]
    all_to_all x4, waiting for transfers between devices: 30.6 us -> 27.5 us  [exchanged(): return lax.all_to_all(pieces, axis, split_axis=0, concat_axis=0, tiled=True)]
    all_to_all x5, blocking collectives: 65.9 us -> 68.8 us  [exchanged(): return lax.all_to_all(pieces, axis, split_axis=0, concat_axis=0, tiled=True)]
    pallas_call x8 -> x9, Pallas kernels: 8.48 us -> 8.57 us  [on_chip(): pl.pallas_call(body, out_shape=shapes, scratch_shapes=scratch, compiler_p...]
  transfers between devices with their start and end apart: 17 -> 13, of which waited for: 7 -> 7; matrix products, arithmetic and copies ran while one was open for 3% -> 2% of each run, Pallas kernels for 3% -> 3%
where the time goes in v4:
time: 208 us; the launch traced here: 207 us
  blocking collectives  68.8 us (33%)
  starting transfers between devices  60.4 us (29%)
  waiting for transfers between devices  43.4 us (21%)
  between operations  15.1 us (7%)
  Pallas kernels  11.7 us (6%)
  local copies, waits for them, and re-layouts  3.67 us (2%)
  matrix products  2.32 us (1%)
    all_to_all x5, blocking collectives, exchanged(): return lax.all_to_all(pieces, axis, split_axis=0, concat_axis=0, tiled=True)  68.8 us
    all_to_all x4, starting transfers between devices, exchanged(): return lax.all_to_all(pieces, axis, split_axis=0, concat_axis=0, tiled=True)  31 us
    all_to_all x4, waiting for transfers between devices, exchanged(): return lax.all_to_all(pieces, axis, split_axis=0, concat_axis=0, tiled=True)  27.5 us
    ppermute x2, starting transfers between devices, tokens_by_features(): mine.append(lax.ppermute(both[i], ('x', 'width'), pairs))  22.2 us
    ppermute x2, waiting for transfers between devices, tokens_by_features(): mine.append(lax.ppermute(both[i], ('x', 'width'), pairs))  10.4 us
    pallas_call x9, Pallas kernels, on_chip(): pl.pallas_call(body, out_shape=shapes, scratch_shapes=scratch, compiler_p...  8.57 us
    ppermute x3, waiting for transfers between devices, added_at_home(): received.append(lax.ppermute(partial[mask], 'x', pairs))  5.36 us
  transfers between devices with their start and end apart: 13, of which 7 were waited for; matrix products, arithmetic and copies ran while one was open for 2% of the time, Pallas kernels for 3%

profile of v4, /device:TPU:33, one launch (start us, length us, event | category | flops | bytes accessed | tf_op | source)
XLA Modules:
  0.0 206.9 jit_solution(4513672390180941539)
XLA Ops:
  7.2 0.1 all-gather.2.cloned.1.call-start
  7.2 1.6 constant_dynamic-slice_fusion
  8.8 0.1 all-gather.2.cloned.1.call-update
  8.9 0.0 copy-start.1
  8.9 1.0 copy-done.1
  9.9 0.1 shard_map.104
  10.1 2.8 %collective-permute-start = (bf16[2,32,2048]{2,1,0:T(8,128)(2,1)S(1)}, bf16[2,32,2048]{2,1,0:T(8,128)(2,1)S(1)}, u32[]{:S(2)}, u32[]{:S(2)}) collective-permute-start(bf16[2,32,2048]{2,1,0:T(8,128)(2,1)S(1)} %get-tuple-element.7), channel_id=1, source_target_pairs={{0,128},{128,0},{1,129},{129,1},{2,130},{130,2},{3,131},{131,3},{4... | collective-permute-start | bytes 786440 | tf_op jit(solution)/shard_map/ppermute | solution.py:330
  12.8 3.2 %project.1 = f32[4,64,1152]{2,1,0:T(8,128)} custom-call(bf16[64,256]{1,0:T(8,128)(2,1)} %bitcast.55, bf16[256,4096]{1,0:T(8,128)(2,1)} %query_hbm.1, bf16[256,512]{1,0:T(8,128)(2,1)} %fresh_hbm.1), custom_call_target="tpu_custom_call" | custom-call | tf_op jit(solution)/shard_map/project/pallas_call | solution.py:74
  16.0 4.3 %all-to-all-start = ((f32[4,64,1152]{2,1,0:T(8,128)}), f32[4,64,1152]{2,1,0:T(8,128)S(1)}, u32[]{:S(2)}, u32[]{:S(2)}) async-start(f32[4,64,1152]{2,1,0:T(8,128)} %project.1), calls=%async_computation | async-start | bytes 2359296 | tf_op jit(solution)/shard_map/all_to_all | solution.py:24
  20.3 0.0 collective-permute-done
  20.3 0.1 pad_maximum_fusion.1
  20.4 0.1 reverse_select_fusion.1
  20.5 22.1 %collective-permute-start.1 = (bf16[2,32,2048]{2,1,0:T(8,128)(2,1)S(1)}, bf16[2,32,2048]{2,1,0:T(8,128)(2,1)S(1)}, u32[]{:S(2)}, u32[]{:S(2)}) collective-permute-start(bf16[2,32,2048]{2,1,0:T(8,128)(2,1)S(1)} %get-tuple-element.4), channel_id=1, source_target_pairs={{0,0},{1,64},{32,32},{33,96},{64,1},{65,65},{96,33},{97,97},{2,2},... | collective-permute-start | bytes 786440 | tf_op jit(solution)/shard_map/ppermute | solution.py:348
  42.6 0.1 collective-permute-start.2
  43.5 0.0 copy-done.6
  43.5 7.7 %collective-permute-done.1 = bf16[2,32,2048]{2,1,0:T(8,128)(2,1)S(1)} collective-permute-done((bf16[2,32,2048]{2,1,0:T(8,128)(2,1)S(1)}, bf16[2,32,2048]{2,1,0:T(8,128)(2,1)S(1)}, u32[]{:S(2)}, u32[]{:S(2)}) %collective-permute-start.1) | collective-permute-done | bytes 262176 | tf_op jit(solution)/shard_map/ppermute | solution.py:348
  51.2 2.7 %collective-permute-done.2 = bf16[2,32,2048]{2,1,0:T(8,128)(2,1)S(1)} collective-permute-done((bf16[2,32,2048]{2,1,0:T(8,128)(2,1)S(1)}, bf16[2,32,2048]{2,1,0:T(8,128)(2,1)S(1)}, u32[]{:S(2)}, u32[]{:S(2)}) %collective-permute-start.2) | collective-permute-done | bytes 262176 | tf_op jit(solution)/shard_map/ppermute | solution.py:348
  53.9 0.1 fusion.11
  53.9 0.1 collective-permute-start.3
  54.1 0.0 all-to-all-done.in_ref
  54.1 0.8 shard_map.105
  54.9 12.6 %all-to-all-start.1 = ((f32[16,8,640]{2,1,0:T(8,128)}), f32[16,8,640]{2,1,0:T(8,128)S(1)}, u32[]{:S(2)}, u32[]{:S(2)}) async-start(f32[16,8,640]{2,1,0:T(8,128)} %shard_map.105), calls=%async_computation.1 | async-start | bytes 655360 | tf_op jit(solution)/shard_map/all_to_all | solution.py:24
  67.6 0.1 lt.30
  67.7 0.1 fusion.10
  67.7 0.1 broadcast_compare_fusion
  67.9 0.7 concatenate.3
  68.6 0.0 collective-permute-done.3
  68.6 0.1 pad_maximum_fusion
  68.7 0.2 reverse_select_fusion
  68.9 18.4 %all-to-all-done.1.in_ref = f32[16,8,640]{2,1,0:T(8,128)S(1)} async-done(((f32[16,8,640]{2,1,0:T(8,128)}), f32[16,8,640]{2,1,0:T(8,128)S(1)}, u32[]{:S(2)}, u32[]{:S(2)}) %all-to-all-start.1) | async-done | bytes 327712 | tf_op jit(solution)/shard_map/all_to_all | solution.py:24
  87.3 0.7 shard_map.106
  88.0 10.4 %all-to-all-start.2 = ((bf16[16,8,640]{2,1,0:T(8,128)(2,1)}), bf16[16,8,640]{2,1,0:T(8,128)(2,1)S(1)}, u32[]{:S(2)}, u32[]{:S(2)}) async-start(bf16[16,8,640]{2,1,0:T(8,128)(2,1)} %shard_map.106), calls=%async_computation.2 | async-start | bytes 327680 | tf_op jit(solution)/shard_map/all_to_all | solution.py:24
  98.5 0.0 all-gather.2.cloned.1.call-done
  98.5 0.0 copy-start.5
  98.5 2.3 %fusion = f32[4,2,32,512]{3,2,0,1:T(8,128)S(1)} fusion(bf16[2048,512]{1,0:T(8,128)(2,1)} %all-gather.2.cloned.1.call-done, bf16[4,2,32,2048]{3,2,1,0:T(8,128)(2,1)S(1)} %bitcast.50), kind=kOutput, calls=%fused_computation | convolution fusion | flops 536870912 | bytes 3670016 | tf_op jit(solution)/shard_map/dot_general | solution.py:28
  100.8 0.0 copy-start.3
  100.8 0.0 copy-start.4
  100.9 0.3 collective-permute-start.4
  101.2 0.0 copy-done.5
  101.2 9.2 %all-to-all-done.2.in_ref = bf16[16,8,640]{2,1,0:T(8,128)(2,1)S(1)} async-done(((bf16[16,8,640]{2,1,0:T(8,128)(2,1)}), bf16[16,8,640]{2,1,0:T(8,128)(2,1)S(1)}, u32[]{:S(2)}, u32[]{:S(2)}) %all-to-all-start.2) | async-done | bytes 163872 | tf_op jit(solution)/shard_map/all_to_all | solution.py:24
  110.3 0.9 shard_map.107
  111.2 3.6 %all-to-all-start.3 = ((bf16[4,64,1152]{2,1,0:T(8,128)(2,1)}), bf16[4,64,1152]{2,1,0:T(8,128)(2,1)S(1)}, u32[]{:S(2)}, u32[]{:S(2)}) async-start(bf16[4,64,1152]{2,1,0:T(8,128)(2,1)} %shard_map.107), calls=%async_computation.3 | async-start | bytes 1179648 | tf_op jit(solution)/shard_map/all_to_all | solution.py:24
  114.8 0.0 collective-permute-done.4
  114.9 1.5 collective-permute-start.5
  116.3 2.4 %collective-permute-start.6 = (f32[32,512]{1,0:T(8,128)S(1)}, f32[32,512]{1,0:T(8,128)S(1)}, u32[]{:S(2)}, u32[]{:S(2)}) collective-permute-start(f32[32,512]{1,0:T(8,128)S(1)} %get-tuple-element.10), channel_id=1, source_target_pairs={{0,64},{32,96},{64,0},{96,32},{1,65},{33,97},{65,1},{97,33},{2,66}... | collective-permute-start | bytes 196616 | tf_op jit(solution)/shard_map/ppermute | solution.py:363
  118.8 0.1 collective-permute-start.7
  118.9 0.0 copy-done.3
  118.9 0.1 copy_bitcast_fusion
  119.0 2.1 %collective-permute-done.5 = f32[32,512]{1,0:T(8,128)S(1)} collective-permute-done((f32[32,512]{1,0:T(8,128)S(1)}, f32[32,512]{1,0:T(8,128)S(1)}, u32[]{:S(2)}, u32[]{:S(2)}) %collective-permute-start.5) | collective-permute-done | bytes 65568 | tf_op jit(solution)/shard_map/ppermute | solution.py:363
  121.2 2.3 %collective-permute-done.6 = f32[32,512]{1,0:T(8,128)S(1)} collective-permute-done((f32[32,512]{1,0:T(8,128)S(1)}, f32[32,512]{1,0:T(8,128)S(1)}, u32[]{:S(2)}, u32[]{:S(2)}) %collective-permute-start.6) | collective-permute-done | bytes 65568 | tf_op jit(solution)/shard_map/ppermute | solution.py:363
  123.5 0.9 collective-permute-done.7
  124.4 0.0 copy-start.2
  124.4 0.0 all-to-all-done.3.q_ref
  124.4 4.8 %shard_map.108 = bf16[4,64,1152]{2,1,0:T(8,128)(2,1)S(1)} custom-call(bf16[4,64,1152]{2,1,0:T(8,128)(2,1)S(1)} %all-to-all-done.3.q_ref, bf16[2,1024,128]{2,1,0:T(8,128)(2,1)S(1)} %get-tuple-element.12.keys_ref, bf16[2,1024,128]{2,1,0:T(8,128)(2,1)S(1)} %get-tuple-element.11.values_ref, bf16[32,512]{1,0:T(8,128)(2,1)S(1)} %fusion.7.span_ref, ...), custom_call_target="tpu_custom_call" | custom-call | tf_op jit(solution)/shard_map/pallas_call | solution.py:35
  129.2 0.0 copy-start
  129.2 9.8 %all_to_all.45.in_ref = bf16[4,64,1152]{2,1,0:T(8,128)(2,1)S(1)} all-to-all(bf16[4,64,1152]{2,1,0:T(8,128)(2,1)S(1)} %shard_map.108), channel_id=1, replica_groups=mesh['groups'=2,'x'=4,'z'=16,'width'=2] {'x'}, dimensions={0} | all-to-all | bytes 1179648 | tf_op jit(solution)/shard_map/all_to_all | solution.py:24
  139.1 0.6 shard_map.109
  139.7 20.8 %all_to_all.46.in_ref = bf16[16,8,640]{2,1,0:T(8,128)(2,1)S(1)} all-to-all(bf16[16,8,640]{2,1,0:T(8,128)(2,1)S(1)} %shard_map.109), channel_id=1, replica_groups=mesh['groups'=2,'x'=4,'z'=16,'width'=2] {'z'}, dimensions={0} | all-to-all | bytes 327680 | tf_op jit(solution)/shard_map/all_to_all | solution.py:24
  160.4 0.3 shard_map.110
  160.7 16.4 %all_to_all.47.in_ref = bf16[16,8,512]{2,1,0:T(8,128)(2,1)S(1)} all-to-all(bf16[16,8,512]{2,1,0:T(8,128)(2,1)S(1)} %shard_map.110), channel_id=1, replica_groups=mesh['groups'=2,'x'=4,'z'=16,'width'=2] {'z'}, dimensions={0} | all-to-all | bytes 262144 | tf_op jit(solution)/shard_map/all_to_all | solution.py:24
  177.1 9.4 %all_to_all.48.in_ref = bf16[4,64,1024]{2,1,0:T(8,128)(2,1)S(1)} all-to-all(bf16[4,64,1024]{2,1,0:T(8,128)(2,1)S(1)} %shard_map.111), channel_id=1, replica_groups=mesh['groups'=2,'x'=4,'z'=16,'width'=2] {'x'}, dimensions={0} | all-to-all | bytes 1048576 | tf_op jit(solution)/shard_map/all_to_all | solution.py:24
  186.5 0.5 shard_map.112
  186.9 12.5 %all_to_all.49 = f32[2,64,128]{2,1,0:T(8,128)S(1)} all-to-all(f32[2,64,128]{2,1,0:T(8,128)S(1)} %shard_map.112), channel_id=1, replica_groups=mesh['groups'=2,'x'=4,'z'=16,'width'=2] {'width'}, dimensions={0} | all-to-all | bytes 131072 | tf_op jit(solution)/shard_map/all_to_all | solution.py:24
  199.4 0.6 fusion.8
  (18 shorter events, 0.3 us)
Async XLA Ops:
  7.2 91.3 %all-gather.2.cloned.1.call-start = ((), (), s32[]{:S(2)}) async-start(), calls=%async_computation.9 | async-start | bytes 2228224 | tf_op jit(solution)/shard_map/all_gather | solution.py:403
  8.9 1.0 copy-start.1
  10.1 10.3 %collective-permute-start = (bf16[2,32,2048]{2,1,0:T(8,128)(2,1)S(1)}, bf16[2,32,2048]{2,1,0:T(8,128)(2,1)S(1)}, u32[]{:S(2)}, u32[]{:S(2)}) collective-permute-start(bf16[2,32,2048]{2,1,0:T(8,128)(2,1)S(1)} %get-tuple-element.7), channel_id=1, source_target_pairs={{0,128},{128,0},{1,129},{129,1},{2,130},{130,2},{3,131},{131,3},{4... | collective-permute-start | bytes 786440 | tf_op jit(solution)/shard_map/ppermute | solution.py:330
  16.0 38.1 %all-to-all-start = ((f32[4,64,1152]{2,1,0:T(8,128)}), f32[4,64,1152]{2,1,0:T(8,128)S(1)}, u32[]{:S(2)}, u32[]{:S(2)}) async-start(f32[4,64,1152]{2,1,0:T(8,128)} %project.1), calls=%async_computation | async-start | bytes 2359296 | tf_op jit(solution)/shard_map/all_to_all | solution.py:24
  20.3 23.1 %copy-start.6 = (s32[32]{0:T(128)S(1)}, s32[32]{0:T(128)}, u32[]{:S(2)}) copy-start(s32[32]{0:T(128)} %param.16) | copy-start | bytes 388
  20.5 30.6 %collective-permute-start.1 = (bf16[2,32,2048]{2,1,0:T(8,128)(2,1)S(1)}, bf16[2,32,2048]{2,1,0:T(8,128)(2,1)S(1)}, u32[]{:S(2)}, u32[]{:S(2)}) collective-permute-start(bf16[2,32,2048]{2,1,0:T(8,128)(2,1)S(1)} %get-tuple-element.4), channel_id=1, source_target_pairs={{0,0},{1,64},{32,32},{33,96},{64,1},{65,65},{96,33},{97,97},{2,2},... | collective-permute-start | bytes 786440 | tf_op jit(solution)/shard_map/ppermute | solution.py:348
  42.6 11.2 %collective-permute-start.2 = (bf16[2,32,2048]{2,1,0:T(8,128)(2,1)S(1)}, bf16[2,32,2048]{2,1,0:T(8,128)(2,1)S(1)}, u32[]{:S(2)}, u32[]{:S(2)}) collective-permute-start(bf16[2,32,2048]{2,1,0:T(8,128)(2,1)S(1)} %get-tuple-element.5), channel_id=1, source_target_pairs={{0,32},{1,96},{32,0},{33,64},{64,33},{65,97},{96,1},{97,65},{2,34}... | collective-permute-start | bytes 786440 | tf_op jit(solution)/shard_map/ppermute | solution.py:348
  53.9 14.7 %collective-permute-start.3 = (bf16[2,2,32,2048]{3,2,1,0:T(8,128)(2,1)S(1)}, bf16[2,2,32,2048]{3,2,1,0:T(8,128)(2,1)S(1)}, u32[]{:S(2)}, u32[]{:S(2)}) collective-permute-start(bf16[2,2,32,2048]{3,2,1,0:T(8,128)(2,1)S(1)} %get-tuple-element.3), channel_id=1, source_target_pairs={{0,1},{1,0},{2,3},{3,2},{4,5},{5,4},{6,7},{7,6},{8,9},{9,8},{10,11... | collective-permute-start | bytes 1572872 | tf_op jit(solution)/shard_map/ppermute | solution.py:350
  54.9 32.4 %all-to-all-start.1 = ((f32[16,8,640]{2,1,0:T(8,128)}), f32[16,8,640]{2,1,0:T(8,128)S(1)}, u32[]{:S(2)}, u32[]{:S(2)}) async-start(f32[16,8,640]{2,1,0:T(8,128)} %shard_map.105), calls=%async_computation.1 | async-start | bytes 655360 | tf_op jit(solution)/shard_map/all_to_all | solution.py:24
  88.0 22.3 %all-to-all-start.2 = ((bf16[16,8,640]{2,1,0:T(8,128)(2,1)}), bf16[16,8,640]{2,1,0:T(8,128)(2,1)S(1)}, u32[]{:S(2)}, u32[]{:S(2)}) async-start(bf16[16,8,640]{2,1,0:T(8,128)(2,1)} %shard_map.106), calls=%async_computation.2 | async-start | bytes 327680 | tf_op jit(solution)/shard_map/all_to_all | solution.py:24
  98.5 2.7 %copy-start.5 = (pred[64,1152]{1,0:T(8,128)(4,1)S(1)}, pred[64,1152]{1,0:T(8,128)(4,1)}, u32[]{:S(2)}) copy-start(pred[64,1152]{1,0:T(8,128)(4,1)} %concatenate.3) | copy-start | bytes 221188
  100.8 18.0 %copy-start.3 = (bf16[1024,2,128]{2,1,0:T(2,128)(2,1)S(1)}, bf16[1024,2,128]{2,1,0:T(2,128)(2,1)}, u32[]{:S(2)}) copy-start(bf16[1024,2,128]{2,1,0:T(2,128)(2,1)} %param.14) | copy-start | bytes 1572868
  100.8 18.0 %copy-start.4 = (bf16[1024,2,128]{2,1,0:T(2,128)(2,1)S(1)}, bf16[1024,2,128]{2,1,0:T(2,128)(2,1)}, u32[]{:S(2)}) copy-start(bf16[1024,2,128]{2,1,0:T(2,128)(2,1)} %param.13) | copy-start | bytes 1572868
  100.9 13.9 %collective-permute-start.4 = (f32[4,32,512]{2,1,0:T(8,128)S(1)}, f32[4,32,512]{2,1,0:T(8,128)S(1)}, u32[]{:S(2)}, u32[]{:S(2)}) collective-permute-start(f32[4,32,512]{2,1,0:T(8,128)S(1)} %slice_bitcast_fusion), channel_id=1, source_target_pairs={{0,128},{128,0},{1,129},{129,1},{2,130},{130,2},{3,131},{131,3},{4... | collective-permute-start | bytes 786440 | tf_op jit(solution)/shard_map/ppermute | solution.py:330
  111.2 13.2 %all-to-all-start.3 = ((bf16[4,64,1152]{2,1,0:T(8,128)(2,1)}), bf16[4,64,1152]{2,1,0:T(8,128)(2,1)S(1)}, u32[]{:S(2)}, u32[]{:S(2)}) async-start(bf16[4,64,1152]{2,1,0:T(8,128)(2,1)} %shard_map.107), calls=%async_computation.3 | async-start | bytes 1179648 | tf_op jit(solution)/shard_map/all_to_all | solution.py:24
  114.9 6.3 %collective-permute-start.5 = (f32[32,512]{1,0:T(8,128)S(1)}, f32[32,512]{1,0:T(8,128)S(1)}, u32[]{:S(2)}, u32[]{:S(2)}) collective-permute-start(f32[32,512]{1,0:T(8,128)S(1)} %get-tuple-element.8), channel_id=1, source_target_pairs={{0,32},{32,0},{64,96},{96,64},{1,33},{33,1},{65,97},{97,65},{2,34}... | collective-permute-start | bytes 196616 | tf_op jit(solution)/shard_map/ppermute | solution.py:363
  116.3 7.2 %collective-permute-start.6 = (f32[32,512]{1,0:T(8,128)S(1)}, f32[32,512]{1,0:T(8,128)S(1)}, u32[]{:S(2)}, u32[]{:S(2)}) collective-permute-start(f32[32,512]{1,0:T(8,128)S(1)} %get-tuple-element.10), channel_id=1, source_target_pairs={{0,64},{32,96},{64,0},{96,32},{1,65},{33,97},{65,1},{97,33},{2,66}... | collective-permute-start | bytes 196616 | tf_op jit(solution)/shard_map/ppermute | solution.py:363
  118.8 5.6 %collective-permute-start.7 = (f32[32,512]{1,0:T(8,128)S(1)}, f32[32,512]{1,0:T(8,128)S(1)}, u32[]{:S(2)}, u32[]{:S(2)}) collective-permute-start(f32[32,512]{1,0:T(8,128)S(1)} %get-tuple-element.9), channel_id=1, source_target_pairs={{0,96},{32,64},{64,32},{96,0},{1,97},{33,65},{65,33},{97,1},{2,98}... | collective-permute-start | bytes 196616 | tf_op jit(solution)/shard_map/ppermute | solution.py:363
  124.4 15.2 %copy-start.2 = (bf16[32,512]{1,0:T(8,128)(2,1)}, bf16[32,512]{1,0:T(8,128)(2,1)S(1)}, u32[]{:S(2)}) copy-start(bf16[32,512]{1,0:T(8,128)(2,1)S(1)} %fusion.7.span_ref) | copy-start | bytes 98308
  129.2 57.2 %copy-start = (bf16[4096,256]{1,0:T(8,128)(2,1)S(1)}, bf16[4096,256]{1,0:T(8,128)(2,1)}, u32[]{:S(2)}) copy-start(bf16[4096,256]{1,0:T(8,128)(2,1)} %weight_ref.1) | copy-start | bytes 6291460
Sparse Core Ops, SparseCore 0:
  9.8 86.7 all-gather.1

commit v5 on v4

--- a/solution.py
+++ b/solution.py
@@ -28,13 +28,26 @@
     return jnp.dot(a, b, preferred_element_type=F32)
 
 
-def on_chip(body, outs, *operands, scratch=()):
+def on_chip(body, outs, *operands, scratch=(), place=None):
     shapes = jax.tree.map(lambda o: pltpu.VMEM(o.shape, o.dtype), outs)
     placed = [pltpu.with_memory_space_constraint(x, pltpu.VMEM) for x in operands]
+    specs = [pl.BlockSpec(memory_space=pltpu.VMEM)] * len(placed)
+    if place is not None:
+        placed.insert(0, place)
+        specs.insert(0, pl.BlockSpec(memory_space=pltpu.SMEM))
     params = pltpu.CompilerParams(vmem_limit_bytes=16 * 2**20)
     return pl.pallas_call(
-        body, out_shape=shapes, scratch_shapes=scratch, compiler_params=params
+        body, in_specs=specs, out_shape=shapes, scratch_shapes=scratch, compiler_params=params
     )(*placed)
+
+
+def exchanged_over_x(pieces):
+    count = lax.axis_size("x")
+    received = [pieces[0]]
+    for mask in range(1, count):
+        pairs = [(i, i ^ mask) for i in range(count)]
+        received.append(lax.ppermute(pieces[mask], "x", pairs))
+    return received
 
 
 def array(shape, dtype):
@@ -45,56 +58,59 @@
     return places // (rows // TILE)
 
 
-def project(states, query_weight, kv_weight, pieces):
-    rows, _ = states.shape
+def project(place, states, query_weight, kv_weight, pieces):
+    rows, depth = states.shape
     columns = query_weight.shape[1] // pieces
     extra = kv_weight.shape[1] // pieces
 
-    def body(states_hbm, query_hbm, fresh_hbm, out_ref, states_ref, query_ref, fresh_ref, sems):
-        copies = [
-            pltpu.make_async_copy(states_hbm, states_ref, sems.at[0]),
-            pltpu.make_async_copy(fresh_hbm, fresh_ref, sems.at[1]),
-        ]
-        for c in range(pieces):
-            cut = slice(c * columns, (c + 1) * columns)
-            copies.append(
-                pltpu.make_async_copy(query_hbm.at[:, cut], query_ref.at[:, cut], sems.at[2 + c])
-            )
+    def body(place_ref, states_hbm, query_hbm, fresh_hbm, *rest):
+        outs = rest[:pieces]
+        states_ref, query_ref, fresh_ref, sems = rest[pieces:]
+        x = place_ref[0]
+        copies = [pltpu.make_async_copy(states_hbm, states_ref, sems.at[2 * pieces])]
+        for m in range(pieces):
+            c = x ^ m
+            more = fresh_hbm.at[:, pl.ds(pl.multiple_of(c * extra, extra), extra)]
+            most = query_hbm.at[:, pl.ds(pl.multiple_of(c * columns, columns), columns)]
+            copies.append(pltpu.make_async_copy(more, fresh_ref.at[m], sems.at[2 * m]))
+            copies.append(pltpu.make_async_copy(most, query_ref.at[m], sems.at[2 * m + 1]))
         for copy in copies:
             copy.start()
         copies[0].wait()
-        copies[1].wait()
         states = states_ref[...]
-        for c in range(pieces):
-            copies[2 + c].wait()
-            out_ref[c, :, :columns] = dot_f32(states, query_ref[:, c * columns : (c + 1) * columns])
-            out_ref[c, :, columns:] = dot_f32(states, fresh_ref[:, c * extra : (c + 1) * extra])
-
-    anywhere = pl.BlockSpec(memory_space=pltpu.HBM)
+        for m in range(pieces):
+            copies[1 + 2 * m].wait()
+            outs[m][:, columns:] = dot_f32(states, fresh_ref[m])
+            copies[2 + 2 * m].wait()
+            outs[m][:, :columns] = dot_f32(states, query_ref[m])
+
+    hbm = [pltpu.with_memory_space_constraint(x, pltpu.HBM) for x in (states, query_weight, kv_weight)]
     return pl.pallas_call(
         body,
-        in_specs=[anywhere, anywhere, anywhere],
-        out_shape=pltpu.VMEM((pieces, rows, columns + extra), F32),
+        in_specs=[pl.BlockSpec(memory_space=pltpu.SMEM)]
+        + [pl.BlockSpec(memory_space=pltpu.HBM)] * len(hbm),
+        out_shape=[pltpu.VMEM((rows, columns + extra), F32)] * pieces,
         scratch_shapes=[
             pltpu.VMEM(states.shape, BF16),
-            pltpu.VMEM(query_weight.shape, BF16),
-            pltpu.VMEM(kv_weight.shape, BF16),
-            pltpu.SemaphoreType.DMA((2 + pieces,)),
+            pltpu.VMEM((pieces, depth, columns), BF16),
+            pltpu.VMEM((pieces, depth, extra), BF16),
+            pltpu.SemaphoreType.DMA((2 * pieces + 1,)),
         ],
         compiler_params=pltpu.CompilerParams(vmem_limit_bytes=16 * 2**20),
         name="project",
-    )(*[pltpu.with_memory_space_constraint(x, pltpu.HBM) for x in (states, query_weight, kv_weight)])
+    )(place, *hbm)
 
 
 def add_over_x(received, places):
-    sources, rows, width = received.shape
+    rows, width = received[0].shape
     parts = parts_of(rows, places)
     columns = (width - HD) // parts
 
-    def body(in_ref, out_ref):
-        total = in_ref[0]
-        for s in range(1, sources):
-            total = total + in_ref[s]
+    def body(*refs):
+        out_ref = refs[-1]
+        total = refs[0][...]
+        for ref in refs[1:-1]:
+            total = total + ref[...]
         for part in range(parts):
             for group in range(rows // TILE):
                 place = part * (rows // TILE) + group
@@ -102,7 +118,7 @@
                 out_ref[place, :, :columns] = some[:, part * columns : (part + 1) * columns]
                 out_ref[place, :, columns:] = some[:, width - HD :]
 
-    return on_chip(body, array((places, TILE, columns + HD), F32), received)
+    return on_chip(body, array((places, TILE, columns + HD), F32), *received)
 
 
 def add_over_z(received):
@@ -117,7 +133,7 @@
     return on_chip(body, array(received.shape, BF16), received)
 
 
-def fan(received, rows, copies, tail):
+def fan(received, rows, tail):
     places, _, width = received.shape
     parts = parts_of(rows, places)
     columns = width - tail
@@ -131,12 +147,11 @@
                     [in_ref[place].astype(F32), in_ref[place + 1].astype(F32)], axis=0
                 ).astype(BF16)
                 at = slice(2 * pair * TILE, 2 * (pair + 1) * TILE)
-                for c in range(copies):
-                    out_ref[c, at, part * columns : (part + 1) * columns] = some[:, :columns]
-                    if tail and part == 0:
-                        out_ref[c, at, parts * columns :] = some[:, columns:]
-
-    return on_chip(body, array((copies, rows, whole), BF16), received)
+                out_ref[at, part * columns : (part + 1) * columns] = some[:, :columns]
+                if tail and part == 0:
+                    out_ref[at, parts * columns :] = some[:, columns:]
+
+    return on_chip(body, array((rows, whole), BF16), received)
 
 
 def three_parts(x):
@@ -162,9 +177,9 @@
     return stats
 
 
-def heads_together(ref, piece, first, count):
+def heads_together(ref, first, count):
     return jnp.concatenate(
-        [ref[piece, :, (first + i) * HD : (first + i + 1) * HD] for i in range(count)], axis=0
+        [ref[:, (first + i) * HD : (first + i + 1) * HD] for i in range(count)], axis=0
     )
 
 
@@ -172,8 +187,9 @@
     return lax.dot_general(q, keys, (((1,), (1,)), ((), ())), preferred_element_type=F32)
 
 
-def attend(projected, keys, values, span_kv, bias, scale):
-    pieces, rows, width = projected.shape
+def attend(place, projected, keys, values, span_kv, bias, scale):
+    pieces = len(projected)
+    rows, width = projected[0].shape
     local_heads, slots, _ = keys.shape
     span = span_kv.shape[0]
     per_head = pieces // local_heads
@@ -183,46 +199,58 @@
     at = heads * HD
     blank_rows = total_keys - slots - rows - span
 
-    def body(q_ref, keys_ref, values_ref, span_ref, bias_ref, out_ref, k_ref, v_ref):
+    def body(place_ref, *refs):
+        q_refs = refs[:pieces]
+        keys_ref, values_ref, span_ref, bias_ref = refs[pieces : pieces + 4]
+        outs = refs[pieces + 4 : 2 * pieces + 4]
+        k_ref, v_ref = refs[2 * pieces + 4 :]
+        x = place_ref[0]
+        odd = (x & 1) == 1
         bias = bias_ref[...]
         lane = lax.broadcasted_iota(jnp.int32, (rows, HD), 1)
         blank = [jnp.zeros((blank_rows, HD), BF16)] if blank_rows else []
         for h in range(local_heads):
-            k_ref[h, :slots, :] = keys_ref[h]
-            v_ref[h, :slots, :] = values_ref[h]
+            head = (x >> 1) ^ h
+            k_ref[h, :slots, :] = keys_ref[head]
+            v_ref[h, :slots, :] = values_ref[head]
+            first = q_refs[h * per_head][:, at:].astype(F32)
+            second = q_refs[h * per_head + 1][:, at:].astype(F32)
+            fresh = (jnp.where(odd, second, first), jnp.where(odd, first, second))
             for side, into in enumerate((k_ref, v_ref)):
-                begin = (2 * h + side) * HD
-                more = [span_ref[:, begin : begin + HD], q_ref[h * per_head + side, :, at:]]
+                begin = pl.multiple_of((2 * head + side) * HD, HD)
+                more = [span_ref[:, pl.ds(begin, HD)], fresh[side].astype(BF16)]
                 into[h, slots:, :] = jnp.concatenate(more + blank, axis=0)
-        for h in range(local_heads):
-            for piece in range(h * per_head, (h + 1) * per_head):
-                peaks = jnp.zeros((rows, HD), F32)
-                totals = jnp.zeros((rows, HD), F32)
-                for first in range(0, heads, per_dot):
-                    q = heads_together(q_ref, piece, first, per_dot)
-                    scores = score(q, k_ref[h])
-                    scores = scores.reshape(per_dot, rows, total_keys) * scale + bias[None]
-                    highest = jnp.max(scores, axis=-1, keepdims=True)
-                    weights = jnp.exp2(scores - highest)
-                    total = jnp.sum(weights, axis=-1, keepdims=True)
-                    weights = weights.reshape(per_dot * rows, total_keys).astype(BF16)
-                    summed = dot_f32(weights, v_ref[h])
-                    for i in range(per_dot):
-                        head = first + i
-                        out_ref[piece, :, head * HD : (head + 1) * HD] = summed[
-                            i * rows : (i + 1) * rows
-                        ].astype(BF16)
-                        peaks = jnp.where(lane == head, highest[i], peaks)
-                        totals = jnp.where(lane == head, total[i], totals)
-                out_ref[piece, :, at:] = split_stats(peaks, totals, heads).astype(BF16)
-
-    out = array((pieces, rows, width), BF16)
+        for piece in range(pieces):
+            h = piece // per_head
+            peaks = jnp.zeros((rows, HD), F32)
+            totals = jnp.zeros((rows, HD), F32)
+            for first in range(0, heads, per_dot):
+                q = heads_together(q_refs[piece], first, per_dot)
+                scores = score(q, k_ref[h])
+                scores = scores.reshape(per_dot, rows, total_keys) * scale + bias[None]
+                highest = jnp.max(scores, axis=-1, keepdims=True)
+                weights = jnp.exp2(scores - highest)
+                total = jnp.sum(weights, axis=-1, keepdims=True)
+                weights = weights.reshape(per_dot * rows, total_keys).astype(BF16)
+                summed = dot_f32(weights, v_ref[h])
+                for i in range(per_dot):
+                    head = first + i
+                    outs[piece][:, head * HD : (head + 1) * HD] = summed[
+                        i * rows : (i + 1) * rows
+                    ].astype(BF16)
+                    peaks = jnp.where(lane == head, highest[i], peaks)
+                    totals = jnp.where(lane == head, total[i], totals)
+            outs[piece][:, at:] = split_stats(peaks, totals, heads).astype(BF16)
+
+    out = [array((rows, width), BF16)] * pieces
     scratch = [pltpu.VMEM((local_heads, total_keys, HD), BF16)] * 2
-    return on_chip(body, out, projected, keys, values, span_kv, bias, scratch=scratch)
+    operands = (*projected, keys, values, span_kv, bias)
+    return on_chip(body, out, *operands, scratch=scratch, place=place)
 
 
 def fold(received, places):
-    sources, rows, width = received.shape
+    sources = len(received)
+    rows, width = received[0].shape
     heads = (width - HD) // HD
     at = heads * HD
     parts = parts_of(rows, places)
@@ -230,9 +258,10 @@
     groups = rows // TILE
     columns = some_heads * HD
 
-    def body(in_ref, out_ref):
+    def body(*refs):
+        out_ref = refs[-1]
         lane = lax.broadcasted_iota(jnp.int32, (rows, HD), 1)
-        stats = [joined_stats(in_ref[s, :, at:].astype(F32), heads) for s in range(sources)]
+        stats = [joined_stats(refs[s][:, at:].astype(F32), heads) for s in range(sources)]
         highest = stats[0][0]
         for s in range(1, sources):
             highest = jnp.maximum(highest, stats[s][0])
@@ -251,17 +280,17 @@
             for i in range(some_heads):
                 head = part * some_heads + i
                 cut = slice(head * HD, (head + 1) * HD)
-                summed = in_ref[0, :, cut].astype(F32) * keeps[0][:, head : head + 1]
+                summed = refs[0][:, cut].astype(F32) * keeps[0][:, head : head + 1]
                 for s in range(1, sources):
                     keep = keeps[s][:, head : head + 1]
-                    summed = summed + in_ref[s, :, cut].astype(F32) * keep
+                    summed = summed + refs[s][:, cut].astype(F32) * keep
                 put(part, slice(i * HD, (i + 1) * HD), summed)
             turn = (HD - part * some_heads) % HD
             peaks = pltpu.roll(highest, turn, 1) if turn else highest
             totals = pltpu.roll(total, turn, 1) if turn else total
             put(part, slice(columns, columns + HD), split_stats(peaks, totals, some_heads))
 
-    return on_chip(body, array((places, TILE, columns + HD), BF16), received)
+    return on_chip(body, array((places, TILE, columns + HD), BF16), *received)
 
 
 def finish(received):
@@ -291,18 +320,25 @@
     return on_chip(body, array((sources, group, at), BF16), received)
 
 
-def close(attention, out_weight, halves):
-    pieces, rows, depth = attention.shape
-    columns = out_weight.shape[1] // halves
-
-    def body(in_ref, weight_ref, out_ref):
-        total = dot_f32(in_ref[0], weight_ref[:depth, :])
-        for c in range(1, pieces):
-            total = total + dot_f32(in_ref[c], weight_ref[c * depth : (c + 1) * depth, :])
-        for w in range(halves):
-            out_ref[w] = total[:, w * columns : (w + 1) * columns]
-
-    return on_chip(body, array((halves, rows, columns), F32), attention, out_weight)
+def close(place, attention, out_weight):
+    pieces = len(attention)
+    rows, depth = attention[0].shape
+    columns = out_weight.shape[1] // 2
+
+    def body(place_ref, *refs):
+        weight_ref, keep_ref, send_ref = refs[pieces:]
+        total = None
+        for m in range(pieces):
+            begin = pl.multiple_of((place_ref[0] ^ m) * depth, depth)
+            more = dot_f32(refs[m][...], weight_ref[pl.ds(begin, depth), :])
+            total = more if total is None else total + more
+        upper = place_ref[1] == 1
+        left, right = total[:, :columns], total[:, columns:]
+        keep_ref[...] = jnp.where(upper, right, left)
+        send_ref[...] = jnp.where(upper, left, right)
+
+    outs = [array((rows, columns), F32)] * 2
+    return on_chip(body, outs, *attention, out_weight, place=place)
 
 
 def swapped_if(flag, x, axis):
@@ -402,8 +438,10 @@
     span_weight = lax.dynamic_slice_in_dim(kv_weight, begin, half, 0)
     span_weight = lax.all_gather(span_weight, "z", axis=0, tiled=True)
 
-    partial = project(hidden.reshape(rows, depth), query_weight, kv_weight, xs)
-    partial = exchanged(partial, "x")
+    place = jnp.stack([lax.axis_index("x"), lax.axis_index("width")])
+
+    partial = project(place, hidden.reshape(rows, depth), query_weight, kv_weight, xs)
+    partial = exchanged_over_x(partial)
     ready = tokens_by_features(span_tokens, span_weight.shape[0])
     partial = add_over_x(partial, zs)
     partial = exchanged(partial, "z")
@@ -411,18 +449,19 @@
     own = exchanged(own, "z")
     span_partial = dot_f32(ready.reshape(-1, span_weight.shape[0]), span_weight)
     span_kv = added_at_home(span_partial.reshape(xs, 2, tokens, kv_weight.shape[1]))
-    columns = fan(own, rows, xs, HD)
-    projected = exchanged(columns, "x")
+    columns = fan(own, rows, HD)
+    projected = exchanged_over_x([columns] * xs)
 
     bias = biases(lengths, offset, step_count, cache_keys.shape[0], tokens)
     keys = cache_keys.transpose(1, 0, 2)
     values = cache_values.transpose(1, 0, 2)
-    partial = attend(projected, keys, values, span_kv, bias, scale)
-    folded = fold(exchanged(partial, "x"), zs)
+    partial = attend(place, projected, keys, values, span_kv, bias, scale)
+    folded = fold(exchanged_over_x(partial), zs)
     ours = finish(exchanged(folded, "z"))
-    attention = exchanged(fan(exchanged(ours, "z"), rows, xs, 0), "x")
-    halves = exchanged(close(attention, out_weight, 2), "width")
-    attended = (halves[0] + halves[1]).astype(BF16)
+    columns = fan(exchanged(ours, "z"), rows, 0)
+    attention = exchanged_over_x([columns] * xs)
+    keep, send = close(place, attention, out_weight)
+    attended = (keep + lax.ppermute(send, "width", [(0, 1), (1, 0)])).astype(BF16)
     return (span_kv, attended.reshape(step_count, branch_count, attended.shape[1]))
 
 

time: 208 us -> 216 us (1.038)
  blocking collectives: 68.8 us -> 34.7 us
  starting transfers between devices: 60.4 us -> 82.4 us
  waiting for transfers between devices: 43.4 us -> 61.5 us
    ppermute x0 -> x13, starting transfers between devices: none -> 34.5 us  [the longest x1 18 us: local(): lax.ppermute(send, 'width', [(0, 1), (1, 0)])]
    all_to_all x5 -> x2, blocking collectives: 68.8 us -> 34.7 us  [exchanged(): return lax.all_to_all(pieces, axis, split_axis=0, concat_axis=0, tiled=True)]
    all_gather x1, waiting for transfers between devices: 0.02 us -> 28.5 us  [local(): span_weight = lax.all_gather(span_weight, 'z', axis=0, tiled=True)]
    all_to_all x4 -> x2, waiting for transfers between devices: 27.5 us -> 7.5 us  [exchanged(): return lax.all_to_all(pieces, axis, split_axis=0, concat_axis=0, tiled=True)]
    ppermute x0 -> x13, waiting for transfers between devices: none -> 15.1 us  [the longest x12 14.2 us: exchanged_over_x(): received.append(lax.ppermute(pieces[mask], 'x', pairs))]
    all_to_all x4 -> x2, starting transfers between devices: 31 us -> 20.2 us  [exchanged(): return lax.all_to_all(pieces, axis, split_axis=0, concat_axis=0, tiled=True)]
    ppermute x3, waiting for transfers between devices: 5.36 us -> 0.01 us  [added_at_home(): received.append(lax.ppermute(partial[mask], 'x', pairs))]
  transfers between devices with their start and end apart: 13 -> 24, of which waited for: 7 -> 13; matrix products, arithmetic and copies ran while one was open for 2% -> 3% of each run, Pallas kernels for 3% -> 2%
where the time goes in v5:
time: 216 us; the launch traced here: 215 us
  starting transfers between devices  82.4 us (38%)
  waiting for transfers between devices  61.5 us (28%)
  blocking collectives  34.7 us (16%)
  between operations  15.1 us (7%)
  Pallas kernels  11.8 us (5%)
  local copies, waits for them, and re-layouts  3.75 us (2%)
  other arithmetic  3.56 us (2%)
  matrix products  2.31 us (1%)
    all_to_all x2, blocking collectives, exchanged(): return lax.all_to_all(pieces, axis, split_axis=0, concat_axis=0, tiled=True)  34.7 us
    all_gather x1, waiting for transfers between devices, local(): span_weight = lax.all_gather(span_weight, 'z', axis=0, tiled=True)  28.5 us
    all_to_all x2, starting transfers between devices, exchanged(): return lax.all_to_all(pieces, axis, split_axis=0, concat_axis=0, tiled=True)  20.2 us
    ppermute x2, starting transfers between devices, tokens_by_features(): mine.append(lax.ppermute(both[i], ('x', 'width'), pairs))  20.1 us
    ppermute x1, starting transfers between devices, local(): lax.ppermute(send, 'width', [(0, 1), (1, 0)])  18 us
    ppermute x12, starting transfers between devices, exchanged_over_x(): received.append(lax.ppermute(pieces[mask], 'x', pairs))  16.5 us
    ppermute x12, waiting for transfers between devices, exchanged_over_x(): received.append(lax.ppermute(pieces[mask], 'x', pairs))  14.2 us
    ppermute x2, waiting for transfers between devices, tokens_by_features(): mine.append(lax.ppermute(both[i], ('x', 'width'), pairs))  10.4 us
  transfers between devices with their start and end apart: 24, of which 13 were waited for; matrix products, arithmetic and copies ran while one was open for 3% of the time, Pallas kernels for 2%

profile of v5, /device:TPU:33, one launch (start us, length us, event | category | flops | bytes accessed | tf_op | source)
XLA Modules:
  0.0 215.2 jit_solution(8227958973654704555)
XLA Ops:
  7.2 0.1 all-gather.2.cloned.1.call-start
  7.2 1.6 constant_dynamic-slice_fusion
  8.8 0.1 all-gather.2.cloned.1.call-update
  8.9 0.0 copy-start.1
  8.9 1.0 copy-done.1
  9.9 0.1 shard_map.104
  10.1 2.8 %collective-permute-start = (bf16[2,32,2048]{2,1,0:T(8,128)(2,1)S(1)}, bf16[2,32,2048]{2,1,0:T(8,128)(2,1)S(1)}, u32[]{:S(2)}, u32[]{:S(2)}) collective-permute-start(bf16[2,32,2048]{2,1,0:T(8,128)(2,1)S(1)} %get-tuple-element.27), channel_id=1, source_target_pairs={{0,128},{128,0},{1,129},{129,1},{2,130},{130,2},{3,131},{131,3},{4... | collective-permute-start | bytes 786440 | tf_op jit(solution)/shard_map/ppermute | solution.py:366
  12.8 0.1 pad_add_fusion.place_ref
  12.9 3.0 %project.1 = (f32[64,1152]{1,0:T(8,128)S(1)}, f32[64,1152]{1,0:T(8,128)S(1)}, f32[64,1152]{1,0:T(8,128)S(1)}, f32[64,1152]{1,0:T(8,128)S(1)}) custom-call(s32[2]{0:T(128)S(1)} %pad_add_fusion.place_ref, bf16[64,256]{1,0:T(8,128)(2,1)} %bitcast.56, bf16[256,4096]{1,0:T(8,128)(2,1)} %query_hbm.1, bf16[256,512]{1,0:T(8,128)(2,1)} %fresh_hbm.1), custom_call_target="tpu_custom_call" | custom-call | tf_op jit(solution)/shard_map/project/pallas_call | solution.py:88
  15.9 3.0 %collective-permute-start.10 = (f32[64,1152]{1,0:T(8,128)S(1)}, f32[64,1152]{1,0:T(8,128)S(1)}, u32[]{:S(2)}, u32[]{:S(2)}) collective-permute-start(f32[64,1152]{1,0:T(8,128)S(1)} %get-tuple-element.15), channel_id=1, source_target_pairs={{0,96},{32,64},{64,32},{96,0},{1,97},{33,65},{65,33},{97,1},{2,98}... | collective-permute-start | bytes 884744 | tf_op jit(solution)/shard_map/ppermute | solution.py:49
  19.0 1.3 collective-permute-start.9
  20.9 0.1 pad_maximum_fusion.1
  21.0 0.1 reverse_select_fusion.1
  21.2 19.8 %collective-permute-start.1 = (bf16[2,32,2048]{2,1,0:T(8,128)(2,1)S(1)}, bf16[2,32,2048]{2,1,0:T(8,128)(2,1)S(1)}, u32[]{:S(2)}, u32[]{:S(2)}) collective-permute-start(bf16[2,32,2048]{2,1,0:T(8,128)(2,1)S(1)} %get-tuple-element.24), channel_id=1, source_target_pairs={{0,0},{1,64},{32,32},{33,96},{64,1},{65,65},{96,33},{97,97},{2,2},... | collective-permute-start | bytes 786440 | tf_op jit(solution)/shard_map/ppermute | solution.py:384
  41.0 0.3 collective-permute-start.2
  41.3 0.1 lt.30
  41.4 7.3 %collective-permute-done.1 = bf16[2,32,2048]{2,1,0:T(8,128)(2,1)S(1)} collective-permute-done((bf16[2,32,2048]{2,1,0:T(8,128)(2,1)S(1)}, bf16[2,32,2048]{2,1,0:T(8,128)(2,1)S(1)}, u32[]{:S(2)}, u32[]{:S(2)}) %collective-permute-start.1) | collective-permute-done | bytes 262176 | tf_op jit(solution)/shard_map/ppermute | solution.py:384
  48.6 3.1 %collective-permute-done.2 = bf16[2,32,2048]{2,1,0:T(8,128)(2,1)S(1)} collective-permute-done((bf16[2,32,2048]{2,1,0:T(8,128)(2,1)S(1)}, bf16[2,32,2048]{2,1,0:T(8,128)(2,1)S(1)}, u32[]{:S(2)}, u32[]{:S(2)}) %collective-permute-start.2) | collective-permute-done | bytes 262176 | tf_op jit(solution)/shard_map/ppermute | solution.py:384
  51.7 0.7 copy-done.5
  52.4 1.0 fusion.10
  53.5 0.1 collective-permute-start.3
  53.6 0.1 fusion.9
  53.7 0.1 broadcast_compare_fusion
  53.8 0.1 concatenate.3
  54.0 0.8 shard_map.105
  54.8 12.3 %all-to-all-start = ((f32[16,8,640]{2,1,0:T(8,128)}), f32[16,8,640]{2,1,0:T(8,128)S(1)}, u32[]{:S(2)}, u32[]{:S(2)}) async-start(f32[16,8,640]{2,1,0:T(8,128)} %shard_map.105), calls=%async_computation | async-start | bytes 655360 | tf_op jit(solution)/shard_map/all_to_all | solution.py:24
  67.1 1.1 pad_maximum_fusion
  68.2 0.2 reverse_select_fusion
  68.4 28.5 %all-gather.2.cloned.1.call-done = bf16[2048,512]{1,0:T(8,128)(2,1)} async-done(((bf16[128,512]{1,0:T(8,128)(2,1)}), bf16[2048,512]{1,0:T(8,128)(2,1)}) %all-gather.2.cloned.1.call-update) | async-done | bytes 2097168 | tf_op jit(solution)/shard_map/all_gather | solution.py:439
  97.0 2.3 %fusion = f32[4,2,32,512]{3,2,0,1:T(8,128)S(1)} fusion(bf16[2048,512]{1,0:T(8,128)(2,1)} %all-gather.2.cloned.1.call-done, bf16[4,2,32,2048]{3,2,1,0:T(8,128)(2,1)S(1)} %bitcast.52), kind=kOutput, calls=%fused_computation | convolution fusion | flops 536870912 | bytes 3670016 | tf_op jit(solution)/shard_map/dot_general | solution.py:28
  99.3 0.0 copy-start.3
  99.3 0.5 collective-permute-start.4
  99.9 0.7 shard_map.106
  100.6 7.9 %all-to-all-start.1 = ((bf16[16,8,640]{2,1,0:T(8,128)(2,1)}), bf16[16,8,640]{2,1,0:T(8,128)(2,1)S(1)}, u32[]{:S(2)}, u32[]{:S(2)}) async-start(bf16[16,8,640]{2,1,0:T(8,128)(2,1)} %shard_map.106), calls=%async_computation.1 | async-start | bytes 327680 | tf_op jit(solution)/shard_map/all_to_all | solution.py:24
  108.6 1.5 collective-permute-start.5
  110.0 2.7 %collective-permute-start.6 = (f32[32,512]{1,0:T(8,128)S(1)}, f32[32,512]{1,0:T(8,128)S(1)}, u32[]{:S(2)}, u32[]{:S(2)}) collective-permute-start(f32[32,512]{1,0:T(8,128)S(1)} %get-tuple-element.30), channel_id=1, source_target_pairs={{0,64},{32,96},{64,0},{96,32},{1,65},{33,97},{65,1},{97,33},{2,66}... | collective-permute-start | bytes 196616 | tf_op jit(solution)/shard_map/ppermute | solution.py:399
  112.8 0.1 copy_bitcast_fusion
  112.9 7.5 %all-to-all-done.1.in_ref = bf16[16,8,640]{2,1,0:T(8,128)(2,1)S(1)} async-done(((bf16[16,8,640]{2,1,0:T(8,128)(2,1)}), bf16[16,8,640]{2,1,0:T(8,128)(2,1)S(1)}, u32[]{:S(2)}, u32[]{:S(2)}) %all-to-all-start.1) | async-done | bytes 163872 | tf_op jit(solution)/shard_map/all_to_all | solution.py:24
  120.4 1.5 collective-permute-start.11
  121.9 2.7 %collective-permute-start.12 = (bf16[64,1152]{1,0:T(8,128)(2,1)S(1)}, bf16[64,1152]{1,0:T(8,128)(2,1)S(1)}, u32[]{:S(2)}, u32[]{:S(2)}) collective-permute-start(bf16[64,1152]{1,0:T(8,128)(2,1)S(1)} %shard_map.107.refs_0_), channel_id=1, source_target_pairs={{0,64},{32,96},{64,0},{96,32},{1,65},{33,97},{65,1},{97,33},{2,66}... | collective-permute-start | bytes 442376 | tf_op jit(solution)/shard_map/ppermute | solution.py:49
  124.6 0.0 copy-start.2
  124.7 0.9 collective-permute-done.11.refs_1_
  125.5 3.5 %collective-permute-done.12.refs_2_ = bf16[64,1152]{1,0:T(8,128)(2,1)S(1)} collective-permute-done((bf16[64,1152]{1,0:T(8,128)(2,1)S(1)}, bf16[64,1152]{1,0:T(8,128)(2,1)S(1)}, u32[]{:S(2)}, u32[]{:S(2)}) %collective-permute-start.12) | collective-permute-done | bytes 147488 | tf_op jit(solution)/shard_map/ppermute | solution.py:49
  129.0 1.5 collective-permute-done.13.refs_3_
  130.5 5.4 %shard_map.108 = (bf16[64,1152]{1,0:T(8,128)(2,1)S(1)}, bf16[64,1152]{1,0:T(8,128)(2,1)S(1)}, bf16[64,1152]{1,0:T(8,128)(2,1)S(1)}, bf16[64,1152]{1,0:T(8,128)(2,1)S(1)}) custom-call(s32[2]{0:T(128)S(1)} %pad_add_fusion.place_ref, bf16[64,1152]{1,0:T(8,128)(2,1)S(1)} %shard_map.107.refs_0_, bf16[64,1152]{1,0:T(8,128)(2,1)S(1)} %collective-permute-done.11.refs_1_, ...), custom_call_target="tpu_custom_call" | custom-call | tf_op jit(solution)/shard_map/pallas_call | solution.py:39
  135.9 0.1 collective-permute-start.14
  136.1 1.9 collective-permute-start.15
  137.9 2.0 collective-permute-start.16
  139.9 0.5 collective-permute-done.14.refs_1_
  140.4 2.1 collective-permute-done.15.refs_2_
  142.5 1.7 collective-permute-done.16.refs_3_
  144.2 0.6 shard_map.109
  144.8 16.9 %all_to_all.20.in_ref = bf16[16,8,640]{2,1,0:T(8,128)(2,1)S(1)} all-to-all(bf16[16,8,640]{2,1,0:T(8,128)(2,1)S(1)} %shard_map.109), channel_id=1, replica_groups=mesh['groups'=2,'x'=4,'z'=16,'width'=2] {'z'}, dimensions={0} | all-to-all | bytes 327680 | tf_op jit(solution)/shard_map/all_to_all | solution.py:24
  161.7 0.3 shard_map.110
  161.9 17.7 %all_to_all.21.in_ref = bf16[16,8,512]{2,1,0:T(8,128)(2,1)S(1)} all-to-all(bf16[16,8,512]{2,1,0:T(8,128)(2,1)S(1)} %shard_map.110), channel_id=1, replica_groups=mesh['groups'=2,'x'=4,'z'=16,'width'=2] {'z'}, dimensions={0} | all-to-all | bytes 262144 | tf_op jit(solution)/shard_map/all_to_all | solution.py:24
  179.7 0.1 collective-permute-start.17
  179.8 2.8 %collective-permute-start.18 = (bf16[64,1024]{1,0:T(8,128)(2,1)S(1)}, bf16[64,1024]{1,0:T(8,128)(2,1)S(1)}, u32[]{:S(2)}, u32[]{:S(2)}) collective-permute-start(bf16[64,1024]{1,0:T(8,128)(2,1)S(1)} %shard_map.111.refs_0_), channel_id=1, source_target_pairs={{0,64},{32,96},{64,0},{96,32},{1,65},{33,97},{65,1},{97,33},{2,66}... | collective-permute-start | bytes 393224 | tf_op jit(solution)/shard_map/ppermute | solution.py:49
  182.6 1.1 collective-permute-start.19
  183.7 2.7 %collective-permute-done.18.refs_2_ = bf16[64,1024]{1,0:T(8,128)(2,1)S(1)} collective-permute-done((bf16[64,1024]{1,0:T(8,128)(2,1)S(1)}, bf16[64,1024]{1,0:T(8,128)(2,1)S(1)}, u32[]{:S(2)}, u32[]{:S(2)}) %collective-permute-start.18) | collective-permute-done | bytes 131104 | tf_op jit(solution)/shard_map/ppermute | solution.py:49
  186.4 1.4 collective-permute-done.19.refs_3_
  187.8 1.0 shard_map.112
  188.8 18.0 %collective-permute-start.20 = (f32[64,128]{1,0:T(8,128)S(1)}, f32[64,128]{1,0:T(8,128)S(1)}, u32[]{:S(2)}, u32[]{:S(2)}) collective-permute-start(f32[64,128]{1,0:T(8,128)S(1)} %get-tuple-element.21), channel_id=1, source_target_pairs={{0,1},{1,0},{2,3},{3,2},{4,5},{5,4},{6,7},{7,6},{8,9},{9,8},{10,11... | collective-permute-start | bytes 98312 | tf_op jit(solution)/shard_map/ppermute | solution.py:464
  206.8 0.9 collective-permute-done.20
  207.7 0.6 add_convert_fusion
  (38 shorter events, 0.3 us)
Async XLA Ops:
  7.2 89.8 %all-gather.2.cloned.1.call-start = ((), (), s32[]{:S(2)}) async-start(), calls=%async_computation.4 | async-start | bytes 2228224 | tf_op jit(solution)/shard_map/all_gather | solution.py:439
  8.9 1.0 copy-start.1
  10.1 10.9 %collective-permute-start = (bf16[2,32,2048]{2,1,0:T(8,128)(2,1)S(1)}, bf16[2,32,2048]{2,1,0:T(8,128)(2,1)S(1)}, u32[]{:S(2)}, u32[]{:S(2)}) collective-permute-start(bf16[2,32,2048]{2,1,0:T(8,128)(2,1)S(1)} %get-tuple-element.27), channel_id=1, source_target_pairs={{0,128},{128,0},{1,129},{129,1},{2,130},{130,2},{3,131},{131,3},{4... | collective-permute-start | bytes 786440 | tf_op jit(solution)/shard_map/ppermute | solution.py:366
  15.9 25.3 %copy-start.6 = (s32[32]{0:T(128)S(1)}, s32[32]{0:T(128)}, u32[]{:S(2)}) copy-start(s32[32]{0:T(128)} %param.16) | copy-start | bytes 388
  15.9 38.0 %collective-permute-start.10 = (f32[64,1152]{1,0:T(8,128)S(1)}, f32[64,1152]{1,0:T(8,128)S(1)}, u32[]{:S(2)}, u32[]{:S(2)}) collective-permute-start(f32[64,1152]{1,0:T(8,128)S(1)} %get-tuple-element.15), channel_id=1, source_target_pairs={{0,96},{32,64},{64,32},{96,0},{1,97},{33,65},{65,33},{97,1},{2,98}... | collective-permute-start | bytes 884744 | tf_op jit(solution)/shard_map/ppermute | solution.py:49
  18.9 35.0 %collective-permute-start.8 = (f32[64,1152]{1,0:T(8,128)S(1)}, f32[64,1152]{1,0:T(8,128)S(1)}, u32[]{:S(2)}, u32[]{:S(2)}) collective-permute-start(f32[64,1152]{1,0:T(8,128)S(1)} %get-tuple-element.13), channel_id=1, source_target_pairs={{0,32},{32,0},{64,96},{96,64},{1,33},{33,1},{65,97},{97,65},{2,34}... | collective-permute-start | bytes 884744 | tf_op jit(solution)/shard_map/ppermute | solution.py:49
  19.0 35.0 %collective-permute-start.9 = (f32[64,1152]{1,0:T(8,128)S(1)}, f32[64,1152]{1,0:T(8,128)S(1)}, u32[]{:S(2)}, u32[]{:S(2)}) collective-permute-start(f32[64,1152]{1,0:T(8,128)S(1)} %get-tuple-element.14), channel_id=1, source_target_pairs={{0,64},{32,96},{64,0},{96,32},{1,65},{33,97},{65,1},{97,33},{2,66}... | collective-permute-start | bytes 884744 | tf_op jit(solution)/shard_map/ppermute | solution.py:49
  21.2 27.5 %collective-permute-start.1 = (bf16[2,32,2048]{2,1,0:T(8,128)(2,1)S(1)}, bf16[2,32,2048]{2,1,0:T(8,128)(2,1)S(1)}, u32[]{:S(2)}, u32[]{:S(2)}) collective-permute-start(bf16[2,32,2048]{2,1,0:T(8,128)(2,1)S(1)} %get-tuple-element.24), channel_id=1, source_target_pairs={{0,0},{1,64},{32,32},{33,96},{64,1},{65,65},{96,33},{97,97},{2,2},... | collective-permute-start | bytes 786440 | tf_op jit(solution)/shard_map/ppermute | solution.py:384
  41.0 10.8 %collective-permute-start.2 = (bf16[2,32,2048]{2,1,0:T(8,128)(2,1)S(1)}, bf16[2,32,2048]{2,1,0:T(8,128)(2,1)S(1)}, u32[]{:S(2)}, u32[]{:S(2)}) collective-permute-start(bf16[2,32,2048]{2,1,0:T(8,128)(2,1)S(1)} %get-tuple-element.25), channel_id=1, source_target_pairs={{0,32},{1,96},{32,0},{33,64},{64,33},{65,97},{96,1},{97,65},{2,34}... | collective-permute-start | bytes 786440 | tf_op jit(solution)/shard_map/ppermute | solution.py:384
  51.7 0.7 copy-start.5
  53.5 13.6 %collective-permute-start.3 = (bf16[2,2,32,2048]{3,2,1,0:T(8,128)(2,1)S(1)}, bf16[2,2,32,2048]{3,2,1,0:T(8,128)(2,1)}, u32[]{:S(2)}, u32[]{:S(2)}) collective-permute-start(bf16[2,2,32,2048]{3,2,1,0:T(8,128)(2,1)S(1)} %get-tuple-element.23), channel_id=1, source_target_pairs={{0,1},{1,0},{2,3},{3,2},{4,5},{5,4},{6,7},{7,6},{8,9},{9,8},{10,11... | collective-permute-start | bytes 1572872 | tf_op jit(solution)/shard_map/ppermute | solution.py:386
  54.8 45.1 %all-to-all-start = ((f32[16,8,640]{2,1,0:T(8,128)}), f32[16,8,640]{2,1,0:T(8,128)S(1)}, u32[]{:S(2)}, u32[]{:S(2)}) async-start(f32[16,8,640]{2,1,0:T(8,128)} %shard_map.105), calls=%async_computation | async-start | bytes 655360 | tf_op jit(solution)/shard_map/all_to_all | solution.py:24
  99.3 13.5 %copy-start.3 = (bf16[1024,2,128]{2,1,0:T(2,128)(2,1)S(1)}, bf16[1024,2,128]{2,1,0:T(2,128)(2,1)}, u32[]{:S(2)}) copy-start(bf16[1024,2,128]{2,1,0:T(2,128)(2,1)} %param.14) | copy-start | bytes 1572868
  99.3 13.4 %copy-start.4 = (bf16[1024,2,128]{2,1,0:T(2,128)(2,1)S(1)}, bf16[1024,2,128]{2,1,0:T(2,128)(2,1)}, u32[]{:S(2)}) copy-start(bf16[1024,2,128]{2,1,0:T(2,128)(2,1)} %param.13) | copy-start | bytes 1572868
  99.3 9.2 %collective-permute-start.4 = (f32[4,32,512]{2,1,0:T(8,128)S(1)}, f32[4,32,512]{2,1,0:T(8,128)S(1)}, u32[]{:S(2)}, u32[]{:S(2)}) collective-permute-start(f32[4,32,512]{2,1,0:T(8,128)S(1)} %slice_bitcast_fusion), channel_id=1, source_target_pairs={{0,128},{128,0},{1,129},{129,1},{2,130},{130,2},{3,131},{131,3},{4... | collective-permute-start | bytes 786440 | tf_op jit(solution)/shard_map/ppermute | solution.py:366
  100.6 19.8 %all-to-all-start.1 = ((bf16[16,8,640]{2,1,0:T(8,128)(2,1)}), bf16[16,8,640]{2,1,0:T(8,128)(2,1)S(1)}, u32[]{:S(2)}, u32[]{:S(2)}) async-start(bf16[16,8,640]{2,1,0:T(8,128)(2,1)} %shard_map.106), calls=%async_computation.1 | async-start | bytes 327680 | tf_op jit(solution)/shard_map/all_to_all | solution.py:24
  108.6 16.0 %collective-permute-start.5 = (f32[32,512]{1,0:T(8,128)S(1)}, f32[32,512]{1,0:T(8,128)S(1)}, u32[]{:S(2)}, u32[]{:S(2)}) collective-permute-start(f32[32,512]{1,0:T(8,128)S(1)} %get-tuple-element.28), channel_id=1, source_target_pairs={{0,32},{32,0},{64,96},{96,64},{1,33},{33,1},{65,97},{97,65},{2,34}... | collective-permute-start | bytes 196616 | tf_op jit(solution)/shard_map/ppermute | solution.py:399
  110.0 14.6 %collective-permute-start.6 = (f32[32,512]{1,0:T(8,128)S(1)}, f32[32,512]{1,0:T(8,128)S(1)}, u32[]{:S(2)}, u32[]{:S(2)}) collective-permute-start(f32[32,512]{1,0:T(8,128)S(1)} %get-tuple-element.30), channel_id=1, source_target_pairs={{0,64},{32,96},{64,0},{96,32},{1,65},{33,97},{65,1},{97,33},{2,66}... | collective-permute-start | bytes 196616 | tf_op jit(solution)/shard_map/ppermute | solution.py:399
  112.7 11.9 %collective-permute-start.7 = (f32[32,512]{1,0:T(8,128)S(1)}, f32[32,512]{1,0:T(8,128)S(1)}, u32[]{:S(2)}, u32[]{:S(2)}) collective-permute-start(f32[32,512]{1,0:T(8,128)S(1)} %get-tuple-element.29), channel_id=1, source_target_pairs={{0,96},{32,64},{64,32},{96,0},{1,97},{33,65},{65,33},{97,1},{2,98}... | collective-permute-start | bytes 196616 | tf_op jit(solution)/shard_map/ppermute | solution.py:399
  120.4 67.4 %copy-start = (bf16[4096,256]{1,0:T(8,128)(2,1)S(1)}, bf16[4096,256]{1,0:T(8,128)(2,1)}, u32[]{:S(2)}) copy-start(bf16[4096,256]{1,0:T(8,128)(2,1)} %refs_4_.1) | copy-start | bytes 6291460
  120.4 5.1 %collective-permute-start.11 = (bf16[64,1152]{1,0:T(8,128)(2,1)S(1)}, bf16[64,1152]{1,0:T(8,128)(2,1)S(1)}, u32[]{:S(2)}, u32[]{:S(2)}) collective-permute-start(bf16[64,1152]{1,0:T(8,128)(2,1)S(1)} %shard_map.107.refs_0_), channel_id=1, source_target_pairs={{0,32},{32,0},{64,96},{96,64},{1,33},{33,1},{65,97},{97,65},{2,34}... | collective-permute-start | bytes 442376 | tf_op jit(solution)/shard_map/ppermute | solution.py:49
  121.9 7.1 %collective-permute-start.12 = (bf16[64,1152]{1,0:T(8,128)(2,1)S(1)}, bf16[64,1152]{1,0:T(8,128)(2,1)S(1)}, u32[]{:S(2)}, u32[]{:S(2)}) collective-permute-start(bf16[64,1152]{1,0:T(8,128)(2,1)S(1)} %shard_map.107.refs_0_), channel_id=1, source_target_pairs={{0,64},{32,96},{64,0},{96,32},{1,65},{33,97},{65,1},{97,33},{2,66}... | collective-permute-start | bytes 442376 | tf_op jit(solution)/shard_map/ppermute | solution.py:49
  124.6 5.9 %collective-permute-start.13 = (bf16[64,1152]{1,0:T(8,128)(2,1)S(1)}, bf16[64,1152]{1,0:T(8,128)(2,1)S(1)}, u32[]{:S(2)}, u32[]{:S(2)}) collective-permute-start(bf16[64,1152]{1,0:T(8,128)(2,1)S(1)} %shard_map.107.refs_0_), channel_id=1, source_target_pairs={{0,96},{32,64},{64,32},{96,0},{1,97},{33,65},{65,33},{97,1},{2,98}... | collective-permute-start | bytes 442376 | tf_op jit(solution)/shard_map/ppermute | solution.py:49
  124.6 64.2 %copy-start.2 = (bf16[32,512]{1,0:T(8,128)(2,1)}, bf16[32,512]{1,0:T(8,128)(2,1)S(1)}, u32[]{:S(2)}) copy-start(bf16[32,512]{1,0:T(8,128)(2,1)S(1)} %fusion.7.refs_6_) | copy-start | bytes 98308
  135.9 4.5 %collective-permute-start.14 = (bf16[64,1152]{1,0:T(8,128)(2,1)S(1)}, bf16[64,1152]{1,0:T(8,128)(2,1)S(1)}, u32[]{:S(2)}, u32[]{:S(2)}) collective-permute-start(bf16[64,1152]{1,0:T(8,128)(2,1)S(1)} %get-tuple-element.17), channel_id=1, source_target_pairs={{0,32},{32,0},{64,96},{96,64},{1,33},{33,1},{65,97},{97,65},{2,34}... | collective-permute-start | bytes 442376 | tf_op jit(solution)/shard_map/ppermute | solution.py:49
  136.1 6.4 %collective-permute-start.15 = (bf16[64,1152]{1,0:T(8,128)(2,1)S(1)}, bf16[64,1152]{1,0:T(8,128)(2,1)S(1)}, u32[]{:S(2)}, u32[]{:S(2)}) collective-permute-start(bf16[64,1152]{1,0:T(8,128)(2,1)S(1)} %get-tuple-element.18), channel_id=1, source_target_pairs={{0,64},{32,96},{64,0},{96,32},{1,65},{33,97},{65,1},{97,33},{2,66}... | collective-permute-start | bytes 442376 | tf_op jit(solution)/shard_map/ppermute | solution.py:49
  137.9 6.2 %collective-permute-start.16 = (bf16[64,1152]{1,0:T(8,128)(2,1)S(1)}, bf16[64,1152]{1,0:T(8,128)(2,1)S(1)}, u32[]{:S(2)}, u32[]{:S(2)}) collective-permute-start(bf16[64,1152]{1,0:T(8,128)(2,1)S(1)} %get-tuple-element.19), channel_id=1, source_target_pairs={{0,96},{32,64},{64,32},{96,0},{1,97},{33,65},{65,33},{97,1},{2,98}... | collective-permute-start | bytes 442376 | tf_op jit(solution)/shard_map/ppermute | solution.py:49
  179.7 4.0 %collective-permute-start.17 = (bf16[64,1024]{1,0:T(8,128)(2,1)S(1)}, bf16[64,1024]{1,0:T(8,128)(2,1)S(1)}, u32[]{:S(2)}, u32[]{:S(2)}) collective-permute-start(bf16[64,1024]{1,0:T(8,128)(2,1)S(1)} %shard_map.111.refs_0_), channel_id=1, source_target_pairs={{0,32},{32,0},{64,96},{96,64},{1,33},{33,1},{65,97},{97,65},{2,34}... | collective-permute-start | bytes 393224 | tf_op jit(solution)/shard_map/ppermute | solution.py:49
  179.8 6.5 %collective-permute-start.18 = (bf16[64,1024]{1,0:T(8,128)(2,1)S(1)}, bf16[64,1024]{1,0:T(8,128)(2,1)S(1)}, u32[]{:S(2)}, u32[]{:S(2)}) collective-permute-start(bf16[64,1024]{1,0:T(8,128)(2,1)S(1)} %shard_map.111.refs_0_), channel_id=1, source_target_pairs={{0,64},{32,96},{64,0},{96,32},{1,65},{33,97},{65,1},{97,33},{2,66}... | collective-permute-start | bytes 393224 | tf_op jit(solution)/shard_map/ppermute | solution.py:49
  182.6 5.2 %collective-permute-start.19 = (bf16[64,1024]{1,0:T(8,128)(2,1)S(1)}, bf16[64,1024]{1,0:T(8,128)(2,1)S(1)}, u32[]{:S(2)}, u32[]{:S(2)}) collective-permute-start(bf16[64,1024]{1,0:T(8,128)(2,1)S(1)} %shard_map.111.refs_0_), channel_id=1, source_target_pairs={{0,96},{32,64},{64,32},{96,0},{1,97},{33,65},{65,33},{97,1},{2,98}... | collective-permute-start | bytes 393224 | tf_op jit(solution)/shard_map/ppermute | solution.py:49
  188.8 18.9 %collective-permute-start.20 = (f32[64,128]{1,0:T(8,128)S(1)}, f32[64,128]{1,0:T(8,128)S(1)}, u32[]{:S(2)}, u32[]{:S(2)}) collective-permute-start(f32[64,128]{1,0:T(8,128)S(1)} %get-tuple-element.21), channel_id=1, source_target_pairs={{0,1},{1,0},{2,3},{3,2},{4,5},{5,4},{6,7},{7,6},{8,9},{9,8},{10,11... | collective-permute-start | bytes 98312 | tf_op jit(solution)/shard_map/ppermute | solution.py:464
Sparse Core Ops, SparseCore 0:
  9.8 87.1 all-gather.1

commit v6 on v5

--- a/solution.py
+++ b/solution.py
@@ -388,16 +388,88 @@
     return swapped_if((core ^ (x >> 1)) == 1, ready, 0).reshape(xs, 2, tokens, depth)
 
 
-def added_at_home(partial):
-    xs = lax.axis_size("x")
-    received = with_neighbour(partial[:, 1])
-    partial = partial[:, 0] + received
-    total = partial[0]
-    received = []
-    for mask in range(1, xs):
-        pairs = [(i, i ^ mask) for i in range(xs)]
-        received.append(lax.ppermute(partial[mask], "x", pairs))
-    for more in received:
+def own_half(place, kv_weight):
+    rows, width = kv_weight.shape
+    half = rows // 2
+
+    def body(place_ref, weight_hbm, out_ref, sem):
+        begin = pl.multiple_of((place_ref[3] & 1) * half, half)
+        copy = pltpu.make_async_copy(weight_hbm.at[pl.ds(begin, half), :], out_ref, sem)
+        copy.start()
+        copy.wait()
+
+    return pl.pallas_call(
+        body,
+        in_specs=[
+            pl.BlockSpec(memory_space=pltpu.SMEM),
+            pl.BlockSpec(memory_space=pltpu.HBM),
+        ],
+        out_shape=pltpu.VMEM((half, width), BF16),
+        scratch_shapes=[pltpu.SemaphoreType.DMA],
+        compiler_params=pltpu.CompilerParams(vmem_limit_bytes=16 * 2**20),
+        name="own_half",
+    )(place, pltpu.with_memory_space_constraint(kv_weight, pltpu.HBM))
+
+
+def gathered_over_z(own):
+    zs = lax.axis_size("z")
+    up = [(i, (i + 1) % zs) for i in range(zs)]
+    down = [(i, (i - 1) % zs) for i in range(zs)]
+    below = above = own
+    blocks = [own]
+    for s in range(1, zs // 2 + 1):
+        below = lax.ppermute(below, "z", up)
+        blocks.append(below)
+        if s < zs // 2:
+            above = lax.ppermute(above, "z", down)
+            blocks.append(above)
+    return blocks
+
+
+def span_dot(place, ready, blocks):
+    xs, groups, tokens, depth = ready.shape
+    zs = len(blocks)
+    block, width = blocks[0].shape
+    offsets = [0]
+    for s in range(1, zs // 2 + 1):
+        offsets += [zs - s, s]
+    offsets = offsets[:zs]
+
+    def body(place_ref, ready_ref, *refs):
+        home_ref, away_ref = refs[zs:]
+
+        def features(i):
+            begin = lax.rem(place_ref[2] + offsets[i], zs) * block
+            return ready_ref[:, pl.ds(pl.multiple_of(begin, block), block)]
+
+        total = None
+        for i in range(0, zs, 2):
+            left = jnp.concatenate([features(i), features(i + 1)], axis=1)
+            right = jnp.concatenate([refs[i][...], refs[i + 1][...]], axis=0)
+            more = dot_f32(left, right)
+            total = more if total is None else total + more
+        for m in range(xs):
+            begin = m * groups * tokens
+            home_ref[m] = total[begin : begin + tokens]
+            away_ref[m] = total[begin + tokens : begin + 2 * tokens]
+
+    flat = ready.reshape(xs * groups * tokens, depth)
+    outs = [array((xs, tokens, width), F32)] * 2
+    return on_chip(body, outs, flat, *blocks, place=place)
+
+
+def added_at_home(home, away):
+    received = with_neighbour(away)
+    count = home.shape[0]
+
+    def body(home_ref, received_ref, *outs):
+        for m in range(count):
+            outs[m][...] = home_ref[m] + received_ref[m]
+
+    outs = [array(home.shape[1:], F32)] * count
+    received = exchanged_over_x(on_chip(body, outs, home, received))
+    total = received[0]
+    for more in received[1:]:
         total = total + more
     return total.astype(BF16)
 
@@ -433,22 +505,16 @@
     rows = step_count * branch_count
     scale = LOG2E / math.sqrt(HD)
     tokens = span_tokens.shape[0]
-    half = kv_weight.shape[0] // 2
-    begin = (lax.axis_index("groups") & 1) * half
-    span_weight = lax.dynamic_slice_in_dim(kv_weight, begin, half, 0)
-    span_weight = lax.all_gather(span_weight, "z", axis=0, tiled=True)
-
-    place = jnp.stack([lax.axis_index("x"), lax.axis_index("width")])
-
+    place = jnp.stack([lax.axis_index(a) for a in ("x", "width", "z", "groups")])
+    blocks = gathered_over_z(own_half(place, kv_weight))
     partial = project(place, hidden.reshape(rows, depth), query_weight, kv_weight, xs)
     partial = exchanged_over_x(partial)
-    ready = tokens_by_features(span_tokens, span_weight.shape[0])
+    ready = tokens_by_features(span_tokens, zs * blocks[0].shape[0])
     partial = add_over_x(partial, zs)
     partial = exchanged(partial, "z")
     own = add_over_z(partial)
     own = exchanged(own, "z")
-    span_partial = dot_f32(ready.reshape(-1, span_weight.shape[0]), span_weight)
-    span_kv = added_at_home(span_partial.reshape(xs, 2, tokens, kv_weight.shape[1]))
+    span_kv = added_at_home(*span_dot(place, ready, blocks))
     columns = fan(own, rows, HD)
     projected = exchanged_over_x([columns] * xs)
 

time: 216 us -> 200 us (0.926)
  waiting for transfers between devices: 61.5 us -> 46.8 us
  between operations: 15.1 us -> 1.71 us
  starting transfers between devices: 82.4 us -> 94.2 us
  Pallas kernels: 11.8 us -> 14.6 us
  matrix products: 2.31 us -> 0 us
    ppermute x3 -> x15, starting transfers between devices: 4.17 us -> 37.8 us  [the longest x7 34.6 us: gathered_over_z(): above = lax.ppermute(above, 'z', down)]
    all_gather x1 -> x0, waiting for transfers between devices: 28.5 us -> none  [local(): span_weight = lax.all_gather(span_weight, 'z', axis=0, tiled=True)]
    ppermute x3 -> x15, waiting for transfers between devices: 0.01 us -> 27.4 us  [the longest x7 21.9 us: gathered_over_z(): above = lax.ppermute(above, 'z', down)]
    ppermute x2, starting transfers between devices: 20.1 us -> 7.51 us  [tokens_by_features(): mine.append(lax.ppermute(both[i], ('x', 'width'), pairs))]
    ppermute x2, waiting for transfers between devices: 10.4 us -> 0.01 us  [tokens_by_features(): mine.append(lax.ppermute(both[i], ('x', 'width'), pairs))]
    ppermute x1, starting transfers between devices: 18 us -> 9.88 us  [local(): lax.ppermute(send, 'width', [(0, 1), (1, 0)])]
    all_to_all x2, starting transfers between devices: 20.2 us -> 16 us  [exchanged(): return lax.all_to_all(pieces, axis, split_axis=0, concat_axis=0, tiled=True)]
    ppermute x12 -> x15, starting transfers between devices: 16.5 us -> 20.2 us  [exchanged_over_x(): received.append(lax.ppermute(pieces[mask], 'x', pairs))]
  transfers between devices with their start and end apart: 24 -> 38, of which waited for: 13 -> 18; matrix products, arithmetic and copies ran while one was open for 3% -> 2% of each run, Pallas kernels for 2% -> 4%
where the time goes in v6:
time: 200 us; the launch traced here: 199 us
  starting transfers between devices  94.2 us (47%)
  waiting for transfers between devices  46.8 us (23%)
  blocking collectives  34.8 us (17%)
  Pallas kernels  14.6 us (7%)
  other arithmetic  3.96 us (2%)
  local copies, waits for them, and re-layouts  3.2 us (2%)
    all_to_all x2, blocking collectives, exchanged(): return lax.all_to_all(pieces, axis, split_axis=0, concat_axis=0, tiled=True)  34.8 us
    ppermute x7, starting transfers between devices, gathered_over_z(): above = lax.ppermute(above, 'z', down)  34.6 us
    ppermute x7, waiting for transfers between devices, gathered_over_z(): above = lax.ppermute(above, 'z', down)  21.9 us
    ppermute x15, starting transfers between devices, exchanged_over_x(): received.append(lax.ppermute(pieces[mask], 'x', pairs))  20.2 us
    all_to_all x2, starting transfers between devices, exchanged(): return lax.all_to_all(pieces, axis, split_axis=0, concat_axis=0, tiled=True)  16 us
    ppermute x15, waiting for transfers between devices, exchanged_over_x(): received.append(lax.ppermute(pieces[mask], 'x', pairs))  12 us
    pallas_call x11, Pallas kernels, on_chip(): pl.pallas_call(body, in_specs=specs, out_shape=shapes, scratch_shapes=scr...  10.1 us
    ppermute x1, starting transfers between devices, local(): lax.ppermute(send, 'width', [(0, 1), (1, 0)])  9.88 us
  transfers between devices with their start and end apart: 38, of which 18 were waited for; matrix products, arithmetic and copies ran while one was open for 2% of the time, Pallas kernels for 4%

profile of v6, /device:TPU:33, one launch (start us, length us, event | category | flops | bytes accessed | tf_op | source)
XLA Modules:
  0.0 199.3 jit_solution(13737267482467544147)
XLA Ops:
  0.6 1.0 copy-done.1
  1.8 0.7 select_bitcast_fusion.1
  2.5 2.7 %collective-permute-start = (bf16[2,32,2048]{2,1,0:T(8,128)(2,1)}, bf16[2,32,2048]{2,1,0:T(8,128)(2,1)S(1)}, u32[]{:S(2)}, u32[]{:S(2)}) collective-permute-start(bf16[2,32,2048]{2,1,0:T(8,128)(2,1)} %get-tuple-element.39), channel_id=1, source_target_pairs={{0,128},{128,0},{1,129},{129,1},{2,130},{130,2},{3,131},{131,3},{4... | collective-permute-start | bytes 786440 | tf_op jit(solution)/shard_map/ppermute | solution.py:366
  5.2 1.5 own_half.1.refs_0_
  6.7 2.6 %collective-permute-start.4 = (bf16[128,512]{1,0:T(8,128)(2,1)S(1)}, bf16[128,512]{1,0:T(8,128)(2,1)S(1)}, u32[]{:S(2)}, u32[]{:S(2)}) collective-permute-start(bf16[128,512]{1,0:T(8,128)(2,1)S(1)} %own_half.1.refs_0_), channel_id=1, source_target_pairs={{0,2},{2,4},{4,6},{6,8},{8,10},{10,12},{12,14},{14,16},{16,18},{18... | collective-permute-start | bytes 393224 | tf_op jit(solution)/shard_map/ppermute | solution.py:421
  9.3 19.7 %collective-permute-start.5 = (bf16[128,512]{1,0:T(8,128)(2,1)S(1)}, bf16[128,512]{1,0:T(8,128)(2,1)S(1)}, u32[]{:S(2)}, u32[]{:S(2)}) collective-permute-start(bf16[128,512]{1,0:T(8,128)(2,1)S(1)} %own_half.1.refs_0_), channel_id=1, source_target_pairs={{0,30},{2,0},{4,2},{6,4},{8,6},{10,8},{12,10},{14,12},{16,14},{18,... | collective-permute-start | bytes 393224 | tf_op jit(solution)/shard_map/ppermute | solution.py:424
  29.1 3.0 %project.1 = (f32[64,1152]{1,0:T(8,128)S(1)}, f32[64,1152]{1,0:T(8,128)S(1)}, f32[64,1152]{1,0:T(8,128)S(1)}, f32[64,1152]{1,0:T(8,128)S(1)}) custom-call(s32[4]{0:T(128)S(1)} %pad_add_fusion.place_ref, bf16[64,256]{1,0:T(8,128)(2,1)} %bitcast.33, bf16[256,4096]{1,0:T(8,128)(2,1)} %query_hbm.1, bf16[256,512]{1,0:T(8,128)(2,1)} %fresh_hbm.1), custom_call_target="tpu_custom_call" | custom-call | tf_op jit(solution)/shard_map/project/pallas_call | solution.py:88
  32.1 1.5 collective-permute-start.23
  33.6 2.7 %collective-permute-start.24 = (f32[64,1152]{1,0:T(8,128)S(1)}, f32[64,1152]{1,0:T(8,128)S(1)}, u32[]{:S(2)}, u32[]{:S(2)}) collective-permute-start(f32[64,1152]{1,0:T(8,128)S(1)} %get-tuple-element.26), channel_id=1, source_target_pairs={{0,64},{32,96},{64,0},{96,32},{1,65},{33,97},{65,1},{97,33},{2,66}... | collective-permute-start | bytes 884744 | tf_op jit(solution)/shard_map/ppermute | solution.py:49
  36.9 0.1 collective-permute-start.25
  37.3 2.6 %collective-permute-start.7 = (bf16[128,512]{1,0:T(8,128)(2,1)S(1)}, bf16[128,512]{1,0:T(8,128)(2,1)S(1)}, u32[]{:S(2)}, u32[]{:S(2)}) collective-permute-start(bf16[128,512]{1,0:T(8,128)(2,1)S(1)} %collective-permute-done.5.refs_2_), channel_id=1, source_target_pairs={{0,30},{2,0},{4,2},{6,4},{8,6},{10,8},{12,10},{14,12},{16,14},{18,... | collective-permute-start | bytes 393224 | tf_op jit(solution)/shard_map/ppermute | solution.py:424
  40.1 2.2 %collective-permute-done.6.refs_3_ = bf16[128,512]{1,0:T(8,128)(2,1)S(1)} collective-permute-done((bf16[128,512]{1,0:T(8,128)(2,1)S(1)}, bf16[128,512]{1,0:T(8,128)(2,1)S(1)}, u32[]{:S(2)}, u32[]{:S(2)}) %collective-permute-start.6) | collective-permute-done | bytes 131104 | tf_op jit(solution)/shard_map/ppermute | solution.py:421
  42.2 0.7 slice_bitcast_fusion.1
  43.0 5.6 %collective-permute-start.2 = (bf16[2,32,2048]{2,1,0:T(8,128)(2,1)}, bf16[2,32,2048]{2,1,0:T(8,128)(2,1)}, u32[]{:S(2)}, u32[]{:S(2)}) collective-permute-start(bf16[2,32,2048]{2,1,0:T(8,128)(2,1)} %get-tuple-element.37), channel_id=1, source_target_pairs={{0,32},{1,96},{32,0},{33,64},{64,33},{65,97},{96,1},{97,65},{2,34}... | collective-permute-start | bytes 786440 | tf_op jit(solution)/shard_map/ppermute | solution.py:384
  48.6 1.9 collective-permute-start.1
  50.5 3.1 %collective-permute-start.9 = (bf16[128,512]{1,0:T(8,128)(2,1)S(1)}, bf16[128,512]{1,0:T(8,128)(2,1)S(1)}, u32[]{:S(2)}, u32[]{:S(2)}) collective-permute-start(bf16[128,512]{1,0:T(8,128)(2,1)S(1)} %collective-permute-done.7.refs_4_), channel_id=1, source_target_pairs={{0,30},{2,0},{4,2},{6,4},{8,6},{10,8},{12,10},{14,12},{16,14},{18,... | collective-permute-start | bytes 393224 | tf_op jit(solution)/shard_map/ppermute | solution.py:424
  53.7 0.8 shard_map.107
  54.5 5.5 %all-to-all-start = ((f32[16,8,640]{2,1,0:T(8,128)}), f32[16,8,640]{2,1,0:T(8,128)S(1)}, u32[]{:S(2)}, u32[]{:S(2)}) async-start(f32[16,8,640]{2,1,0:T(8,128)} %shard_map.107), calls=%async_computation | async-start | bytes 655360 | tf_op jit(solution)/shard_map/all_to_all | solution.py:24
  60.1 2.5 %collective-permute-start.11 = (bf16[128,512]{1,0:T(8,128)(2,1)S(1)}, bf16[128,512]{1,0:T(8,128)(2,1)S(1)}, u32[]{:S(2)}, u32[]{:S(2)}) collective-permute-start(bf16[128,512]{1,0:T(8,128)(2,1)S(1)} %collective-permute-done.9.refs_6_), channel_id=1, source_target_pairs={{0,30},{2,0},{4,2},{6,4},{8,6},{10,8},{12,10},{14,12},{16,14},{18,... | collective-permute-start | bytes 393224 | tf_op jit(solution)/shard_map/ppermute | solution.py:424
  62.6 1.8 fusion.2
  64.4 14.7 %collective-permute-done.11.refs_8_ = bf16[128,512]{1,0:T(8,128)(2,1)S(1)} collective-permute-done((bf16[128,512]{1,0:T(8,128)(2,1)S(1)}, bf16[128,512]{1,0:T(8,128)(2,1)S(1)}, u32[]{:S(2)}, u32[]{:S(2)}) %collective-permute-start.11) | collective-permute-done | bytes 131104 | tf_op jit(solution)/shard_map/ppermute | solution.py:424
  79.1 1.0 collective-permute-start.13
  80.0 0.5 collective-permute-start.14
  80.7 3.6 %collective-permute-done.13.refs_10_ = bf16[128,512]{1,0:T(8,128)(2,1)S(1)} collective-permute-done((bf16[128,512]{1,0:T(8,128)(2,1)S(1)}, bf16[128,512]{1,0:T(8,128)(2,1)S(1)}, u32[]{:S(2)}, u32[]{:S(2)}) %collective-permute-start.13) | collective-permute-done | bytes 131104 | tf_op jit(solution)/shard_map/ppermute | solution.py:424
  84.2 2.2 %collective-permute-start.15 = (bf16[128,512]{1,0:T(8,128)(2,1)S(1)}, bf16[128,512]{1,0:T(8,128)(2,1)S(1)}, u32[]{:S(2)}, u32[]{:S(2)}) collective-permute-start(bf16[128,512]{1,0:T(8,128)(2,1)S(1)} %collective-permute-done.13.refs_10_), channel_id=1, source_target_pairs={{0,30},{2,0},{4,2},{6,4},{8,6},{10,8},{12,10},{14,12},{16,14},{18,... | collective-permute-start | bytes 393224 | tf_op jit(solution)/shard_map/ppermute | solution.py:424
  86.8 2.1 %collective-permute-done.15.refs_12_ = bf16[128,512]{1,0:T(8,128)(2,1)S(1)} collective-permute-done((bf16[128,512]{1,0:T(8,128)(2,1)S(1)}, bf16[128,512]{1,0:T(8,128)(2,1)S(1)}, u32[]{:S(2)}, u32[]{:S(2)}) %collective-permute-start.15) | collective-permute-done | bytes 131104 | tf_op jit(solution)/shard_map/ppermute | solution.py:424
  88.9 3.4 %collective-permute-start.17 = (bf16[128,512]{1,0:T(8,128)(2,1)S(1)}, bf16[128,512]{1,0:T(8,128)(2,1)S(1)}, u32[]{:S(2)}, u32[]{:S(2)}) collective-permute-start(bf16[128,512]{1,0:T(8,128)(2,1)S(1)} %collective-permute-done.15.refs_12_), channel_id=1, source_target_pairs={{0,30},{2,0},{4,2},{6,4},{8,6},{10,8},{12,10},{14,12},{16,14},{18,... | collective-permute-start | bytes 393224 | tf_op jit(solution)/shard_map/ppermute | solution.py:424
  92.5 0.2 reverse_select_fusion
  92.7 1.6 collective-permute-done.17.refs_14_
  94.3 3.1 %collective-permute-done.18.refs_15_ = bf16[128,512]{1,0:T(8,128)(2,1)S(1)} collective-permute-done((bf16[128,512]{1,0:T(8,128)(2,1)S(1)}, bf16[128,512]{1,0:T(8,128)(2,1)S(1)}, u32[]{:S(2)}, u32[]{:S(2)}) %collective-permute-start.18) | collective-permute-done | bytes 131104 | tf_op jit(solution)/shard_map/ppermute | solution.py:421
  97.4 1.3 shard_map.105
  98.7 0.1 collective-permute-start.19
  98.8 0.7 shard_map.108
  99.5 10.4 %all-to-all-start.1 = ((bf16[16,8,640]{2,1,0:T(8,128)(2,1)}), bf16[16,8,640]{2,1,0:T(8,128)(2,1)S(1)}, u32[]{:S(2)}, u32[]{:S(2)}) async-start(bf16[16,8,640]{2,1,0:T(8,128)(2,1)} %shard_map.108), calls=%async_computation.1 | async-start | bytes 327680 | tf_op jit(solution)/shard_map/all_to_all | solution.py:24
  110.1 0.1 collective-permute-start.20
  110.2 0.1 collective-permute-start.21
  110.3 3.7 %collective-permute-start.22 = (f32[32,512]{1,0:T(8,128)S(1)}, f32[32,512]{1,0:T(8,128)S(1)}, u32[]{:S(2)}, u32[]{:S(2)}) collective-permute-start(f32[32,512]{1,0:T(8,128)S(1)} %get-tuple-element.23), channel_id=1, source_target_pairs={{0,96},{32,64},{64,32},{96,0},{1,97},{33,65},{65,33},{97,1},{2,98}... | collective-permute-start | bytes 196616 | tf_op jit(solution)/shard_map/ppermute | solution.py:49
  114.0 1.2 copy_bitcast_fusion
  115.2 6.6 %all-to-all-done.1.in_ref = bf16[16,8,640]{2,1,0:T(8,128)(2,1)S(1)} async-done(((bf16[16,8,640]{2,1,0:T(8,128)(2,1)}), bf16[16,8,640]{2,1,0:T(8,128)(2,1)S(1)}, u32[]{:S(2)}, u32[]{:S(2)}) %all-to-all-start.1) | async-done | bytes 163872 | tf_op jit(solution)/shard_map/all_to_all | solution.py:24
  121.9 0.1 collective-permute-start.26
  122.0 0.1 collective-permute-start.27
  122.2 3.7 %collective-permute-start.28 = (bf16[64,1152]{1,0:T(8,128)(2,1)S(1)}, bf16[64,1152]{1,0:T(8,128)(2,1)S(1)}, u32[]{:S(2)}, u32[]{:S(2)}) collective-permute-start(bf16[64,1152]{1,0:T(8,128)(2,1)S(1)} %shard_map.109.refs_0_), channel_id=1, source_target_pairs={{0,96},{32,64},{64,32},{96,0},{1,97},{33,65},{65,33},{97,1},{2,98}... | collective-permute-start | bytes 442376 | tf_op jit(solution)/shard_map/ppermute | solution.py:49
  125.9 0.4 collective-permute-done.26.refs_1_
  126.3 1.7 collective-permute-done.27.refs_2_
  128.0 1.2 collective-permute-done.28.refs_3_
  129.2 5.4 %shard_map.110 = (bf16[64,1152]{1,0:T(8,128)(2,1)S(1)}, bf16[64,1152]{1,0:T(8,128)(2,1)S(1)}, bf16[64,1152]{1,0:T(8,128)(2,1)S(1)}, bf16[64,1152]{1,0:T(8,128)(2,1)S(1)}) custom-call(s32[4]{0:T(128)S(1)} %pad_add_fusion.place_ref, bf16[64,1152]{1,0:T(8,128)(2,1)S(1)} %shard_map.109.refs_0_, bf16[64,1152]{1,0:T(8,128)(2,1)S(1)} %collective-permute-done.26.refs_1_, ...), custom_call_target="tpu_custom_call" | custom-call | tf_op jit(solution)/shard_map/pallas_call | solution.py:39
  134.7 0.5 collective-permute-start.29
  135.1 3.2 %collective-permute-start.30 = (bf16[64,1152]{1,0:T(8,128)(2,1)S(1)}, bf16[64,1152]{1,0:T(8,128)(2,1)S(1)}, u32[]{:S(2)}, u32[]{:S(2)}) collective-permute-start(bf16[64,1152]{1,0:T(8,128)(2,1)S(1)} %get-tuple-element.30), channel_id=1, source_target_pairs={{0,64},{32,96},{64,0},{96,32},{1,65},{33,97},{65,1},{97,33},{2,66}... | collective-permute-start | bytes 442376 | tf_op jit(solution)/shard_map/ppermute | solution.py:49
  138.3 0.4 collective-permute-start.31
  138.8 3.7 %collective-permute-done.30.refs_2_ = bf16[64,1152]{1,0:T(8,128)(2,1)S(1)} collective-permute-done((bf16[64,1152]{1,0:T(8,128)(2,1)S(1)}, bf16[64,1152]{1,0:T(8,128)(2,1)S(1)}, u32[]{:S(2)}, u32[]{:S(2)}) %collective-permute-start.30) | collective-permute-done | bytes 147488 | tf_op jit(solution)/shard_map/ppermute | solution.py:49
  142.4 1.5 collective-permute-done.31.refs_3_
  144.0 0.6 shard_map.111
  144.6 18.5 %all_to_all.20.in_ref = bf16[16,8,640]{2,1,0:T(8,128)(2,1)S(1)} all-to-all(bf16[16,8,640]{2,1,0:T(8,128)(2,1)S(1)} %shard_map.111), channel_id=1, replica_groups=mesh['groups'=2,'x'=4,'z'=16,'width'=2] {'z'}, dimensions={0} | all-to-all | bytes 327680 | tf_op jit(solution)/shard_map/all_to_all | solution.py:24
  163.0 0.3 shard_map.112
  163.3 16.4 %all_to_all.21.in_ref = bf16[16,8,512]{2,1,0:T(8,128)(2,1)S(1)} all-to-all(bf16[16,8,512]{2,1,0:T(8,128)(2,1)S(1)} %shard_map.112), channel_id=1, replica_groups=mesh['groups'=2,'x'=4,'z'=16,'width'=2] {'z'}, dimensions={0} | all-to-all | bytes 262144 | tf_op jit(solution)/shard_map/all_to_all | solution.py:24
  179.8 1.5 collective-permute-start.33
  181.3 2.3 %collective-permute-start.34 = (bf16[64,1024]{1,0:T(8,128)(2,1)S(1)}, bf16[64,1024]{1,0:T(8,128)(2,1)S(1)}, u32[]{:S(2)}, u32[]{:S(2)}) collective-permute-start(bf16[64,1024]{1,0:T(8,128)(2,1)S(1)} %shard_map.113.refs_0_), channel_id=1, source_target_pairs={{0,96},{32,64},{64,32},{96,0},{1,97},{33,65},{65,33},{97,1},{2,98}... | collective-permute-start | bytes 393224 | tf_op jit(solution)/shard_map/ppermute | solution.py:49
  183.6 0.3 collective-permute-done.32.refs_1_
  183.9 1.7 collective-permute-done.33.refs_2_
  185.5 1.4 collective-permute-done.34.refs_3_
  186.9 1.0 shard_map.114
  188.0 9.9 %collective-permute-start.35 = (f32[64,128]{1,0:T(8,128)S(1)}, f32[64,128]{1,0:T(8,128)S(1)}, u32[]{:S(2)}, u32[]{:S(2)}) collective-permute-start(f32[64,128]{1,0:T(8,128)S(1)} %get-tuple-element.33), channel_id=1, source_target_pairs={{0,1},{1,0},{2,3},{3,2},{4,5},{5,4},{6,7},{7,6},{8,9},{9,8},{10,11... | collective-permute-start | bytes 98312 | tf_op jit(solution)/shard_map/ppermute | solution.py:530
  197.9 0.9 collective-permute-done.35
  198.7 0.6 add_convert_fusion.1
  (59 shorter events, 1.5 us)
Async XLA Ops:
  0.6 1.0 copy-start.1
  2.5 34.7 %collective-permute-start = (bf16[2,32,2048]{2,1,0:T(8,128)(2,1)}, bf16[2,32,2048]{2,1,0:T(8,128)(2,1)S(1)}, u32[]{:S(2)}, u32[]{:S(2)}) collective-permute-start(bf16[2,32,2048]{2,1,0:T(8,128)(2,1)} %get-tuple-element.39), channel_id=1, source_target_pairs={{0,128},{128,0},{1,129},{129,1},{2,130},{130,2},{3,131},{131,3},{4... | collective-permute-start | bytes 786440 | tf_op jit(solution)/shard_map/ppermute | solution.py:366
  6.7 30.2 %collective-permute-start.4 = (bf16[128,512]{1,0:T(8,128)(2,1)S(1)}, bf16[128,512]{1,0:T(8,128)(2,1)S(1)}, u32[]{:S(2)}, u32[]{:S(2)}) collective-permute-start(bf16[128,512]{1,0:T(8,128)(2,1)S(1)} %own_half.1.refs_0_), channel_id=1, source_target_pairs={{0,2},{2,4},{4,6},{6,8},{8,10},{10,12},{12,14},{14,16},{16,18},{18... | collective-permute-start | bytes 393224 | tf_op jit(solution)/shard_map/ppermute | solution.py:421
  9.3 27.8 %collective-permute-start.5 = (bf16[128,512]{1,0:T(8,128)(2,1)S(1)}, bf16[128,512]{1,0:T(8,128)(2,1)S(1)}, u32[]{:S(2)}, u32[]{:S(2)}) collective-permute-start(bf16[128,512]{1,0:T(8,128)(2,1)S(1)} %own_half.1.refs_0_), channel_id=1, source_target_pairs={{0,30},{2,0},{4,2},{6,4},{8,6},{10,8},{12,10},{14,12},{16,14},{18,... | collective-permute-start | bytes 393224 | tf_op jit(solution)/shard_map/ppermute | solution.py:424
  32.1 21.5 %copy-start.4 = (s32[32]{0:T(128)S(1)}, s32[32]{0:T(128)}, u32[]{:S(2)}) copy-start(s32[32]{0:T(128)} %param.16) | copy-start | bytes 388
  32.1 16.5 %collective-permute-start.23 = (f32[64,1152]{1,0:T(8,128)S(1)}, f32[64,1152]{1,0:T(8,128)S(1)}, u32[]{:S(2)}, u32[]{:S(2)}) collective-permute-start(f32[64,1152]{1,0:T(8,128)S(1)} %get-tuple-element.25), channel_id=1, source_target_pairs={{0,32},{32,0},{64,96},{96,64},{1,33},{33,1},{65,97},{97,65},{2,34}... | collective-permute-start | bytes 884744 | tf_op jit(solution)/shard_map/ppermute | solution.py:49
  33.6 17.0 %collective-permute-start.24 = (f32[64,1152]{1,0:T(8,128)S(1)}, f32[64,1152]{1,0:T(8,128)S(1)}, u32[]{:S(2)}, u32[]{:S(2)}) collective-permute-start(f32[64,1152]{1,0:T(8,128)S(1)} %get-tuple-element.26), channel_id=1, source_target_pairs={{0,64},{32,96},{64,0},{96,32},{1,65},{33,97},{65,1},{97,33},{2,66}... | collective-permute-start | bytes 884744 | tf_op jit(solution)/shard_map/ppermute | solution.py:49
  36.9 16.8 %collective-permute-start.25 = (f32[64,1152]{1,0:T(8,128)S(1)}, f32[64,1152]{1,0:T(8,128)S(1)}, u32[]{:S(2)}, u32[]{:S(2)}) collective-permute-start(f32[64,1152]{1,0:T(8,128)S(1)} %get-tuple-element.27), channel_id=1, source_target_pairs={{0,96},{32,64},{64,32},{96,0},{1,97},{33,65},{65,33},{97,1},{2,98}... | collective-permute-start | bytes 884744 | tf_op jit(solution)/shard_map/ppermute | solution.py:49
  37.1 5.1 %collective-permute-start.6 = (bf16[128,512]{1,0:T(8,128)(2,1)S(1)}, bf16[128,512]{1,0:T(8,128)(2,1)S(1)}, u32[]{:S(2)}, u32[]{:S(2)}) collective-permute-start(bf16[128,512]{1,0:T(8,128)(2,1)S(1)} %collective-permute-done.4.refs_1_), channel_id=1, source_target_pairs={{0,2},{2,4},{4,6},{6,8},{8,10},{10,12},{12,14},{14,16},{16,18},{18... | collective-permute-start | bytes 393224 | tf_op jit(solution)/shard_map/ppermute | solution.py:421
  37.3 5.7 %collective-permute-start.7 = (bf16[128,512]{1,0:T(8,128)(2,1)S(1)}, bf16[128,512]{1,0:T(8,128)(2,1)S(1)}, u32[]{:S(2)}, u32[]{:S(2)}) collective-permute-start(bf16[128,512]{1,0:T(8,128)(2,1)S(1)} %collective-permute-done.5.refs_2_), channel_id=1, source_target_pairs={{0,30},{2,0},{4,2},{6,4},{8,6},{10,8},{12,10},{14,12},{16,14},{18,... | collective-permute-start | bytes 393224 | tf_op jit(solution)/shard_map/ppermute | solution.py:424
  42.2 11.4 %collective-permute-start.8 = (bf16[128,512]{1,0:T(8,128)(2,1)S(1)}, bf16[128,512]{1,0:T(8,128)(2,1)S(1)}, u32[]{:S(2)}, u32[]{:S(2)}) collective-permute-start(bf16[128,512]{1,0:T(8,128)(2,1)S(1)} %collective-permute-done.6.refs_3_), channel_id=1, source_target_pairs={{0,2},{2,4},{4,6},{6,8},{8,10},{10,12},{12,14},{14,16},{16,18},{18... | collective-permute-start | bytes 393224 | tf_op jit(solution)/shard_map/ppermute | solution.py:421
  43.0 19.6 %collective-permute-start.2 = (bf16[2,32,2048]{2,1,0:T(8,128)(2,1)}, bf16[2,32,2048]{2,1,0:T(8,128)(2,1)}, u32[]{:S(2)}, u32[]{:S(2)}) collective-permute-start(bf16[2,32,2048]{2,1,0:T(8,128)(2,1)} %get-tuple-element.37), channel_id=1, source_target_pairs={{0,32},{1,96},{32,0},{33,64},{64,33},{65,97},{96,1},{97,65},{2,34}... | collective-permute-start | bytes 786440 | tf_op jit(solution)/shard_map/ppermute | solution.py:384
  48.6 14.0 %collective-permute-start.1 = (bf16[2,32,2048]{2,1,0:T(8,128)(2,1)S(1)}, bf16[2,32,2048]{2,1,0:T(8,128)(2,1)S(1)}, u32[]{:S(2)}, u32[]{:S(2)}) collective-permute-start(bf16[2,32,2048]{2,1,0:T(8,128)(2,1)S(1)} %get-tuple-element.36), channel_id=1, source_target_pairs={{0,0},{1,64},{32,32},{33,96},{64,1},{65,65},{96,33},{97,97},{2,2},... | collective-permute-start | bytes 786440 | tf_op jit(solution)/shard_map/ppermute | solution.py:384
  50.5 9.5 %collective-permute-start.9 = (bf16[128,512]{1,0:T(8,128)(2,1)S(1)}, bf16[128,512]{1,0:T(8,128)(2,1)S(1)}, u32[]{:S(2)}, u32[]{:S(2)}) collective-permute-start(bf16[128,512]{1,0:T(8,128)(2,1)S(1)} %collective-permute-done.7.refs_4_), channel_id=1, source_target_pairs={{0,30},{2,0},{4,2},{6,4},{8,6},{10,8},{12,10},{14,12},{16,14},{18,... | collective-permute-start | bytes 393224 | tf_op jit(solution)/shard_map/ppermute | solution.py:424
  53.6 9.0 %collective-permute-start.10 = (bf16[128,512]{1,0:T(8,128)(2,1)S(1)}, bf16[128,512]{1,0:T(8,128)(2,1)S(1)}, u32[]{:S(2)}, u32[]{:S(2)}) collective-permute-start(bf16[128,512]{1,0:T(8,128)(2,1)S(1)} %collective-permute-done.8.refs_5_), channel_id=1, source_target_pairs={{0,2},{2,4},{4,6},{6,8},{8,10},{10,12},{12,14},{14,16},{16,18},{18... | collective-permute-start | bytes 393224 | tf_op jit(solution)/shard_map/ppermute | solution.py:421
  54.5 44.3 %all-to-all-start = ((f32[16,8,640]{2,1,0:T(8,128)}), f32[16,8,640]{2,1,0:T(8,128)S(1)}, u32[]{:S(2)}, u32[]{:S(2)}) async-start(f32[16,8,640]{2,1,0:T(8,128)} %shard_map.107), calls=%async_computation | async-start | bytes 655360 | tf_op jit(solution)/shard_map/all_to_all | solution.py:24
  60.1 19.0 %collective-permute-start.11 = (bf16[128,512]{1,0:T(8,128)(2,1)S(1)}, bf16[128,512]{1,0:T(8,128)(2,1)S(1)}, u32[]{:S(2)}, u32[]{:S(2)}) collective-permute-start(bf16[128,512]{1,0:T(8,128)(2,1)S(1)} %collective-permute-done.9.refs_6_), channel_id=1, source_target_pairs={{0,30},{2,0},{4,2},{6,4},{8,6},{10,8},{12,10},{14,12},{16,14},{18,... | collective-permute-start | bytes 393224 | tf_op jit(solution)/shard_map/ppermute | solution.py:424
  62.6 17.5 %collective-permute-start.12 = (bf16[128,512]{1,0:T(8,128)(2,1)S(1)}, bf16[128,512]{1,0:T(8,128)(2,1)S(1)}, u32[]{:S(2)}, u32[]{:S(2)}) collective-permute-start(bf16[128,512]{1,0:T(8,128)(2,1)S(1)} %collective-permute-done.10.refs_7_), channel_id=1, source_target_pairs={{0,2},{2,4},{4,6},{6,8},{8,10},{10,12},{12,14},{14,16},{16,18},{18... | collective-permute-start | bytes 393224 | tf_op jit(solution)/shard_map/ppermute | solution.py:421
  64.4 28.0 %collective-permute-start.3 = (bf16[2,2,32,2048]{3,2,1,0:T(8,128)(2,1)}, bf16[2,2,32,2048]{3,2,1,0:T(8,128)(2,1)S(1)}, u32[]{:S(2)}, u32[]{:S(2)}) collective-permute-start(bf16[2,2,32,2048]{3,2,1,0:T(8,128)(2,1)} %get-tuple-element.35), channel_id=1, source_target_pairs={{0,1},{1,0},{2,3},{3,2},{4,5},{5,4},{6,7},{7,6},{8,9},{9,8},{10,11... | collective-permute-start | bytes 1572872 | tf_op jit(solution)/shard_map/ppermute | solution.py:386
  79.1 5.2 %collective-permute-start.13 = (bf16[128,512]{1,0:T(8,128)(2,1)S(1)}, bf16[128,512]{1,0:T(8,128)(2,1)S(1)}, u32[]{:S(2)}, u32[]{:S(2)}) collective-permute-start(bf16[128,512]{1,0:T(8,128)(2,1)S(1)} %collective-permute-done.11.refs_8_), channel_id=1, source_target_pairs={{0,30},{2,0},{4,2},{6,4},{8,6},{10,8},{12,10},{14,12},{16,14},{18,... | collective-permute-start | bytes 393224 | tf_op jit(solution)/shard_map/ppermute | solution.py:424
  80.0 6.6 %collective-permute-start.14 = (bf16[128,512]{1,0:T(8,128)(2,1)S(1)}, bf16[128,512]{1,0:T(8,128)(2,1)S(1)}, u32[]{:S(2)}, u32[]{:S(2)}) collective-permute-start(bf16[128,512]{1,0:T(8,128)(2,1)S(1)} %collective-permute-done.12.refs_9_), channel_id=1, source_target_pairs={{0,2},{2,4},{4,6},{6,8},{8,10},{10,12},{12,14},{14,16},{16,18},{18... | collective-permute-start | bytes 393224 | tf_op jit(solution)/shard_map/ppermute | solution.py:421
  84.2 4.7 %collective-permute-start.15 = (bf16[128,512]{1,0:T(8,128)(2,1)S(1)}, bf16[128,512]{1,0:T(8,128)(2,1)S(1)}, u32[]{:S(2)}, u32[]{:S(2)}) collective-permute-start(bf16[128,512]{1,0:T(8,128)(2,1)S(1)} %collective-permute-done.13.refs_10_), channel_id=1, source_target_pairs={{0,30},{2,0},{4,2},{6,4},{8,6},{10,8},{12,10},{14,12},{16,14},{18,... | collective-permute-start | bytes 393224 | tf_op jit(solution)/shard_map/ppermute | solution.py:424
  86.6 5.8 %collective-permute-start.16 = (bf16[128,512]{1,0:T(8,128)(2,1)S(1)}, bf16[128,512]{1,0:T(8,128)(2,1)S(1)}, u32[]{:S(2)}, u32[]{:S(2)}) collective-permute-start(bf16[128,512]{1,0:T(8,128)(2,1)S(1)} %collective-permute-done.14.refs_11_), channel_id=1, source_target_pairs={{0,2},{2,4},{4,6},{6,8},{8,10},{10,12},{12,14},{14,16},{16,18},{18... | collective-permute-start | bytes 393224 | tf_op jit(solution)/shard_map/ppermute | solution.py:421
  88.9 5.4 %collective-permute-start.17 = (bf16[128,512]{1,0:T(8,128)(2,1)S(1)}, bf16[128,512]{1,0:T(8,128)(2,1)S(1)}, u32[]{:S(2)}, u32[]{:S(2)}) collective-permute-start(bf16[128,512]{1,0:T(8,128)(2,1)S(1)} %collective-permute-done.15.refs_12_), channel_id=1, source_target_pairs={{0,30},{2,0},{4,2},{6,4},{8,6},{10,8},{12,10},{14,12},{16,14},{18,... | collective-permute-start | bytes 393224 | tf_op jit(solution)/shard_map/ppermute | solution.py:424
  92.4 5.0 %collective-permute-start.18 = (bf16[128,512]{1,0:T(8,128)(2,1)S(1)}, bf16[128,512]{1,0:T(8,128)(2,1)S(1)}, u32[]{:S(2)}, u32[]{:S(2)}) collective-permute-start(bf16[128,512]{1,0:T(8,128)(2,1)S(1)} %collective-permute-done.16.refs_13_), channel_id=1, source_target_pairs={{0,2},{2,4},{4,6},{6,8},{8,10},{10,12},{12,14},{14,16},{16,18},{18... | collective-permute-start | bytes 393224 | tf_op jit(solution)/shard_map/ppermute | solution.py:421
  97.4 16.6 %copy-start.3 = (bf16[1024,2,128]{2,1,0:T(2,128)(2,1)S(1)}, bf16[1024,2,128]{2,1,0:T(2,128)(2,1)}, u32[]{:S(2)}) copy-start(bf16[1024,2,128]{2,1,0:T(2,128)(2,1)} %param.14) | copy-start | bytes 1572868
  98.7 11.3 %collective-permute-start.19 = (f32[4,32,512]{2,1,0:T(8,128)S(1)}, f32[4,32,512]{2,1,0:T(8,128)S(1)}, u32[]{:S(2)}, u32[]{:S(2)}) collective-permute-start(f32[4,32,512]{2,1,0:T(8,128)S(1)} %get-tuple-element.19), channel_id=1, source_target_pairs={{0,128},{128,0},{1,129},{129,1},{2,130},{130,2},{3,131},{131,3},{4... | collective-permute-start | bytes 786440 | tf_op jit(solution)/shard_map/ppermute | solution.py:366
  99.5 22.4 %all-to-all-start.1 = ((bf16[16,8,640]{2,1,0:T(8,128)(2,1)}), bf16[16,8,640]{2,1,0:T(8,128)(2,1)S(1)}, u32[]{:S(2)}, u32[]{:S(2)}) async-start(bf16[16,8,640]{2,1,0:T(8,128)(2,1)} %shard_map.108), calls=%async_computation.1 | async-start | bytes 327680 | tf_op jit(solution)/shard_map/all_to_all | solution.py:24
  110.1 12.2 %collective-permute-start.20 = (f32[32,512]{1,0:T(8,128)S(1)}, f32[32,512]{1,0:T(8,128)S(1)}, u32[]{:S(2)}, u32[]{:S(2)}) collective-permute-start(f32[32,512]{1,0:T(8,128)S(1)} %get-tuple-element.21), channel_id=1, source_target_pairs={{0,32},{32,0},{64,96},{96,64},{1,33},{33,1},{65,97},{97,65},{2,34}... | collective-permute-start | bytes 196616 | tf_op jit(solution)/shard_map/ppermute | solution.py:49
  110.2 15.7 %collective-permute-start.21 = (f32[32,512]{1,0:T(8,128)S(1)}, f32[32,512]{1,0:T(8,128)S(1)}, u32[]{:S(2)}, u32[]{:S(2)}) collective-permute-start(f32[32,512]{1,0:T(8,128)S(1)} %get-tuple-element.22), channel_id=1, source_target_pairs={{0,64},{32,96},{64,0},{96,32},{1,65},{33,97},{65,1},{97,33},{2,66}... | collective-permute-start | bytes 196616 | tf_op jit(solution)/shard_map/ppermute | solution.py:49
  110.3 15.5 %collective-permute-start.22 = (f32[32,512]{1,0:T(8,128)S(1)}, f32[32,512]{1,0:T(8,128)S(1)}, u32[]{:S(2)}, u32[]{:S(2)}) collective-permute-start(f32[32,512]{1,0:T(8,128)S(1)} %get-tuple-element.23), channel_id=1, source_target_pairs={{0,96},{32,64},{64,32},{96,0},{1,97},{33,65},{65,33},{97,1},{2,98}... | collective-permute-start | bytes 196616 | tf_op jit(solution)/shard_map/ppermute | solution.py:49
  121.9 65.1 %copy-start = (bf16[4096,256]{1,0:T(8,128)(2,1)S(1)}, bf16[4096,256]{1,0:T(8,128)(2,1)}, u32[]{:S(2)}) copy-start(bf16[4096,256]{1,0:T(8,128)(2,1)} %refs_4_.1) | copy-start | bytes 6291460
  121.9 4.4 %collective-permute-start.26 = (bf16[64,1152]{1,0:T(8,128)(2,1)S(1)}, bf16[64,1152]{1,0:T(8,128)(2,1)S(1)}, u32[]{:S(2)}, u32[]{:S(2)}) collective-permute-start(bf16[64,1152]{1,0:T(8,128)(2,1)S(1)} %shard_map.109.refs_0_), channel_id=1, source_target_pairs={{0,32},{32,0},{64,96},{96,64},{1,33},{33,1},{65,97},{97,65},{2,34}... | collective-permute-start | bytes 442376 | tf_op jit(solution)/shard_map/ppermute | solution.py:49
  122.0 6.0 %collective-permute-start.27 = (bf16[64,1152]{1,0:T(8,128)(2,1)S(1)}, bf16[64,1152]{1,0:T(8,128)(2,1)S(1)}, u32[]{:S(2)}, u32[]{:S(2)}) collective-permute-start(bf16[64,1152]{1,0:T(8,128)(2,1)S(1)} %shard_map.109.refs_0_), channel_id=1, source_target_pairs={{0,64},{32,96},{64,0},{96,32},{1,65},{33,97},{65,1},{97,33},{2,66}... | collective-permute-start | bytes 442376 | tf_op jit(solution)/shard_map/ppermute | solution.py:49
  122.2 7.0 %collective-permute-start.28 = (bf16[64,1152]{1,0:T(8,128)(2,1)S(1)}, bf16[64,1152]{1,0:T(8,128)(2,1)S(1)}, u32[]{:S(2)}, u32[]{:S(2)}) collective-permute-start(bf16[64,1152]{1,0:T(8,128)(2,1)S(1)} %shard_map.109.refs_0_), channel_id=1, source_target_pairs={{0,96},{32,64},{64,32},{96,0},{1,97},{33,65},{65,33},{97,1},{2,98}... | collective-permute-start | bytes 442376 | tf_op jit(solution)/shard_map/ppermute | solution.py:49
  125.9 62.1 %copy-start.2 = (bf16[32,512]{1,0:T(8,128)(2,1)}, bf16[32,512]{1,0:T(8,128)(2,1)S(1)}, u32[]{:S(2)}) copy-start(bf16[32,512]{1,0:T(8,128)(2,1)S(1)} %add_convert_fusion.refs_6_) | copy-start | bytes 98308
  134.7 4.1 %collective-permute-start.29 = (bf16[64,1152]{1,0:T(8,128)(2,1)S(1)}, bf16[64,1152]{1,0:T(8,128)(2,1)S(1)}, u32[]{:S(2)}, u32[]{:S(2)}) collective-permute-start(bf16[64,1152]{1,0:T(8,128)(2,1)S(1)} %get-tuple-element.29), channel_id=1, source_target_pairs={{0,32},{32,0},{64,96},{96,64},{1,33},{33,1},{65,97},{97,65},{2,34}... | collective-permute-start | bytes 442376 | tf_op jit(solution)/shard_map/ppermute | solution.py:49
  135.1 7.3 %collective-permute-start.30 = (bf16[64,1152]{1,0:T(8,128)(2,1)S(1)}, bf16[64,1152]{1,0:T(8,128)(2,1)S(1)}, u32[]{:S(2)}, u32[]{:S(2)}) collective-permute-start(bf16[64,1152]{1,0:T(8,128)(2,1)S(1)} %get-tuple-element.30), channel_id=1, source_target_pairs={{0,64},{32,96},{64,0},{96,32},{1,65},{33,97},{65,1},{97,33},{2,66}... | collective-permute-start | bytes 442376 | tf_op jit(solution)/shard_map/ppermute | solution.py:49
  138.3 5.7 %collective-permute-start.31 = (bf16[64,1152]{1,0:T(8,128)(2,1)S(1)}, bf16[64,1152]{1,0:T(8,128)(2,1)S(1)}, u32[]{:S(2)}, u32[]{:S(2)}) collective-permute-start(bf16[64,1152]{1,0:T(8,128)(2,1)S(1)} %get-tuple-element.31), channel_id=1, source_target_pairs={{0,96},{32,64},{64,32},{96,0},{1,97},{33,65},{65,33},{97,1},{2,98}... | collective-permute-start | bytes 442376 | tf_op jit(solution)/shard_map/ppermute | solution.py:49
  179.7 4.2 %collective-permute-start.32 = (bf16[64,1024]{1,0:T(8,128)(2,1)S(1)}, bf16[64,1024]{1,0:T(8,128)(2,1)S(1)}, u32[]{:S(2)}, u32[]{:S(2)}) collective-permute-start(bf16[64,1024]{1,0:T(8,128)(2,1)S(1)} %shard_map.113.refs_0_), channel_id=1, source_target_pairs={{0,32},{32,0},{64,96},{96,64},{1,33},{33,1},{65,97},{97,65},{2,34}... | collective-permute-start | bytes 393224 | tf_op jit(solution)/shard_map/ppermute | solution.py:49
  179.8 5.7 %collective-permute-start.33 = (bf16[64,1024]{1,0:T(8,128)(2,1)S(1)}, bf16[64,1024]{1,0:T(8,128)(2,1)S(1)}, u32[]{:S(2)}, u32[]{:S(2)}) collective-permute-start(bf16[64,1024]{1,0:T(8,128)(2,1)S(1)} %shard_map.113.refs_0_), channel_id=1, source_target_pairs={{0,64},{32,96},{64,0},{96,32},{1,65},{33,97},{65,1},{97,33},{2,66}... | collective-permute-start | bytes 393224 | tf_op jit(solution)/shard_map/ppermute | solution.py:49
  181.3 5.6 %collective-permute-start.34 = (bf16[64,1024]{1,0:T(8,128)(2,1)S(1)}, bf16[64,1024]{1,0:T(8,128)(2,1)S(1)}, u32[]{:S(2)}, u32[]{:S(2)}) collective-permute-start(bf16[64,1024]{1,0:T(8,128)(2,1)S(1)} %shard_map.113.refs_0_), channel_id=1, source_target_pairs={{0,96},{32,64},{64,32},{96,0},{1,97},{33,65},{65,33},{97,1},{2,98}... | collective-permute-start | bytes 393224 | tf_op jit(solution)/shard_map/ppermute | solution.py:49
  188.0 10.7 %collective-permute-start.35 = (f32[64,128]{1,0:T(8,128)S(1)}, f32[64,128]{1,0:T(8,128)S(1)}, u32[]{:S(2)}, u32[]{:S(2)}) collective-permute-start(f32[64,128]{1,0:T(8,128)S(1)} %get-tuple-element.33), channel_id=1, source_target_pairs={{0,1},{1,0},{2,3},{3,2},{4,5},{5,4},{6,7},{7,6},{8,9},{9,8},{10,11... | collective-permute-start | bytes 98312 | tf_op jit(solution)/shard_map/ppermute | solution.py:530

commit v7 on v6

--- a/solution.py
+++ b/solution.py
@@ -341,24 +341,35 @@
     return on_chip(body, outs, *attention, out_weight, place=place)
 
 
-def swapped_if(flag, x, axis):
-    return jnp.where(flag, jnp.flip(x, axis), x)
-
-
-def halves_of_blocks(span_tokens, places):
+def halves_of_blocks(place, span_tokens, places):
     tokens, width = span_tokens.shape
     block = width // (4 * places)
 
-    def body(in_ref, out_ref):
+    def body(place_ref, in_ref, own_ref, other_ref):
+        odd = place_ref[3] & 1
         for k in range(2):
-            for place in range(places):
-                for half in range(2):
-                    begin = ((k * places + place) * 2 + half) * block
-                    cut = slice(place * block, (place + 1) * block)
-                    out_ref[half, k, :, cut] = in_ref[:, begin : begin + block]
-
-    out = array((2, 2, tokens, places * block), BF16)
-    return on_chip(body, out, span_tokens)
+            for spot in range(places):
+                first = (k * places + spot) * 2
+                cut = slice(spot * block, (spot + 1) * block)
+                for out_ref, half in ((own_ref, odd), (other_ref, 1 - odd)):
+                    begin = pl.multiple_of((first + half) * block, block)
+                    out_ref[k, :, cut] = in_ref[:, pl.ds(begin, block)]
+
+    outs = [array((2, tokens, places * block), BF16)] * 2
+    return on_chip(body, outs, span_tokens, place=place)
+
+
+def by_parity(place, own, received):
+    _, tokens, depth = own.shape
+
+    def body(place_ref, own_ref, received_ref, *outs):
+        for i in range(2):
+            k = (place_ref[0] & 1) ^ i
+            outs[i][0] = own_ref[k]
+            outs[i][1] = received_ref[k]
+
+    outs = [array((2, tokens, depth), BF16)] * 2
+    return on_chip(body, outs, own, received, place=place)
 
 
 def with_neighbour(x):
@@ -366,26 +377,21 @@
     return lax.ppermute(x, "groups", [(g, g ^ 1) for g in range(count)])
 
 
-def tokens_by_features(span_tokens, depth):
+def tokens_by_features(place, span_tokens):
     xs, zs = (lax.axis_size(a) for a in ("x", "z"))
-    tokens = span_tokens.shape[0]
-    group, x, core = (lax.axis_index(a) for a in ("groups", "x", "width"))
-    odd = (group & 1) == 1
-    pieces = halves_of_blocks(span_tokens, zs)
-    received = with_neighbour(jnp.where(odd, pieces[0], pieces[1]))
-    both = jnp.stack([jnp.where(odd, pieces[1], pieces[0]), received], axis=1)
-    both = swapped_if((x & 1) == 1, both, 0)
+    own, other = halves_of_blocks(place, span_tokens, zs)
+    received = with_neighbour(other)
     mine = []
-    for i in range(2):
+    for i, piece in enumerate(by_parity(place, own, received)):
         pairs = []
         for a in range(xs):
             for w in range(2):
                 pairs.append((a * 2 + w, (2 * w + ((a & 1) ^ i)) * 2 + (a >> 1)))
-        mine.append(lax.ppermute(both[i], ("x", "width"), pairs))
-    mine = jnp.stack(mine)
-    theirs = lax.ppermute(mine, "width", [(0, 1), (1, 0)])
-    ready = jnp.stack([mine, theirs])
-    return swapped_if((core ^ (x >> 1)) == 1, ready, 0).reshape(xs, 2, tokens, depth)
+        mine.append(lax.ppermute(piece, ("x", "width"), pairs))
+    theirs = []
+    for i in range(2):
+        theirs.append(lax.ppermute(mine[i], "width", [(0, 1), (1, 0)]))
+    return mine + theirs
 
 
 def own_half(place, kv_weight):
@@ -427,7 +433,8 @@
 
 
 def span_dot(place, ready, blocks):
-    xs, groups, tokens, depth = ready.shape
+    groups, tokens, _ = ready[0].shape
+    count = len(ready)
     zs = len(blocks)
     block, width = blocks[0].shape
     offsets = [0]
@@ -435,27 +442,33 @@
         offsets += [zs - s, s]
     offsets = offsets[:zs]
 
-    def body(place_ref, ready_ref, *refs):
-        home_ref, away_ref = refs[zs:]
+    def body(place_ref, *refs):
+        tokens_refs = refs[:count]
+        block_refs = refs[count : count + zs]
+        home_ref, away_ref = refs[count + zs :]
 
         def features(i):
             begin = lax.rem(place_ref[2] + offsets[i], zs) * block
-            return ready_ref[:, pl.ds(pl.multiple_of(begin, block), block)]
+            cut = pl.ds(pl.multiple_of(begin, block), block)
+            return jnp.concatenate(
+                [ref[o, :, cut] for ref in tokens_refs for o in range(groups)], axis=0
+            )
 
         total = None
         for i in range(0, zs, 2):
             left = jnp.concatenate([features(i), features(i + 1)], axis=1)
-            right = jnp.concatenate([refs[i][...], refs[i + 1][...]], axis=0)
+            right = jnp.concatenate([block_refs[i][...], block_refs[i + 1][...]], axis=0)
             more = dot_f32(left, right)
             total = more if total is None else total + more
-        for m in range(xs):
-            begin = m * groups * tokens
+        turned = place_ref[1] ^ (place_ref[0] >> 1)
+        for n in range(count):
+            m = 2 * ((n >> 1) ^ turned) + (n & 1)
+            begin = n * groups * tokens
             home_ref[m] = total[begin : begin + tokens]
             away_ref[m] = total[begin + tokens : begin + 2 * tokens]
 
-    flat = ready.reshape(xs * groups * tokens, depth)
-    outs = [array((xs, tokens, width), F32)] * 2
-    return on_chip(body, outs, flat, *blocks, place=place)
+    outs = [array((count, tokens, width), F32)] * 2
+    return on_chip(body, outs, *ready, *blocks, place=place)
 
 
 def added_at_home(home, away):
@@ -509,7 +522,7 @@
     blocks = gathered_over_z(own_half(place, kv_weight))
     partial = project(place, hidden.reshape(rows, depth), query_weight, kv_weight, xs)
     partial = exchanged_over_x(partial)
-    ready = tokens_by_features(span_tokens, zs * blocks[0].shape[0])
+    ready = tokens_by_features(place, span_tokens)
     partial = add_over_x(partial, zs)
     partial = exchanged(partial, "z")
     own = add_over_z(partial)

time: 200 us -> 209 us (1.045)
  blocking collectives: 34.8 us -> 41.2 us
  waiting for transfers between devices: 46.8 us -> 42.9 us
  local copies, waits for them, and re-layouts: 3.2 us -> 6.7 us
  starting transfers between devices: 94.2 us -> 97.7 us
    all_to_all x2, starting transfers between devices: 16 us -> 24.8 us  [exchanged(): return lax.all_to_all(pieces, axis, split_axis=0, concat_axis=0, tiled=True)]
    all_to_all x2, blocking collectives: 34.8 us -> 41.2 us  [exchanged(): return lax.all_to_all(pieces, axis, split_axis=0, concat_axis=0, tiled=True)]
    ppermute x7, waiting for transfers between devices: 21.9 us -> 17.2 us  [gathered_over_z(): above = lax.ppermute(above, 'z', down)]
    ppermute x1, starting transfers between devices: 9.88 us -> 5.2 us  [local(): lax.ppermute(send, 'width', [(0, 1), (1, 0)])]
    ppermute x3 -> x4, waiting for transfers between devices: 0.01 us -> 3.48 us  [the longest x2 3.47 us: tokens_by_features(): mine.append(lax.ppermute(piece, ('x', 'width'), pairs))]
    ppermute x8, waiting for transfers between devices: 5.41 us -> 2.36 us  [gathered_over_z(): below = lax.ppermute(below, 'z', up)]
    pallas_call x11 -> x12, Pallas kernels: 10.1 us -> 12.1 us  [on_chip(): pl.pallas_call(body, in_specs=specs, out_shape=shapes, scratch_shapes=scr...]
    ppermute x3 -> x4, starting transfers between devices: 7.52 us -> 6.01 us  [the longest x2 5.33 us: tokens_by_features(): mine.append(lax.ppermute(piece, ('x', 'width'), pairs))]
  transfers between devices with their start and end apart: 38 -> 39, of which waited for: 18 -> 16; matrix products, arithmetic and copies ran while one was open for 2% -> 2% of each run, Pallas kernels for 4% -> 4%
where the time goes in v7:
time: 209 us
  starting transfers between devices  97.7 us (47%)
  waiting for transfers between devices  42.9 us (21%)
  blocking collectives  41.2 us (20%)
  Pallas kernels  16.5 us (8%)
  local copies, waits for them, and re-layouts  6.7 us (3%)
  other arithmetic  2.16 us (1%)
    all_to_all x2, blocking collectives, exchanged(): return lax.all_to_all(pieces, axis, split_axis=0, concat_axis=0, tiled=True)  41.2 us
    ppermute x7, starting transfers between devices, gathered_over_z(): above = lax.ppermute(above, 'z', down)  34.7 us
    all_to_all x2, starting transfers between devices, exchanged(): return lax.all_to_all(pieces, axis, split_axis=0, concat_axis=0, tiled=True)  24.8 us
    ppermute x15, starting transfers between devices, exchanged_over_x(): received.append(lax.ppermute(pieces[mask], 'x', pairs))  20.1 us
    ppermute x7, waiting for transfers between devices, gathered_over_z(): above = lax.ppermute(above, 'z', down)  17.2 us
    pallas_call x12, Pallas kernels, on_chip(): pl.pallas_call(body, in_specs=specs, out_shape=shapes, scratch_shapes=scr...  12.1 us
    ppermute x15, waiting for transfers between devices, exchanged_over_x(): received.append(lax.ppermute(pieces[mask], 'x', pairs))  11.7 us
    all_to_all x2, waiting for transfers between devices, exchanged(): return lax.all_to_all(pieces, axis, split_axis=0, concat_axis=0, tiled=True)  6.52 us
  transfers between devices with their start and end apart: 39, of which 16 were waited for; matrix products, arithmetic and copies ran while one was open for 2% of the time, Pallas kernels for 4%

profile of v7, /device:TPU:33, one launch (start us, length us, event | category | flops | bytes accessed | tf_op | source)
XLA Modules:
  0.0 208.8 jit_solution(2711845488351880354)
XLA Ops:
  0.7 1.5 own_half.1.refs_4_
  2.2 3.4 %collective-permute-start.5 = (bf16[128,512]{1,0:T(8,128)(2,1)S(1)}, bf16[128,512]{1,0:T(8,128)(2,1)S(1)}, u32[]{:S(2)}, u32[]{:S(2)}) collective-permute-start(bf16[128,512]{1,0:T(8,128)(2,1)S(1)} %own_half.1.refs_4_), channel_id=1, source_target_pairs={{0,2},{2,4},{4,6},{6,8},{8,10},{10,12},{12,14},{14,16},{16,18},{18... | collective-permute-start | bytes 393224 | tf_op jit(solution)/shard_map/ppermute | solution.py:427
  5.6 3.0 %project.1 = (f32[64,1152]{1,0:T(8,128)S(1)}, f32[64,1152]{1,0:T(8,128)S(1)}, f32[64,1152]{1,0:T(8,128)S(1)}, f32[64,1152]{1,0:T(8,128)S(1)}) custom-call(s32[4]{0:T(128)S(1)} %pad_add_fusion.place_ref, bf16[64,256]{1,0:T(8,128)(2,1)} %bitcast.12, bf16[256,4096]{1,0:T(8,128)(2,1)} %query_hbm.1, bf16[256,512]{1,0:T(8,128)(2,1)} %fresh_hbm.1), custom_call_target="tpu_custom_call" | custom-call | tf_op jit(solution)/shard_map/project/pallas_call | solution.py:88
  8.6 1.5 collective-permute-start.24
  10.1 2.7 %collective-permute-start.25 = (f32[64,1152]{1,0:T(8,128)S(1)}, f32[64,1152]{1,0:T(8,128)S(1)}, u32[]{:S(2)}, u32[]{:S(2)}) collective-permute-start(f32[64,1152]{1,0:T(8,128)S(1)} %get-tuple-element.34), channel_id=1, source_target_pairs={{0,64},{32,96},{64,0},{96,32},{1,65},{33,97},{65,1},{97,33},{2,66}... | collective-permute-start | bytes 884744 | tf_op jit(solution)/shard_map/ppermute | solution.py:49
  12.8 19.6 %collective-permute-start.6 = (bf16[128,512]{1,0:T(8,128)(2,1)S(1)}, bf16[128,512]{1,0:T(8,128)(2,1)S(1)}, u32[]{:S(2)}, u32[]{:S(2)}) collective-permute-start(bf16[128,512]{1,0:T(8,128)(2,1)S(1)} %own_half.1.refs_4_), channel_id=1, source_target_pairs={{0,30},{2,0},{4,2},{6,4},{8,6},{10,8},{12,10},{14,12},{16,14},{18,... | collective-permute-start | bytes 393224 | tf_op jit(solution)/shard_map/ppermute | solution.py:430
  32.5 1.9 collective-permute-done.6.refs_6_
  34.4 3.1 %collective-permute-start.8 = (bf16[128,512]{1,0:T(8,128)(2,1)S(1)}, bf16[128,512]{1,0:T(8,128)(2,1)S(1)}, u32[]{:S(2)}, u32[]{:S(2)}) collective-permute-start(bf16[128,512]{1,0:T(8,128)(2,1)S(1)} %collective-permute-done.6.refs_6_), channel_id=1, source_target_pairs={{0,30},{2,0},{4,2},{6,4},{8,6},{10,8},{12,10},{14,12},{16,14},{18,... | collective-permute-start | bytes 393224 | tf_op jit(solution)/shard_map/ppermute | solution.py:430
  37.5 0.8 shard_map.108
  38.3 12.3 %all-to-all-start = ((f32[16,8,640]{2,1,0:T(8,128)}), f32[16,8,640]{2,1,0:T(8,128)S(1)}, u32[]{:S(2)}, u32[]{:S(2)}) async-start(f32[16,8,640]{2,1,0:T(8,128)} %shard_map.108), calls=%async_computation | async-start | bytes 655360 | tf_op jit(solution)/shard_map/all_to_all | solution.py:24
  50.7 2.5 %collective-permute-start.10 = (bf16[128,512]{1,0:T(8,128)(2,1)S(1)}, bf16[128,512]{1,0:T(8,128)(2,1)S(1)}, u32[]{:S(2)}, u32[]{:S(2)}) collective-permute-start(bf16[128,512]{1,0:T(8,128)(2,1)S(1)} %collective-permute-done.8.refs_8_), channel_id=1, source_target_pairs={{0,30},{2,0},{4,2},{6,4},{8,6},{10,8},{12,10},{14,12},{16,14},{18,... | collective-permute-start | bytes 393224 | tf_op jit(solution)/shard_map/ppermute | solution.py:430
  53.2 15.2 %collective-permute-done.10.refs_10_ = bf16[128,512]{1,0:T(8,128)(2,1)S(1)} collective-permute-done((bf16[128,512]{1,0:T(8,128)(2,1)S(1)}, bf16[128,512]{1,0:T(8,128)(2,1)S(1)}, u32[]{:S(2)}, u32[]{:S(2)}) %collective-permute-start.10) | collective-permute-done | bytes 131104 | tf_op jit(solution)/shard_map/ppermute | solution.py:430
  68.4 1.4 collective-permute-start.12
  69.9 0.7 shard_map.104
  70.5 2.0 collective-permute-start
  73.2 2.8 %collective-permute-start.14 = (bf16[128,512]{1,0:T(8,128)(2,1)S(1)}, bf16[128,512]{1,0:T(8,128)(2,1)S(1)}, u32[]{:S(2)}, u32[]{:S(2)}) collective-permute-start(bf16[128,512]{1,0:T(8,128)(2,1)S(1)} %collective-permute-done.12.refs_12_), channel_id=1, source_target_pairs={{0,30},{2,0},{4,2},{6,4},{8,6},{10,8},{12,10},{14,12},{16,14},{18,... | collective-permute-start | bytes 393224 | tf_op jit(solution)/shard_map/ppermute | solution.py:430
  76.0 0.7 collective-permute-done.received_ref
  76.7 0.6 shard_map.105
  77.3 3.5 %collective-permute-start.1 = (bf16[2,32,2048]{2,1,0:T(8,128)(2,1)S(1)}, bf16[2,32,2048]{2,1,0:T(8,128)(2,1)S(1)}, u32[]{:S(2)}, u32[]{:S(2)}) collective-permute-start(bf16[2,32,2048]{2,1,0:T(8,128)(2,1)S(1)} %get-tuple-element.24), channel_id=1, source_target_pairs={{0,0},{1,64},{32,32},{33,96},{64,1},{65,65},{96,33},{97,97},{2,2},... | collective-permute-start | bytes 786440 | tf_op jit(solution)/shard_map/ppermute | solution.py:390
  80.8 1.9 collective-permute-start.2
  82.7 2.7 %collective-permute-start.16 = (bf16[128,512]{1,0:T(8,128)(2,1)S(1)}, bf16[128,512]{1,0:T(8,128)(2,1)S(1)}, u32[]{:S(2)}, u32[]{:S(2)}) collective-permute-start(bf16[128,512]{1,0:T(8,128)(2,1)S(1)} %collective-permute-done.14.refs_14_), channel_id=1, source_target_pairs={{0,30},{2,0},{4,2},{6,4},{8,6},{10,8},{12,10},{14,12},{16,14},{18,... | collective-permute-start | bytes 393224 | tf_op jit(solution)/shard_map/ppermute | solution.py:430
  85.4 0.7 broadcast_compare_fusion
  86.1 0.5 collective-permute-done.1.refs_0_
  86.6 3.0 %collective-permute-done.2.refs_1_ = bf16[2,32,2048]{2,1,0:T(8,128)(2,1)S(1)} collective-permute-done((bf16[2,32,2048]{2,1,0:T(8,128)(2,1)S(1)}, bf16[2,32,2048]{2,1,0:T(8,128)(2,1)S(1)}, u32[]{:S(2)}, u32[]{:S(2)}) %collective-permute-start.2) | collective-permute-done | bytes 262176 | tf_op jit(solution)/shard_map/ppermute | solution.py:390
  89.6 0.7 collective-permute-start.4
  90.3 2.6 %collective-permute-start.18 = (bf16[128,512]{1,0:T(8,128)(2,1)S(1)}, bf16[128,512]{1,0:T(8,128)(2,1)S(1)}, u32[]{:S(2)}, u32[]{:S(2)}) collective-permute-start(bf16[128,512]{1,0:T(8,128)(2,1)S(1)} %collective-permute-done.16.refs_16_), channel_id=1, source_target_pairs={{0,30},{2,0},{4,2},{6,4},{8,6},{10,8},{12,10},{14,12},{16,14},{18,... | collective-permute-start | bytes 393224 | tf_op jit(solution)/shard_map/ppermute | solution.py:430
  93.0 0.7 fusion.1
  93.6 0.6 broadcast_in_dim.19
  94.2 0.6 broadcast_in_dim.20
  94.8 1.0 concatenate.3
  95.8 0.6 copy-done.3
  96.5 2.3 %collective-permute-done.19.refs_19_ = bf16[128,512]{1,0:T(8,128)(2,1)S(1)} collective-permute-done((bf16[128,512]{1,0:T(8,128)(2,1)S(1)}, bf16[128,512]{1,0:T(8,128)(2,1)S(1)}, u32[]{:S(2)}, u32[]{:S(2)}) %collective-permute-start.19) | collective-permute-done | bytes 131104 | tf_op jit(solution)/shard_map/ppermute | solution.py:427
  98.8 0.7 copy-done.5
  99.5 0.9 copy-done.4
  100.4 0.9 copy-done.6
  101.3 2.0 shard_map.106
  103.3 1.5 collective-permute-start.20
  104.7 0.7 shard_map.109
  105.5 12.5 %all-to-all-start.1 = ((bf16[16,8,640]{2,1,0:T(8,128)(2,1)}), bf16[16,8,640]{2,1,0:T(8,128)(2,1)S(1)}, u32[]{:S(2)}, u32[]{:S(2)}) async-start(bf16[16,8,640]{2,1,0:T(8,128)(2,1)} %shard_map.109), calls=%async_computation.1 | async-start | bytes 327680 | tf_op jit(solution)/shard_map/all_to_all | solution.py:24
  118.2 3.5 %collective-permute-start.22 = (f32[32,512]{1,0:T(8,128)S(1)}, f32[32,512]{1,0:T(8,128)S(1)}, u32[]{:S(2)}, u32[]{:S(2)}) collective-permute-start(f32[32,512]{1,0:T(8,128)S(1)} %get-tuple-element.30), channel_id=1, source_target_pairs={{0,64},{32,96},{64,0},{96,32},{1,65},{33,97},{65,1},{97,33},{2,66}... | collective-permute-start | bytes 196616 | tf_op jit(solution)/shard_map/ppermute | solution.py:49
  121.7 0.3 collective-permute-start.23
  122.0 1.3 copy_bitcast_fusion
  123.4 6.5 %all-to-all-done.1.in_ref = bf16[16,8,640]{2,1,0:T(8,128)(2,1)S(1)} async-done(((bf16[16,8,640]{2,1,0:T(8,128)(2,1)}), bf16[16,8,640]{2,1,0:T(8,128)(2,1)S(1)}, u32[]{:S(2)}, u32[]{:S(2)}) %all-to-all-start.1) | async-done | bytes 163872 | tf_op jit(solution)/shard_map/all_to_all | solution.py:24
  130.0 3.5 %collective-permute-start.28 = (bf16[64,1152]{1,0:T(8,128)(2,1)S(1)}, bf16[64,1152]{1,0:T(8,128)(2,1)S(1)}, u32[]{:S(2)}, u32[]{:S(2)}) collective-permute-start(bf16[64,1152]{1,0:T(8,128)(2,1)S(1)} %shard_map.110.refs_0_), channel_id=1, source_target_pairs={{0,64},{32,96},{64,0},{96,32},{1,65},{33,97},{65,1},{97,33},{2,66}... | collective-permute-start | bytes 442376 | tf_op jit(solution)/shard_map/ppermute | solution.py:49
  133.6 0.3 collective-permute-start.29
  133.9 0.2 collective-permute-done.27.refs_1_
  134.2 3.6 %collective-permute-done.28.refs_2_ = bf16[64,1152]{1,0:T(8,128)(2,1)S(1)} collective-permute-done((bf16[64,1152]{1,0:T(8,128)(2,1)S(1)}, bf16[64,1152]{1,0:T(8,128)(2,1)S(1)}, u32[]{:S(2)}, u32[]{:S(2)}) %collective-permute-start.28) | collective-permute-done | bytes 147488 | tf_op jit(solution)/shard_map/ppermute | solution.py:49
  137.7 1.5 collective-permute-done.29.refs_3_
  139.3 5.4 %shard_map.111 = (bf16[64,1152]{1,0:T(8,128)(2,1)S(1)}, bf16[64,1152]{1,0:T(8,128)(2,1)S(1)}, bf16[64,1152]{1,0:T(8,128)(2,1)S(1)}, bf16[64,1152]{1,0:T(8,128)(2,1)S(1)}) custom-call(s32[4]{0:T(128)S(1)} %pad_add_fusion.place_ref, bf16[64,1152]{1,0:T(8,128)(2,1)S(1)} %shard_map.110.refs_0_, bf16[64,1152]{1,0:T(8,128)(2,1)S(1)} %collective-permute-done.27.refs_1_, ...), custom_call_target="tpu_custom_call" | custom-call | tf_op jit(solution)/shard_map/pallas_call | solution.py:39
  144.8 1.5 collective-permute-start.31
  146.3 2.3 %collective-permute-start.32 = (bf16[64,1152]{1,0:T(8,128)(2,1)S(1)}, bf16[64,1152]{1,0:T(8,128)(2,1)S(1)}, u32[]{:S(2)}, u32[]{:S(2)}) collective-permute-start(bf16[64,1152]{1,0:T(8,128)(2,1)S(1)} %get-tuple-element.39), channel_id=1, source_target_pairs={{0,96},{32,64},{64,32},{96,0},{1,97},{33,65},{65,33},{97,1},{2,98}... | collective-permute-start | bytes 442376 | tf_op jit(solution)/shard_map/ppermute | solution.py:49
  148.8 1.7 collective-permute-done.31.refs_2_
  150.5 1.5 collective-permute-done.32.refs_3_
  152.0 0.6 shard_map.112
  152.6 22.4 %all_to_all.20.in_ref = bf16[16,8,640]{2,1,0:T(8,128)(2,1)S(1)} all-to-all(bf16[16,8,640]{2,1,0:T(8,128)(2,1)S(1)} %shard_map.112), channel_id=1, replica_groups=mesh['groups'=2,'x'=4,'z'=16,'width'=2] {'z'}, dimensions={0} | all-to-all | bytes 327680 | tf_op jit(solution)/shard_map/all_to_all | solution.py:24
  175.0 0.3 shard_map.113
  175.3 18.8 %all_to_all.21.in_ref = bf16[16,8,512]{2,1,0:T(8,128)(2,1)S(1)} all-to-all(bf16[16,8,512]{2,1,0:T(8,128)(2,1)S(1)} %shard_map.113), channel_id=1, replica_groups=mesh['groups'=2,'x'=4,'z'=16,'width'=2] {'z'}, dimensions={0} | all-to-all | bytes 262144 | tf_op jit(solution)/shard_map/all_to_all | solution.py:24
  194.4 3.7 %collective-permute-start.35 = (bf16[64,1024]{1,0:T(8,128)(2,1)S(1)}, bf16[64,1024]{1,0:T(8,128)(2,1)S(1)}, u32[]{:S(2)}, u32[]{:S(2)}) collective-permute-start(bf16[64,1024]{1,0:T(8,128)(2,1)S(1)} %shard_map.114.refs_0_), channel_id=1, source_target_pairs={{0,96},{32,64},{64,32},{96,0},{1,97},{33,65},{65,33},{97,1},{2,98}... | collective-permute-start | bytes 393224 | tf_op jit(solution)/shard_map/ppermute | solution.py:49
  198.0 1.7 collective-permute-done.34.refs_2_
  199.7 1.3 collective-permute-done.35.refs_3_
  201.1 1.0 shard_map.115
  202.1 5.2 %collective-permute-start.36 = (f32[64,128]{1,0:T(8,128)S(1)}, f32[64,128]{1,0:T(8,128)S(1)}, u32[]{:S(2)}, u32[]{:S(2)}) collective-permute-start(f32[64,128]{1,0:T(8,128)S(1)} %get-tuple-element.41), channel_id=1, source_target_pairs={{0,1},{1,0},{2,3},{3,2},{4,5},{5,4},{6,7},{7,6},{8,9},{9,8},{10,11... | collective-permute-start | bytes 98312 | tf_op jit(solution)/shard_map/ppermute | solution.py:543
  207.3 0.9 collective-permute-done.36
  208.2 0.6 add_convert_fusion.1
  (61 shorter events, 1.3 us)
Async XLA Ops:
  2.2 30.3 %collective-permute-start.5 = (bf16[128,512]{1,0:T(8,128)(2,1)S(1)}, bf16[128,512]{1,0:T(8,128)(2,1)S(1)}, u32[]{:S(2)}, u32[]{:S(2)}) collective-permute-start(bf16[128,512]{1,0:T(8,128)(2,1)S(1)} %own_half.1.refs_4_), channel_id=1, source_target_pairs={{0,2},{2,4},{4,6},{6,8},{8,10},{10,12},{12,14},{14,16},{16,18},{18... | collective-permute-start | bytes 393224 | tf_op jit(solution)/shard_map/ppermute | solution.py:427
  5.6 64.2 %copy-start.1 = (bf16[32,8192]{1,0:T(8,128)(2,1)S(1)}, bf16[32,8192]{1,0:T(8,128)(2,1)}, u32[]{:S(2)}) copy-start(bf16[32,8192]{1,0:T(8,128)(2,1)} %in_ref.1) | copy-start | bytes 1572868
  5.6 70.3 %copy-start.7 = (s32[32]{0:T(128)S(1)}, s32[32]{0:T(128)}, u32[]{:S(2)}) copy-start(s32[32]{0:T(128)} %param.16) | copy-start | bytes 388
  8.6 28.9 %collective-permute-start.24 = (f32[64,1152]{1,0:T(8,128)S(1)}, f32[64,1152]{1,0:T(8,128)S(1)}, u32[]{:S(2)}, u32[]{:S(2)}) collective-permute-start(f32[64,1152]{1,0:T(8,128)S(1)} %get-tuple-element.33), channel_id=1, source_target_pairs={{0,32},{32,0},{64,96},{96,64},{1,33},{33,1},{65,97},{97,65},{2,34}... | collective-permute-start | bytes 884744 | tf_op jit(solution)/shard_map/ppermute | solution.py:49
  10.1 27.4 %collective-permute-start.25 = (f32[64,1152]{1,0:T(8,128)S(1)}, f32[64,1152]{1,0:T(8,128)S(1)}, u32[]{:S(2)}, u32[]{:S(2)}) collective-permute-start(f32[64,1152]{1,0:T(8,128)S(1)} %get-tuple-element.34), channel_id=1, source_target_pairs={{0,64},{32,96},{64,0},{96,32},{1,65},{33,97},{65,1},{97,33},{2,66}... | collective-permute-start | bytes 884744 | tf_op jit(solution)/shard_map/ppermute | solution.py:49
  12.8 24.7 %collective-permute-start.26 = (f32[64,1152]{1,0:T(8,128)S(1)}, f32[64,1152]{1,0:T(8,128)S(1)}, u32[]{:S(2)}, u32[]{:S(2)}) collective-permute-start(f32[64,1152]{1,0:T(8,128)S(1)} %get-tuple-element.35), channel_id=1, source_target_pairs={{0,96},{32,64},{64,32},{96,0},{1,97},{33,65},{65,33},{97,1},{2,98}... | collective-permute-start | bytes 884744 | tf_op jit(solution)/shard_map/ppermute | solution.py:49
  12.8 21.6 %collective-permute-start.6 = (bf16[128,512]{1,0:T(8,128)(2,1)S(1)}, bf16[128,512]{1,0:T(8,128)(2,1)S(1)}, u32[]{:S(2)}, u32[]{:S(2)}) collective-permute-start(bf16[128,512]{1,0:T(8,128)(2,1)S(1)} %own_half.1.refs_4_), channel_id=1, source_target_pairs={{0,30},{2,0},{4,2},{6,4},{8,6},{10,8},{12,10},{14,12},{16,14},{18,... | collective-permute-start | bytes 393224 | tf_op jit(solution)/shard_map/ppermute | solution.py:430
  32.5 5.0 %collective-permute-start.7 = (bf16[128,512]{1,0:T(8,128)(2,1)S(1)}, bf16[128,512]{1,0:T(8,128)(2,1)S(1)}, u32[]{:S(2)}, u32[]{:S(2)}) collective-permute-start(bf16[128,512]{1,0:T(8,128)(2,1)S(1)} %collective-permute-done.5.refs_5_), channel_id=1, source_target_pairs={{0,2},{2,4},{4,6},{6,8},{8,10},{10,12},{12,14},{14,16},{16,18},{18... | collective-permute-start | bytes 393224 | tf_op jit(solution)/shard_map/ppermute | solution.py:427
  34.4 16.2 %collective-permute-start.8 = (bf16[128,512]{1,0:T(8,128)(2,1)S(1)}, bf16[128,512]{1,0:T(8,128)(2,1)S(1)}, u32[]{:S(2)}, u32[]{:S(2)}) collective-permute-start(bf16[128,512]{1,0:T(8,128)(2,1)S(1)} %collective-permute-done.6.refs_6_), channel_id=1, source_target_pairs={{0,30},{2,0},{4,2},{6,4},{8,6},{10,8},{12,10},{14,12},{16,14},{18,... | collective-permute-start | bytes 393224 | tf_op jit(solution)/shard_map/ppermute | solution.py:430
  37.5 15.6 %collective-permute-start.9 = (bf16[128,512]{1,0:T(8,128)(2,1)S(1)}, bf16[128,512]{1,0:T(8,128)(2,1)S(1)}, u32[]{:S(2)}, u32[]{:S(2)}) collective-permute-start(bf16[128,512]{1,0:T(8,128)(2,1)S(1)} %collective-permute-done.7.refs_7_), channel_id=1, source_target_pairs={{0,2},{2,4},{4,6},{6,8},{8,10},{10,12},{12,14},{14,16},{16,18},{18... | collective-permute-start | bytes 393224 | tf_op jit(solution)/shard_map/ppermute | solution.py:427
  38.3 66.4 %all-to-all-start = ((f32[16,8,640]{2,1,0:T(8,128)}), f32[16,8,640]{2,1,0:T(8,128)S(1)}, u32[]{:S(2)}, u32[]{:S(2)}) async-start(f32[16,8,640]{2,1,0:T(8,128)} %shard_map.108), calls=%async_computation | async-start | bytes 655360 | tf_op jit(solution)/shard_map/all_to_all | solution.py:24
  50.7 17.7 %collective-permute-start.10 = (bf16[128,512]{1,0:T(8,128)(2,1)S(1)}, bf16[128,512]{1,0:T(8,128)(2,1)S(1)}, u32[]{:S(2)}, u32[]{:S(2)}) collective-permute-start(bf16[128,512]{1,0:T(8,128)(2,1)S(1)} %collective-permute-done.8.refs_8_), channel_id=1, source_target_pairs={{0,30},{2,0},{4,2},{6,4},{8,6},{10,8},{12,10},{14,12},{16,14},{18,... | collective-permute-start | bytes 393224 | tf_op jit(solution)/shard_map/ppermute | solution.py:430
  53.1 16.7 %collective-permute-start.11 = (bf16[128,512]{1,0:T(8,128)(2,1)S(1)}, bf16[128,512]{1,0:T(8,128)(2,1)S(1)}, u32[]{:S(2)}, u32[]{:S(2)}) collective-permute-start(bf16[128,512]{1,0:T(8,128)(2,1)S(1)} %collective-permute-done.9.refs_9_), channel_id=1, source_target_pairs={{0,2},{2,4},{4,6},{6,8},{8,10},{10,12},{12,14},{14,16},{16,18},{18... | collective-permute-start | bytes 393224 | tf_op jit(solution)/shard_map/ppermute | solution.py:427
  68.4 4.8 %collective-permute-start.12 = (bf16[128,512]{1,0:T(8,128)(2,1)S(1)}, bf16[128,512]{1,0:T(8,128)(2,1)S(1)}, u32[]{:S(2)}, u32[]{:S(2)}) collective-permute-start(bf16[128,512]{1,0:T(8,128)(2,1)S(1)} %collective-permute-done.10.refs_10_), channel_id=1, source_target_pairs={{0,30},{2,0},{4,2},{6,4},{8,6},{10,8},{12,10},{14,12},{16,14},{18,... | collective-permute-start | bytes 393224 | tf_op jit(solution)/shard_map/ppermute | solution.py:430
  69.8 6.1 %collective-permute-start.13 = (bf16[128,512]{1,0:T(8,128)(2,1)S(1)}, bf16[128,512]{1,0:T(8,128)(2,1)S(1)}, u32[]{:S(2)}, u32[]{:S(2)}) collective-permute-start(bf16[128,512]{1,0:T(8,128)(2,1)S(1)} %collective-permute-done.11.refs_11_), channel_id=1, source_target_pairs={{0,2},{2,4},{4,6},{6,8},{8,10},{10,12},{12,14},{14,16},{16,18},{18... | collective-permute-start | bytes 393224 | tf_op jit(solution)/shard_map/ppermute | solution.py:427
  70.5 6.2 %collective-permute-start = (bf16[2,32,2048]{2,1,0:T(8,128)(2,1)S(1)}, bf16[2,32,2048]{2,1,0:T(8,128)(2,1)S(1)}, u32[]{:S(2)}, u32[]{:S(2)}) collective-permute-start(bf16[2,32,2048]{2,1,0:T(8,128)(2,1)S(1)} %get-tuple-element.23), channel_id=1, source_target_pairs={{0,128},{128,0},{1,129},{129,1},{2,130},{130,2},{3,131},{131,3},{4... | collective-permute-start | bytes 786440 | tf_op jit(solution)/shard_map/ppermute | solution.py:377
  73.2 9.5 %collective-permute-start.14 = (bf16[128,512]{1,0:T(8,128)(2,1)S(1)}, bf16[128,512]{1,0:T(8,128)(2,1)S(1)}, u32[]{:S(2)}, u32[]{:S(2)}) collective-permute-start(bf16[128,512]{1,0:T(8,128)(2,1)S(1)} %collective-permute-done.12.refs_12_), channel_id=1, source_target_pairs={{0,30},{2,0},{4,2},{6,4},{8,6},{10,8},{12,10},{14,12},{16,14},{18,... | collective-permute-start | bytes 393224 | tf_op jit(solution)/shard_map/ppermute | solution.py:430
  75.9 9.5 %collective-permute-start.15 = (bf16[128,512]{1,0:T(8,128)(2,1)S(1)}, bf16[128,512]{1,0:T(8,128)(2,1)S(1)}, u32[]{:S(2)}, u32[]{:S(2)}) collective-permute-start(bf16[128,512]{1,0:T(8,128)(2,1)S(1)} %collective-permute-done.13.refs_13_), channel_id=1, source_target_pairs={{0,2},{2,4},{4,6},{6,8},{8,10},{10,12},{12,14},{14,16},{16,18},{18... | collective-permute-start | bytes 393224 | tf_op jit(solution)/shard_map/ppermute | solution.py:427
  77.3 9.3 %collective-permute-start.1 = (bf16[2,32,2048]{2,1,0:T(8,128)(2,1)S(1)}, bf16[2,32,2048]{2,1,0:T(8,128)(2,1)S(1)}, u32[]{:S(2)}, u32[]{:S(2)}) collective-permute-start(bf16[2,32,2048]{2,1,0:T(8,128)(2,1)S(1)} %get-tuple-element.24), channel_id=1, source_target_pairs={{0,0},{1,64},{32,32},{33,96},{64,1},{65,65},{96,33},{97,97},{2,2},... | collective-permute-start | bytes 786440 | tf_op jit(solution)/shard_map/ppermute | solution.py:390
  80.8 8.9 %collective-permute-start.2 = (bf16[2,32,2048]{2,1,0:T(8,128)(2,1)S(1)}, bf16[2,32,2048]{2,1,0:T(8,128)(2,1)S(1)}, u32[]{:S(2)}, u32[]{:S(2)}) collective-permute-start(bf16[2,32,2048]{2,1,0:T(8,128)(2,1)S(1)} %get-tuple-element.25), channel_id=1, source_target_pairs={{0,32},{1,96},{32,0},{33,64},{64,33},{65,97},{96,1},{97,65},{2,34}... | collective-permute-start | bytes 786440 | tf_op jit(solution)/shard_map/ppermute | solution.py:390
  82.7 7.6 %collective-permute-start.16 = (bf16[128,512]{1,0:T(8,128)(2,1)S(1)}, bf16[128,512]{1,0:T(8,128)(2,1)S(1)}, u32[]{:S(2)}, u32[]{:S(2)}) collective-permute-start(bf16[128,512]{1,0:T(8,128)(2,1)S(1)} %collective-permute-done.14.refs_14_), channel_id=1, source_target_pairs={{0,30},{2,0},{4,2},{6,4},{8,6},{10,8},{12,10},{14,12},{16,14},{18,... | collective-permute-start | bytes 393224 | tf_op jit(solution)/shard_map/ppermute | solution.py:430
  85.4 7.5 %collective-permute-start.17 = (bf16[128,512]{1,0:T(8,128)(2,1)S(1)}, bf16[128,512]{1,0:T(8,128)(2,1)S(1)}, u32[]{:S(2)}, u32[]{:S(2)}) collective-permute-start(bf16[128,512]{1,0:T(8,128)(2,1)S(1)} %collective-permute-done.15.refs_15_), channel_id=1, source_target_pairs={{0,2},{2,4},{4,6},{6,8},{8,10},{10,12},{12,14},{14,16},{16,18},{18... | collective-permute-start | bytes 393224 | tf_op jit(solution)/shard_map/ppermute | solution.py:427
  86.6 9.2 %collective-permute-start.3 = (bf16[2,32,2048]{2,1,0:T(8,128)(2,1)S(1)}, bf16[2,32,2048]{2,1,0:T(8,128)(2,1)S(1)}, u32[]{:S(2)}, u32[]{:S(2)}) collective-permute-start(bf16[2,32,2048]{2,1,0:T(8,128)(2,1)S(1)} %collective-permute-done.1.refs_0_), channel_id=1, source_target_pairs={{0,1},{1,0},{2,3},{3,2},{4,5},{5,4},{6,7},{7,6},{8,9},{9,8},{10,11... | collective-permute-start | bytes 786440 | tf_op jit(solution)/shard_map/ppermute | solution.py:393
  89.6 6.2 %collective-permute-start.4 = (bf16[2,32,2048]{2,1,0:T(8,128)(2,1)S(1)}, bf16[2,32,2048]{2,1,0:T(8,128)(2,1)S(1)}, u32[]{:S(2)}, u32[]{:S(2)}) collective-permute-start(bf16[2,32,2048]{2,1,0:T(8,128)(2,1)S(1)} %collective-permute-done.2.refs_1_), channel_id=1, source_target_pairs={{0,1},{1,0},{2,3},{3,2},{4,5},{5,4},{6,7},{7,6},{8,9},{9,8},{10,11... | collective-permute-start | bytes 786440 | tf_op jit(solution)/shard_map/ppermute | solution.py:393
  90.3 5.5 %collective-permute-start.18 = (bf16[128,512]{1,0:T(8,128)(2,1)S(1)}, bf16[128,512]{1,0:T(8,128)(2,1)S(1)}, u32[]{:S(2)}, u32[]{:S(2)}) collective-permute-start(bf16[128,512]{1,0:T(8,128)(2,1)S(1)} %collective-permute-done.16.refs_16_), channel_id=1, source_target_pairs={{0,30},{2,0},{4,2},{6,4},{8,6},{10,8},{12,10},{14,12},{16,14},{18,... | collective-permute-start | bytes 393224 | tf_op jit(solution)/shard_map/ppermute | solution.py:430
  92.9 5.9 %collective-permute-start.19 = (bf16[128,512]{1,0:T(8,128)(2,1)S(1)}, bf16[128,512]{1,0:T(8,128)(2,1)S(1)}, u32[]{:S(2)}, u32[]{:S(2)}) collective-permute-start(bf16[128,512]{1,0:T(8,128)(2,1)S(1)} %collective-permute-done.17.refs_17_), channel_id=1, source_target_pairs={{0,2},{2,4},{4,6},{6,8},{8,10},{10,12},{12,14},{14,16},{16,18},{18... | collective-permute-start | bytes 393224 | tf_op jit(solution)/shard_map/ppermute | solution.py:427
  95.8 0.6 copy-start.3
  98.8 0.7 copy-start.5
  99.5 0.9 copy-start.4
  100.4 0.9 copy-start.6
  103.3 14.7 %collective-permute-start.20 = (f32[4,32,512]{2,1,0:T(8,128)}, f32[4,32,512]{2,1,0:T(8,128)S(1)}, u32[]{:S(2)}, u32[]{:S(2)}) collective-permute-start(f32[4,32,512]{2,1,0:T(8,128)} %get-tuple-element.27), channel_id=1, source_target_pairs={{0,128},{128,0},{1,129},{129,1},{2,130},{130,2},{3,131},{131,3},{4... | collective-permute-start | bytes 786440 | tf_op jit(solution)/shard_map/ppermute | solution.py:377
  105.5 24.4 %all-to-all-start.1 = ((bf16[16,8,640]{2,1,0:T(8,128)(2,1)}), bf16[16,8,640]{2,1,0:T(8,128)(2,1)S(1)}, u32[]{:S(2)}, u32[]{:S(2)}) async-start(bf16[16,8,640]{2,1,0:T(8,128)(2,1)} %shard_map.109), calls=%async_computation.1 | async-start | bytes 327680 | tf_op jit(solution)/shard_map/all_to_all | solution.py:24
  118.0 15.5 %collective-permute-start.21 = (f32[32,512]{1,0:T(8,128)S(1)}, f32[32,512]{1,0:T(8,128)S(1)}, u32[]{:S(2)}, u32[]{:S(2)}) collective-permute-start(f32[32,512]{1,0:T(8,128)S(1)} %get-tuple-element.29), channel_id=1, source_target_pairs={{0,32},{32,0},{64,96},{96,64},{1,33},{33,1},{65,97},{97,65},{2,34}... | collective-permute-start | bytes 196616 | tf_op jit(solution)/shard_map/ppermute | solution.py:49
  118.2 15.7 %collective-permute-start.22 = (f32[32,512]{1,0:T(8,128)S(1)}, f32[32,512]{1,0:T(8,128)S(1)}, u32[]{:S(2)}, u32[]{:S(2)}) collective-permute-start(f32[32,512]{1,0:T(8,128)S(1)} %get-tuple-element.30), channel_id=1, source_target_pairs={{0,64},{32,96},{64,0},{96,32},{1,65},{33,97},{65,1},{97,33},{2,66}... | collective-permute-start | bytes 196616 | tf_op jit(solution)/shard_map/ppermute | solution.py:49
  121.7 12.2 %collective-permute-start.23 = (f32[32,512]{1,0:T(8,128)S(1)}, f32[32,512]{1,0:T(8,128)S(1)}, u32[]{:S(2)}, u32[]{:S(2)}) collective-permute-start(f32[32,512]{1,0:T(8,128)S(1)} %get-tuple-element.31), channel_id=1, source_target_pairs={{0,96},{32,64},{64,32},{96,0},{1,97},{33,65},{65,33},{97,1},{2,98}... | collective-permute-start | bytes 196616 | tf_op jit(solution)/shard_map/ppermute | solution.py:49
  129.9 71.2 %copy-start = (bf16[4096,256]{1,0:T(8,128)(2,1)S(1)}, bf16[4096,256]{1,0:T(8,128)(2,1)}, u32[]{:S(2)}) copy-start(bf16[4096,256]{1,0:T(8,128)(2,1)} %refs_4_.1) | copy-start | bytes 6291460
  129.9 4.3 %collective-permute-start.27 = (bf16[64,1152]{1,0:T(8,128)(2,1)S(1)}, bf16[64,1152]{1,0:T(8,128)(2,1)S(1)}, u32[]{:S(2)}, u32[]{:S(2)}) collective-permute-start(bf16[64,1152]{1,0:T(8,128)(2,1)S(1)} %shard_map.110.refs_0_), channel_id=1, source_target_pairs={{0,32},{32,0},{64,96},{96,64},{1,33},{33,1},{65,97},{97,65},{2,34}... | collective-permute-start | bytes 442376 | tf_op jit(solution)/shard_map/ppermute | solution.py:49
  130.0 7.7 %collective-permute-start.28 = (bf16[64,1152]{1,0:T(8,128)(2,1)S(1)}, bf16[64,1152]{1,0:T(8,128)(2,1)S(1)}, u32[]{:S(2)}, u32[]{:S(2)}) collective-permute-start(bf16[64,1152]{1,0:T(8,128)(2,1)S(1)} %shard_map.110.refs_0_), channel_id=1, source_target_pairs={{0,64},{32,96},{64,0},{96,32},{1,65},{33,97},{65,1},{97,33},{2,66}... | collective-permute-start | bytes 442376 | tf_op jit(solution)/shard_map/ppermute | solution.py:49
  133.6 5.7 %collective-permute-start.29 = (bf16[64,1152]{1,0:T(8,128)(2,1)S(1)}, bf16[64,1152]{1,0:T(8,128)(2,1)S(1)}, u32[]{:S(2)}, u32[]{:S(2)}) collective-permute-start(bf16[64,1152]{1,0:T(8,128)(2,1)S(1)} %shard_map.110.refs_0_), channel_id=1, source_target_pairs={{0,96},{32,64},{64,32},{96,0},{1,97},{33,65},{65,33},{97,1},{2,98}... | collective-permute-start | bytes 442376 | tf_op jit(solution)/shard_map/ppermute | solution.py:49
  133.9 68.2 %copy-start.2 = (bf16[32,512]{1,0:T(8,128)(2,1)}, bf16[32,512]{1,0:T(8,128)(2,1)S(1)}, u32[]{:S(2)}) copy-start(bf16[32,512]{1,0:T(8,128)(2,1)S(1)} %add_convert_fusion.refs_6_) | copy-start | bytes 98308
  144.7 4.1 %collective-permute-start.30 = (bf16[64,1152]{1,0:T(8,128)(2,1)S(1)}, bf16[64,1152]{1,0:T(8,128)(2,1)S(1)}, u32[]{:S(2)}, u32[]{:S(2)}) collective-permute-start(bf16[64,1152]{1,0:T(8,128)(2,1)S(1)} %get-tuple-element.37), channel_id=1, source_target_pairs={{0,32},{32,0},{64,96},{96,64},{1,33},{33,1},{65,97},{97,65},{2,34}... | collective-permute-start | bytes 442376 | tf_op jit(solution)/shard_map/ppermute | solution.py:49
  144.8 5.7 %collective-permute-start.31 = (bf16[64,1152]{1,0:T(8,128)(2,1)S(1)}, bf16[64,1152]{1,0:T(8,128)(2,1)S(1)}, u32[]{:S(2)}, u32[]{:S(2)}) collective-permute-start(bf16[64,1152]{1,0:T(8,128)(2,1)S(1)} %get-tuple-element.38), channel_id=1, source_target_pairs={{0,64},{32,96},{64,0},{96,32},{1,65},{33,97},{65,1},{97,33},{2,66}... | collective-permute-start | bytes 442376 | tf_op jit(solution)/shard_map/ppermute | solution.py:49
  146.3 5.7 %collective-permute-start.32 = (bf16[64,1152]{1,0:T(8,128)(2,1)S(1)}, bf16[64,1152]{1,0:T(8,128)(2,1)S(1)}, u32[]{:S(2)}, u32[]{:S(2)}) collective-permute-start(bf16[64,1152]{1,0:T(8,128)(2,1)S(1)} %get-tuple-element.39), channel_id=1, source_target_pairs={{0,96},{32,64},{64,32},{96,0},{1,97},{33,65},{65,33},{97,1},{2,98}... | collective-permute-start | bytes 442376 | tf_op jit(solution)/shard_map/ppermute | solution.py:49
  194.1 4.0 %collective-permute-start.33 = (bf16[64,1024]{1,0:T(8,128)(2,1)S(1)}, bf16[64,1024]{1,0:T(8,128)(2,1)S(1)}, u32[]{:S(2)}, u32[]{:S(2)}) collective-permute-start(bf16[64,1024]{1,0:T(8,128)(2,1)S(1)} %shard_map.114.refs_0_), channel_id=1, source_target_pairs={{0,32},{32,0},{64,96},{96,64},{1,33},{33,1},{65,97},{97,65},{2,34}... | collective-permute-start | bytes 393224 | tf_op jit(solution)/shard_map/ppermute | solution.py:49
  194.2 5.5 %collective-permute-start.34 = (bf16[64,1024]{1,0:T(8,128)(2,1)S(1)}, bf16[64,1024]{1,0:T(8,128)(2,1)S(1)}, u32[]{:S(2)}, u32[]{:S(2)}) collective-permute-start(bf16[64,1024]{1,0:T(8,128)(2,1)S(1)} %shard_map.114.refs_0_), channel_id=1, source_target_pairs={{0,64},{32,96},{64,0},{96,32},{1,65},{33,97},{65,1},{97,33},{2,66}... | collective-permute-start | bytes 393224 | tf_op jit(solution)/shard_map/ppermute | solution.py:49
  194.4 6.7 %collective-permute-start.35 = (bf16[64,1024]{1,0:T(8,128)(2,1)S(1)}, bf16[64,1024]{1,0:T(8,128)(2,1)S(1)}, u32[]{:S(2)}, u32[]{:S(2)}) collective-permute-start(bf16[64,1024]{1,0:T(8,128)(2,1)S(1)} %shard_map.114.refs_0_), channel_id=1, source_target_pairs={{0,96},{32,64},{64,32},{96,0},{1,97},{33,65},{65,33},{97,1},{2,98}... | collective-permute-start | bytes 393224 | tf_op jit(solution)/shard_map/ppermute | solution.py:49
  202.1 6.1 %collective-permute-start.36 = (f32[64,128]{1,0:T(8,128)S(1)}, f32[64,128]{1,0:T(8,128)S(1)}, u32[]{:S(2)}, u32[]{:S(2)}) collective-permute-start(f32[64,128]{1,0:T(8,128)S(1)} %get-tuple-element.41), channel_id=1, source_target_pairs={{0,1},{1,0},{2,3},{3,2},{4,5},{5,4},{6,7},{7,6},{8,9},{9,8},{10,11... | collective-permute-start | bytes 98312 | tf_op jit(solution)/shard_map/ppermute | solution.py:543
